TPU v7x, 32 devices: a whole 2x2x4 slice. The times are simulated.
32 devices in a mesh: wide: 16 (over z, x, core), narrow: 2 (over y).
Axes of the slice: x: 2, y: 2, z: 4, core: 2. Of those that a mesh axis runs over, the one named last changes fastest.
Arguments:
- tokens: bfloat16 [2, 32768, 768], P(None, ('wide', 'narrow')), may hold values from -6 to 6
- grad_out: bfloat16 [2, 32768, 768], P(None, ('wide', 'narrow')), may hold values from -6 to 6
- route_ids: int32 [2, 32768], P(None, ('wide', 'narrow')), may hold values from 0 to 15, as said below
- slot_ids: int32 [2, 32768], P(None, ('wide', 'narrow')), may hold values from 0 to 63, as said below
- keep_ids: int32 [2, 32768], P(None, ('wide', 'narrow')), may hold values from 0 to 1, as said below
- gain_one: float32 [768], replicated, may hold values from 0.5 to 1.5
- w_query: bfloat16 [768, 768], replicated, may hold values from -0.21875 to 0.21875
- w_key: bfloat16 [768, 768], replicated, may hold values from -0.21875 to 0.21875
- w_value: bfloat16 [768, 768], replicated, may hold values from -0.21875 to 0.21875
- w_out: bfloat16 [768, 768], replicated, may hold values from -4 to 4
- gain_two: float32 [768], replicated, may hold values from 0.5 to 1.5
- w_route: bfloat16 [768, 16], replicated, may hold values from -0.21875 to 0.21875
- embed: float32 [16, 16], replicated, may hold values from -6 to 6
- w_in: bfloat16 [16, 768, 3072], P('wide', None, 'narrow'), may hold values from -0.21875 to 0.21875
- w_outer: bfloat16 [16, 3072, 768], P('wide', 'narrow'), may hold values from -1.75 to 1.75
Outputs:
- block_out: bfloat16 [2, 32768, 768], P(None, ('wide', 'narrow'))
- grad_tokens: bfloat16 [2, 32768, 768], P(None, ('wide', 'narrow'))
- grad_gain_one: float32 [768], replicated
- grad_w_query: float32 [768, 768], replicated
- grad_w_key: float32 [768, 768], replicated
- grad_w_value: float32 [768, 768], replicated
- grad_w_out: float32 [768, 768], replicated
- grad_gain_two: float32 [768], replicated
- grad_w_route: float32 [768, 16], replicated
- grad_embed: float32 [16, 16], replicated
- grad_w_in: float32 [16, 768, 3072], P('wide', None, 'narrow')
- grad_w_outer: float32 [16, 3072, 768], P('wide', 'narrow')
Inputs may be any that keep to these rules, and one draw needn't show every extreme that they name: `route_ids`: an expert's number for every token. `slot_ids`: within one aligned block of 1024 tokens of a micro-batch, the kept tokens bound for one expert carry slots 0, 1, 2, ... in token order; a token that would need slot 64 or more is dropped and carries 0. In every block some expert has all 64 slots filled and more tokens than that. `keep_ids`: 1 exactly for the tokens that got a slot; tokens are dropped in token order once an expert's 64 slots of the block are taken.
All inputs are finite; a program needn't handle non-finite values.
Results may differ from a plain program's by a relative error of at most 0.015.
Values may be sent and summed in bfloat16 or wider, within the bound.
A program may use at most 384 MiB of HBM per device.

v0:
```python
import jax
import jax.numpy as jnp
from jax import lax
from jax.sharding import PartitionSpec as P

D = 768
HEADS = 12
HEAD_DIM = 64
LENGTH = 1024


def layer_norm(values, gain_vec):
    centred = values - jnp.mean(values, axis=-1, keepdims=True)
    spread_sq = jnp.mean(centred * centred, axis=-1, keepdims=True)
    return centred * lax.rsqrt(spread_sq + 1e-05) * gain_vec


def gate_from(projected, embed_rows, route_row):
    unit_rows = projected * lax.rsqrt(jnp.sum(projected * projected, axis=-1, keepdims=True) + 1.0)
    anchor = embed_rows * lax.rsqrt(jnp.sum(embed_rows * embed_rows, axis=-1, keepdims=True) + 1.0)
    logits = 3.0 * jnp.dot(
        unit_rows, anchor.T, precision=lax.Precision.HIGHEST, preferred_element_type=jnp.float32
    )
    soft_rows = jax.nn.softmax(logits, axis=-1)
    picked = route_row[:, None] == jnp.arange(soft_rows.shape[1], dtype=jnp.int32)[None, :]
    return jnp.sum(jnp.where(picked, soft_rows, 0.0), axis=-1)


def contract_rows(left, right, precise=None):
    return lax.dot_general(
        left, right, (((0,), (0,)), ((), ())), precision=precise, preferred_element_type=jnp.float32
    )


def contract_cols(left, right, precise=None):
    return lax.dot_general(
        left, right, (((1,), (1,)), ((), ())), precision=precise, preferred_element_type=jnp.float32
    )


def gelu_exact(values):
    return jax.nn.gelu(values, approximate=False)


def split_heads(flat_rows):
    return flat_rows.reshape(flat_rows.shape[0] // LENGTH, LENGTH, HEADS, HEAD_DIM)


def attention_forward(qkv_rows):
    tok_count = qkv_rows.shape[0]
    block_rows = min(512, LENGTH)
    count_blocks = LENGTH // block_rows
    score_scale = HEAD_DIM ** (-0.5)
    queries = split_heads(qkv_rows[:, :D])
    keys_in = split_heads(qkv_rows[:, D : 2 * D])
    values_in = split_heads(qkv_rows[:, 2 * D :])

    def one_block(row_start):
        query_block = lax.dynamic_slice_in_dim(queries, row_start, block_rows, 1)
        scores = (
            jnp.einsum("sqhd,skhd->shqk", query_block, keys_in, preferred_element_type=jnp.float32)
            * score_scale
        )
        row_max = jnp.max(scores, axis=-1, keepdims=True)
        exp_scores = jnp.exp(scores - row_max)
        row_total = jnp.sum(exp_scores, axis=-1, keepdims=True)
        soft_weights = (exp_scores / row_total).astype(jnp.bfloat16)
        mixed_block = jnp.einsum(
            "shqk,skhd->sqhd", soft_weights, values_in, preferred_element_type=jnp.float32
        )
        return (mixed_block.astype(jnp.bfloat16), (row_max + jnp.log(row_total))[..., 0])

    starts = jnp.arange(count_blocks, dtype=jnp.int32) * block_rows
    mixed_blocks, log_totals = lax.map(one_block, starts)
    mixed_rows = jnp.moveaxis(mixed_blocks, 0, 1).reshape(tok_count, D)
    return (mixed_rows, log_totals)


def attention_backward(qkv_rows, log_totals, grad_mixed):
    tok_count = qkv_rows.shape[0]
    block_rows = min(512, LENGTH)
    count_blocks = LENGTH // block_rows
    score_scale = HEAD_DIM ** (-0.5)
    queries = split_heads(qkv_rows[:, :D])
    keys_in = split_heads(qkv_rows[:, D : 2 * D])
    values_in = split_heads(qkv_rows[:, 2 * D :])
    grad_heads = split_heads(grad_mixed)

    def one_block(carry, block_index):
        grad_keys, grad_values = carry
        row_start = block_index * block_rows
        query_block = lax.dynamic_slice_in_dim(queries, row_start, block_rows, 1)
        grad_block = lax.dynamic_slice_in_dim(grad_heads, row_start, block_rows, 1)
        scores = (
            jnp.einsum("sqhd,skhd->shqk", query_block, keys_in, preferred_element_type=jnp.float32)
            * score_scale
        )
        soft_weights = jnp.exp(scores - log_totals[block_index][..., None])
        grad_soft = jnp.einsum(
            "sqhd,skhd->shqk", grad_block, values_in, preferred_element_type=jnp.float32
        )
        inner_term = jnp.sum(soft_weights * grad_soft, axis=-1, keepdims=True)
        grad_scores = (soft_weights * (grad_soft - inner_term)).astype(jnp.bfloat16)
        grad_query = (
            jnp.einsum("shqk,skhd->sqhd", grad_scores, keys_in, preferred_element_type=jnp.float32)
            * score_scale
        )
        grad_keys = (
            grad_keys
            + jnp.einsum(
                "shqk,sqhd->skhd", grad_scores, query_block, preferred_element_type=jnp.float32
            )
            * score_scale
        )
        grad_values = grad_values + jnp.einsum(
            "shqk,sqhd->skhd",
            soft_weights.astype(jnp.bfloat16),
            grad_block,
            preferred_element_type=jnp.float32,
        )
        return ((grad_keys, grad_values), grad_query)

    zero_heads = jnp.zeros(queries.shape, jnp.float32)
    (grad_keys, grad_values), grad_queries = lax.scan(
        one_block, (zero_heads, zero_heads), jnp.arange(count_blocks, dtype=jnp.int32)
    )
    grad_queries = jnp.moveaxis(grad_queries, 0, 1).reshape(tok_count, D)
    joined = jnp.concatenate(
        [grad_queries, grad_keys.reshape(tok_count, D), grad_values.reshape(tok_count, D)], axis=1
    )
    return joined.astype(jnp.bfloat16)


def local(
    tokens,
    grad_out,
    route_ids,
    slot_ids,
    keep_ids,
    gain_one,
    w_query,
    w_key,
    w_value,
    w_out,
    gain_two,
    w_route,
    embed,
    w_in,
    w_outer,
):
    micro_count, tok_count, feat_width = tokens.shape
    wide_count = lax.axis_size("wide")
    expert_count = embed.shape[0]
    slot_cap = max(2, tok_count // expert_count)
    w_qkv = jnp.concatenate([w_query, w_key, w_value], axis=1)
    route_float = w_route.astype(jnp.float32)
    local_in = w_in[0]
    local_outer = w_outer[0]
    acc_in = jnp.zeros(local_in.shape, jnp.float32)
    acc_outer = jnp.zeros(local_outer.shape, jnp.float32)
    acc_gain_one = jnp.zeros(gain_one.shape, jnp.float32)
    acc_qkv = jnp.zeros(w_qkv.shape, jnp.float32)
    acc_wo = jnp.zeros(w_out.shape, jnp.float32)
    acc_gain_two = jnp.zeros(gain_two.shape, jnp.float32)
    acc_route = jnp.zeros(w_route.shape, jnp.float32)
    acc_embed = jnp.zeros(embed.shape, jnp.float32)
    outputs = []
    input_grads = []
    slot_columns = jnp.arange(expert_count * slot_cap, dtype=jnp.int32)
    for micro_step in range(micro_count):
        route_row = route_ids[micro_step]
        inputs = tokens[micro_step].astype(jnp.float32)
        normed_one, pull_one = jax.vjp(layer_norm, inputs, gain_one)
        normed_low = normed_one.astype(jnp.bfloat16)
        qkv_rows = jnp.dot(normed_low, w_qkv, preferred_element_type=jnp.float32).astype(
            jnp.bfloat16
        )
        mixed_rows, log_totals = attention_forward(qkv_rows)
        first_sum = inputs + jnp.dot(mixed_rows, w_out, preferred_element_type=jnp.float32)
        normed_two, pull_two = jax.vjp(layer_norm, first_sum, gain_two)
        second_low = normed_two.astype(jnp.bfloat16)
        projected = jnp.dot(second_low, w_route, preferred_element_type=jnp.float32)
        gate_prob, pull_gate = jax.vjp(
            lambda proj_in, embed_in: gate_from(proj_in, embed_in, route_row), projected, embed
        )
        slot_index = jnp.where(
            keep_ids[micro_step] > 0, route_row * slot_cap + slot_ids[micro_step], -1
        )
        slot_table = (slot_index[:, None] == slot_columns[None, :]).astype(jnp.bfloat16)
        sent_rows = (
            contract_rows(slot_table, second_low)
            .astype(jnp.bfloat16)
            .reshape(expert_count, slot_cap, feat_width)
        )
        arrived = lax.all_to_all(
            sent_rows, "wide", split_axis=0, concat_axis=0, tiled=True
        ).reshape(-1, feat_width)
        all_rows = lax.all_gather(arrived, "narrow", axis=0, tiled=True)
        pre_act = jnp.dot(all_rows, local_in, preferred_element_type=jnp.float32)
        hidden = gelu_exact(pre_act).astype(jnp.bfloat16)
        partial_rows = jnp.dot(hidden, local_outer, preferred_element_type=jnp.float32)
        result_rows = lax.psum_scatter(
            partial_rows.astype(jnp.bfloat16), "narrow", scatter_dimension=0, tiled=True
        )
        back_rows = lax.all_to_all(
            result_rows.reshape(wide_count, slot_cap, feat_width),
            "wide",
            split_axis=0,
            concat_axis=0,
            tiled=True,
        )
        returned = jnp.dot(
            slot_table, back_rows.reshape(-1, feat_width), preferred_element_type=jnp.float32
        )
        block_sum = first_sum + gate_prob[:, None] * returned
        outputs.append(block_sum.astype(jnp.bfloat16))
        grad_sum = grad_out[micro_step].astype(jnp.float32)
        grad_gate = jnp.sum(grad_sum * returned, axis=-1)
        grad_returned = (gate_prob[:, None] * grad_sum).astype(jnp.bfloat16)
        grad_buffer = (
            contract_rows(slot_table, grad_returned)
            .astype(jnp.bfloat16)
            .reshape(expert_count, slot_cap, feat_width)
        )
        grad_result = lax.all_to_all(
            grad_buffer, "wide", split_axis=0, concat_axis=0, tiled=True
        ).reshape(-1, feat_width)
        grad_all = lax.all_gather(grad_result, "narrow", axis=0, tiled=True)
        acc_outer = acc_outer + contract_rows(hidden, grad_all)
        grad_hidden = contract_cols(grad_all, local_outer)
        grad_pre = jax.vjp(gelu_exact, pre_act)[1](grad_hidden)[0].astype(jnp.bfloat16)
        acc_in = acc_in + contract_rows(all_rows, grad_pre)
        grad_part = contract_cols(grad_pre, local_in)
        grad_arrived = lax.psum_scatter(
            grad_part.astype(jnp.bfloat16), "narrow", scatter_dimension=0, tiled=True
        )
        grad_sent = lax.all_to_all(
            grad_arrived.reshape(wide_count, slot_cap, feat_width),
            "wide",
            split_axis=0,
            concat_axis=0,
            tiled=True,
        )
        grad_second = jnp.dot(
            slot_table, grad_sent.reshape(-1, feat_width), preferred_element_type=jnp.float32
        )
        grad_projected, grad_embed_part = pull_gate(grad_gate)
        grad_second = grad_second + contract_cols(
            grad_projected, route_float, lax.Precision.HIGHEST
        )
        acc_route = acc_route + contract_rows(
            second_low.astype(jnp.float32), grad_projected, lax.Precision.HIGHEST
        )
        acc_embed = acc_embed + grad_embed_part
        grad_first_norm, grad_gain_b = pull_two(grad_second)
        acc_gain_two = acc_gain_two + grad_gain_b
        grad_first = grad_sum + grad_first_norm
        grad_branch = grad_first.astype(jnp.bfloat16)
        acc_wo = acc_wo + contract_rows(mixed_rows, grad_branch)
        grad_mixed = contract_cols(grad_branch, w_out).astype(jnp.bfloat16)
        grad_qkv = attention_backward(qkv_rows, log_totals, grad_mixed)
        acc_qkv = acc_qkv + contract_rows(normed_low, grad_qkv)
        grad_normed = contract_cols(grad_qkv, w_qkv)
        grad_input_norm, grad_gain_a = pull_one(grad_normed)
        acc_gain_one = acc_gain_one + grad_gain_a
        input_grads.append((grad_first + grad_input_norm).astype(jnp.bfloat16))
    sum_gain_one, sum_qkv, sum_wo, sum_gain_two, sum_route, sum_embed = lax.psum(
        (acc_gain_one, acc_qkv, acc_wo, acc_gain_two, acc_route, acc_embed), ("wide", "narrow")
    )
    grad_in_local, grad_outer_local = (acc_in, acc_outer)
    return (
        jnp.stack(outputs),
        jnp.stack(input_grads),
        sum_gain_one,
        sum_qkv[:, :feat_width],
        sum_qkv[:, feat_width : 2 * feat_width],
        sum_qkv[:, 2 * feat_width :],
        sum_wo,
        sum_gain_two,
        sum_route,
        sum_embed,
        grad_in_local[None],
        grad_outer_local[None],
    )


def solution(mesh):
    placed = (
        P(None, ("wide", "narrow"), None),
        P(None, ("wide", "narrow"), None),
        P(None, ("wide", "narrow")),
        P(None, ("wide", "narrow")),
        P(None, ("wide", "narrow")),
        P(),
        P(),
        P(),
        P(),
        P(),
        P(),
        P(),
        P(),
        P("wide", None, "narrow"),
        P("wide", "narrow", None),
    )
    return jax.shard_map(
        local,
        mesh=mesh,
        in_specs=placed,
        out_specs=(
            P(None, ("wide", "narrow"), None),
            P(None, ("wide", "narrow"), None),
            P(),
            P(),
            P(),
            P(),
            P(),
            P(),
            P(),
            P(),
            P("wide", None, "narrow"),
            P("wide", "narrow", None),
        ),
        check_vma=False,
    )
```

profile of v0, /device:TPU:0, one launch (start us, length us, event | category | flops | bytes accessed | tf_op | source)
XLA Modules:
  0.0 1653.7 jit_solution(5152117024401113663)
XLA Ops:
  45.7 78.8 %while.55 = (s32[]{:T(128)}, bf16[2,1,512,12,64]{2,4,3,1,0:T(8,128)(2,1)}, f32[2,1,12,512]{3,2,1,0:T(8,128)S(1)}, s32[2]{0:T(128)S(1)}, bf16[1,1024,12,64]{1,3,2...) while((s32[]{:T(128)}, ...), condition=%wide.region_19.20_spmd, body=%wide.region_16.19_spmd.sunk | while | flops 1667622912 | bytes 99328248 | solution.py:74
  148.7 78.6 %while.54 = (s32[]{:T(128)}, bf16[2,1,512,12,64]{2,4,3,1,0:T(8,128)(2,1)}, f32[2,1,12,512]{3,2,1,0:T(8,128)S(1)}, s32[2]{0:T(128)S(1)}, bf16[1,1024,12,64]{1,3,2...) while((s32[]{:T(128)}, ...), condition=%wide.region_5.6_spmd, body=%wide.region_2.5_spmd.sunk | while | flops 1667622912 | bytes 99328248 | solution.py:74
  238.1 43.3 %all_to_all.40 = bf16[16,64,768]{2,1,0:T(8,128)(2,1)} all-to-all(bf16[16,64,768]{2,1,0:T(8,128)(2,1)S(1)} %bitcast.480), channel_id=1, replica_groups=mesh['wide'=16,'narrow'=2] {'wide'}, dimensions={0} | all-to-all | bytes 3145728 | tf_op jit(solution)/shard_map/all_to_all | solution.py:195
  281.6 45.4 %all-gather.5.cloned.1.call-done = bf16[2048,768]{1,0:T(8,128)(2,1)} async-done(((bf16[1024,768]{1,0:T(8,128)(2,1)}), bf16[2048,768]{1,0:T(8,128)(2,1)}) %all-gather.5.cloned.1.call-update) | async-done | bytes 3145744 | tf_op jit(solution)/shard_map/all_gather | solution.py:198
  327.0 33.7 %multiply_convert_fusion.3 = (bf16[2048,1536]{1,0:T(8,128)(2,1)S(1)}, f32[2048,1536]{1,0:T(8,128)}, f32[2048,1536]{1,0:T(8,128)}) fusion(bf16[2048,768]{1,0:T(8,128)(2,1)} %all-gather.5.cloned.1.call-done, bf16[1,768,1536]{2,1,0:T(8,128)(2,1)S(1)} %copy-done), kind=kOutput, calls=%fused_computation.111 | convolution fusion | flops 5036310528 | bytes 36962304 | tf_op jit(solution)/shard_map/dot_general | solution.py:199
  369.7 43.5 %reduce-scatter.5.cloned.1.call-done = bf16[1024,768]{1,0:T(8,128)(2,1)} async-done(((bf16[2048,768]{1,0:T(8,128)(2,1)}), bf16[1024,768]{1,0:T(8,128)(2,1)}) %reduce-scatter.5.cloned.1.call-update) | async-done | bytes 1572880 | tf_op jit(solution)/shard_map/reduce_scatter | solution.py:202
  427.6 23.3 %all-to-all-done.1 = bf16[16,64,768]{2,1,0:T(8,128)(2,1)} async-done(((bf16[16,64,768]{2,1,0:T(8,128)(2,1)}), bf16[16,64,768]{2,1,0:T(8,128)(2,1)}, u32[]{:S(2)}, u32[]{:S(2)}) %all-to-all-start.1) | async-done | bytes 1572896 | tf_op jit(solution)/shard_map/all_to_all | solution.py:205
  458.7 45.1 %all_to_all.41 = bf16[16,64,768]{2,1,0:T(8,128)(2,1)} all-to-all(bf16[16,64,768]{2,1,0:T(8,128)(2,1)S(1)} %bitcast.481), channel_id=1, replica_groups=mesh['wide'=16,'narrow'=2] {'wide'}, dimensions={0} | all-to-all | bytes 3145728 | tf_op jit(solution)/shard_map/all_to_all | solution.py:225
  503.9 44.5 %all-gather.9.cloned.1.call-done = bf16[2048,768]{1,0:T(8,128)(2,1)} async-done(((bf16[1024,768]{1,0:T(8,128)(2,1)}), bf16[2048,768]{1,0:T(8,128)(2,1)}) %all-gather.9.cloned.1.call-update) | async-done | bytes 3145744 | tf_op jit(solution)/shard_map/all_gather | solution.py:228
  573.9 43.5 %reduce-scatter.9.cloned.1.call-done = bf16[1024,768]{1,0:T(8,128)(2,1)} async-done(((bf16[2048,768]{1,0:T(8,128)(2,1)}), bf16[1024,768]{1,0:T(8,128)(2,1)}) %reduce-scatter.9.cloned.1.call-update) | async-done | bytes 1572880 | tf_op jit(solution)/shard_map/reduce_scatter | solution.py:234
  623.8 31.3 %all-to-all-done.5 = bf16[16,64,768]{2,1,0:T(8,128)(2,1)} async-done(((bf16[16,64,768]{2,1,0:T(8,128)(2,1)}), bf16[16,64,768]{2,1,0:T(8,128)(2,1)}, u32[]{:S(2)}, u32[]{:S(2)}) %all-to-all-start.5) | async-done | bytes 1572896 | tf_op jit(solution)/shard_map/all_to_all | solution.py:237
  667.9 45.1 %all_to_all.42 = bf16[16,64,768]{2,1,0:T(8,128)(2,1)} all-to-all(bf16[16,64,768]{2,1,0:T(8,128)(2,1)S(1)} %bitcast.482), channel_id=1, replica_groups=mesh['wide'=16,'narrow'=2] {'wide'}, dimensions={0} | all-to-all | bytes 3145728 | tf_op jit(solution)/shard_map/all_to_all | solution.py:195
  713.1 44.5 %all-gather.7.cloned.1.call-done = bf16[2048,768]{1,0:T(8,128)(2,1)} async-done(((bf16[1024,768]{1,0:T(8,128)(2,1)}), bf16[2048,768]{1,0:T(8,128)(2,1)}) %all-gather.7.cloned.1.call-update) | async-done | bytes 3145744 | tf_op jit(solution)/shard_map/all_gather | solution.py:198
  757.6 33.5 %multiply_convert_fusion.2 = (bf16[2048,1536]{1,0:T(8,128)(2,1)S(1)}, f32[2048,1536]{1,0:T(8,128)}, f32[2048,1536]{1,0:T(8,128)}) fusion(bf16[2048,768]{1,0:T(8,128)(2,1)} %all-gather.7.cloned.1.call-done, bf16[1,768,1536]{2,1,0:T(8,128)(2,1)S(1)} %copy-done), kind=kOutput, calls=%fused_computation.98 | convolution fusion | flops 5036310528 | bytes 36962304 | tf_op jit(solution)/shard_map/dot_general | solution.py:199
  800.2 43.5 %reduce-scatter.7.cloned.1.call-done = bf16[1024,768]{1,0:T(8,128)(2,1)} async-done(((bf16[2048,768]{1,0:T(8,128)(2,1)}), bf16[1024,768]{1,0:T(8,128)(2,1)}) %reduce-scatter.7.cloned.1.call-update) | async-done | bytes 1572880 | tf_op jit(solution)/shard_map/reduce_scatter | solution.py:202
  854.6 26.7 %all-to-all-done.3 = bf16[16,64,768]{2,1,0:T(8,128)(2,1)} async-done(((bf16[16,64,768]{2,1,0:T(8,128)(2,1)}), bf16[16,64,768]{2,1,0:T(8,128)(2,1)}, u32[]{:S(2)}, u32[]{:S(2)}) %all-to-all-start.3) | async-done | bytes 1572896 | tf_op jit(solution)/shard_map/all_to_all | solution.py:205
  903.6 28.6 %all-to-all-done.6 = bf16[16,64,768]{2,1,0:T(8,128)(2,1)} async-done(((bf16[16,64,768]{2,1,0:T(8,128)(2,1)}), bf16[16,64,768]{2,1,0:T(8,128)(2,1)}, u32[]{:S(2)}, u32[]{:S(2)}) %all-to-all-start.6) | async-done | bytes 1572896 | tf_op jit(solution)/shard_map/all_to_all | solution.py:225
  957.1 23.7 %all-gather.11.cloned.1.call-done = bf16[2048,768]{1,0:T(8,128)(2,1)} async-done(((bf16[1024,768]{1,0:T(8,128)(2,1)}), bf16[2048,768]{1,0:T(8,128)(2,1)}) %all-gather.11.cloned.1.call-update) | async-done | bytes 3145744 | tf_op jit(solution)/shard_map/all_gather | solution.py:228
  1007.9 170.1 %while.56 = (s32[]{:T(128)}, f32[1,1024,12,64]{1,3,2,0:T(8,128)}, f32[1,1024,12,64]{1,3,2,0:T(8,128)}, bf16[2,1,512,12,64]{2,4,3,1,0:T(8,128)(2,1)}, s32[2]{0:T(...) while((s32[]{:T(128)}, f32[1,1024,12,64]{1,3,2,0:T(8,128)}, ...), condition=%wide.region_35.36_spmd.clone, body=%wide.region_33.35_spmd.clone.sunk | while | flops 4106348544 | bytes 217235760 | solution.py:124
  1137.2 21.5 %multiply_convert_fusion.8 = bf16[12,512,1024]{2,1,0:T(8,128)(2,1)} fusion(f32[12,512,1024]{2,1,0:T(8,128)} %get-tuple-element.703, f32[12,512,1024]{2,1,0:T(8,128)} %fusion.350, f32[12,512]{1,0:T(8,128)S(1)} %get-tuple-element.704, f32[12,512]{1,0:T(8,128)S(1)} %dynamic-slice_bitcast_fusion.4), kind=kLoop, calls=%fused_computation.32.clone.1 | loop fusion | flops 31457280 | bytes 62963712 | tf_op jit(solution)/shard_map/while/body/eval_jaxpr/convert_element_type | solution.py:103
  1256.4 170.1 %while.57 = (s32[]{:T(128)}, f32[1,1024,12,64]{1,3,2,0:T(8,128)}, f32[1,1024,12,64]{1,3,2,0:T(8,128)}, bf16[2,1,512,12,64]{2,4,3,1,0:T(8,128)(2,1)}, s32[2]{0:T(...) while((s32[]{:T(128)}, f32[1,1024,12,64]{1,3,2,0:T(8,128)}, ...), condition=%wide.region_46.47_spmd.clone, body=%wide.region_44.46_spmd.clone.sunk | while | flops 4106348544 | bytes 217235760 | solution.py:124
  1300.7 21.5 %multiply_convert_fusion.9 = bf16[12,512,1024]{2,1,0:T(8,128)(2,1)} fusion(f32[12,512,1024]{2,1,0:T(8,128)} %get-tuple-element.715, f32[12,512,1024]{2,1,0:T(8,128)} %fusion.359, f32[12,512]{1,0:T(8,128)S(1)} %get-tuple-element.716, f32[12,512]{1,0:T(8,128)S(1)} %dynamic-slice_bitcast_fusion.5), kind=kLoop, calls=%fused_computation.62.clone.1 | loop fusion | flops 31457280 | bytes 62963712 | tf_op jit(solution)/shard_map/while/body/eval_jaxpr/convert_element_type | solution.py:103
  1471.9 46.7 %all-reduce = (f32[768]{0:T(1024)}, f32[768]{0:T(1024)}, f32[768,16]{0,1:T(8,128)}, f32[16,16]{0,1:T(8,128)S(1)}) all-reduce(f32[768]{0:T(1024)S(1)} %add.254, f32[768]{0:T(1024)S(1)} %add.257, f32[768,16]{0,1:T(8,128)S(1)} %copy-done.79, f32[16,16]{0,1:T(8,128)S(1)} %copy-done.134), channel_id=1, replica_groups=mesh['wide'=16,'narrow'=2] {'wide','narrow'}, use_global_device_ids=true, to_apply=%region_51.52 | all-reduce | flops 14080 | bytes 112640 | tf_op jit(solution)/shard_map/psum | solution.py:267
  1527.3 111.6 %all-reduce.4.cloned.1.call-done = (f32[768,2304]{1,0:T(8,128)}, f32[768,768]{1,0:T(8,128)}) async-done(((f32[768,2304]{1,0:T(8,128)}, f32[768,768]{1,0:T(8,128)}), (f32[768,2304]{1,0:T(8,128)}, f32[768,768]{1,0:T(8,128)})) %all-reduce.4.cloned.1.call-update) | async-done | bytes 9437200 | tf_op jit(solution)/shard_map/psum | solution.py:267
  (586 shorter events, 817.6 us)
Async XLA Ops:
  7.2 319.8 %copy-start = (bf16[1,768,1536]{2,1,0:T(8,128)(2,1)S(1)}, bf16[1,768,1536]{2,1,0:T(8,128)(2,1)}, u32[]{:S(2)}) copy-start(bf16[1,768,1536]{2,1,0:T(8,128)(2,1)} %param.36) | copy-start | bytes 7077892
  7.2 319.8 %all-gather.5.cloned.1.call-start = ((), (), s32[]{:S(2)}) async-start(), calls=%async_computation.12 | async-start | bytes 4718592 | tf_op jit(solution)/shard_map/all_gather | solution.py:198
  281.5 131.7 %reduce-scatter.5.cloned.1.call-start = ((), (), s32[]{:S(2)}) async-start(), calls=%async_computation.13 | async-start | bytes 4718592 | tf_op jit(solution)/shard_map/reduce_scatter | solution.py:202
  413.2 37.7 %all-to-all-start.1 = ((bf16[16,64,768]{2,1,0:T(8,128)(2,1)}), bf16[16,64,768]{2,1,0:T(8,128)(2,1)}, u32[]{:S(2)}, u32[]{:S(2)}) async-start(bf16[16,64,768]{2,1,0:T(8,128)(2,1)} %bitcast.472), calls=%async_computation.2 | async-start | bytes 3145728 | tf_op jit(solution)/shard_map/all_to_all | solution.py:205
  418.9 129.5 %all-gather.9.cloned.1.call-start = ((), (), s32[]{:S(2)}) async-start(), calls=%async_computation.16 | async-start | bytes 4718592 | tf_op jit(solution)/shard_map/all_gather | solution.py:228
  419.0 435.3 %copy-start.80 = (f32[16,16]{0,1:T(8,128)}, f32[16,16]{0,1:T(8,128)S(1)}, u32[]{:S(2)}) copy-start(f32[16,16]{0,1:T(8,128)S(1)} %copy.56) | copy-start | bytes 3076
  425.5 428.8 %copy-start.150 = (f32[16]{0:T(128)}, f32[16]{0:T(128)S(1)}, u32[]{:S(2)}) copy-start(f32[16]{0:T(128)S(1)} %add_rsqrt_fusion.2) | copy-start | bytes 196
  427.2 473.0 %copy-start.62 = (f32[1024,16]{0,1:T(8,128)}, f32[1024,16]{0,1:T(8,128)S(1)}, u32[]{:S(2)}) copy-start(f32[1024,16]{0,1:T(8,128)S(1)} %get-tuple-element.465) | copy-start | bytes 196612
  427.2 472.9 %copy-start.90 = (f32[1024]{0:T(1024)}, f32[1024]{0:T(1024)S(1)}, u32[]{:S(2)}) copy-start(f32[1024]{0:T(1024)S(1)} %add_rsqrt_fusion.1) | copy-start | bytes 12292
  427.5 195.6 %copy-start.68 = (f32[1024,16]{0,1:T(8,128)}, f32[1024,16]{0,1:T(8,128)S(1)}, u32[]{:S(2)}) copy-start(f32[1024,16]{0,1:T(8,128)S(1)} %get-tuple-element.467) | copy-start | bytes 196612
  427.5 195.6 %copy-start.110 = (f32[1024]{0:T(1024)}, f32[1024]{0:T(1024)S(1)}, u32[]{:S(2)}) copy-start(f32[1024]{0:T(1024)S(1)} %get-tuple-element.466) | copy-start | bytes 12292
  427.6 195.6 %copy-start.114 = (f32[1024]{0:T(1024)}, f32[1024]{0:T(1024)S(1)}, u32[]{:S(2)}) copy-start(f32[1024]{0:T(1024)S(1)} %fusion.213) | copy-start | bytes 12292
  456.6 166.6 %copy-start.152 = (f32[1024]{0:T(1024)}, f32[1024]{0:T(1024)S(1)}, u32[]{:S(2)}) copy-start(f32[1024]{0:T(1024)S(1)} %get-tuple-element.468) | copy-start | bytes 12292
  503.9 113.6 %reduce-scatter.9.cloned.1.call-start = ((), (), s32[]{:S(2)}) async-start(), calls=%async_computation.17 | async-start | bytes 4718592 | tf_op jit(solution)/shard_map/reduce_scatter | solution.py:234
  617.5 37.7 %all-to-all-start.5 = ((bf16[16,64,768]{2,1,0:T(8,128)(2,1)}), bf16[16,64,768]{2,1,0:T(8,128)(2,1)}, u32[]{:S(2)}, u32[]{:S(2)}) async-start(bf16[16,64,768]{2,1,0:T(8,128)(2,1)} %bitcast.476), calls=%async_computation.8 | async-start | bytes 3145728 | tf_op jit(solution)/shard_map/all_to_all | solution.py:237
  623.1 134.5 %all-gather.7.cloned.1.call-start = ((), (), s32[]{:S(2)}) async-start(), calls=%async_computation.14 | async-start | bytes 4718592 | tf_op jit(solution)/shard_map/all_gather | solution.py:198
  713.1 130.6 %reduce-scatter.7.cloned.1.call-start = ((), (), s32[]{:S(2)}) async-start(), calls=%async_computation.15 | async-start | bytes 4718592 | tf_op jit(solution)/shard_map/reduce_scatter | solution.py:202
  843.7 37.7 %all-to-all-start.3 = ((bf16[16,64,768]{2,1,0:T(8,128)(2,1)}), bf16[16,64,768]{2,1,0:T(8,128)(2,1)}, u32[]{:S(2)}, u32[]{:S(2)}) async-start(bf16[16,64,768]{2,1,0:T(8,128)(2,1)} %bitcast.475), calls=%async_computation.5 | async-start | bytes 3145728 | tf_op jit(solution)/shard_map/all_to_all | solution.py:205
  890.9 41.2 %all-to-all-start.6 = ((bf16[16,64,768]{2,1,0:T(8,128)(2,1)}), bf16[16,64,768]{2,1,0:T(8,128)(2,1)}, u32[]{:S(2)}, u32[]{:S(2)}) async-start(bf16[16,64,768]{2,1,0:T(8,128)(2,1)} %bitcast.477), calls=%async_computation.9 | async-start | bytes 3145728 | tf_op jit(solution)/shard_map/all_to_all | solution.py:225
  900.1 80.6 %all-gather.11.cloned.1.call-start = ((), (), s32[]{:S(2)}) async-start(), calls=%async_computation.18 | async-start | bytes 4718592 | tf_op jit(solution)/shard_map/all_gather | solution.py:228
  932.2 268.7 %reduce-scatter.11.cloned.1.call-start = ((), (), s32[]{:S(2)}) async-start(), calls=%async_computation.19 | async-start | bytes 4718592 | tf_op jit(solution)/shard_map/reduce_scatter | solution.py:234
  1200.9 37.7 %all-to-all-start.7 = ((bf16[16,64,768]{2,1,0:T(8,128)(2,1)}), bf16[16,64,768]{2,1,0:T(8,128)(2,1)}, u32[]{:S(2)}, u32[]{:S(2)}) async-start(bf16[16,64,768]{2,1,0:T(8,128)(2,1)} %bitcast.471), calls=%async_computation.11 | async-start | bytes 3145728 | tf_op jit(solution)/shard_map/all_to_all | solution.py:237
  1206.6 432.3 %all-reduce.4.cloned.1.call-start = ((), (), s32[]{:S(2)}) async-start(), calls=%async_computation.20 | async-start | bytes 18874368 | tf_op jit(solution)/shard_map/psum | solution.py:267
  1467.1 52.2 %copy-start.35 = (bf16[1,1024,768]{1,2,0:T(8,128)(2,1)S(1)}, bf16[1,1024,768]{1,2,0:T(8,128)(2,1)}, u32[]{:S(2)}) copy-start(bf16[1,1024,768]{1,2,0:T(8,128)(2,1)} %get-tuple-element.448) | copy-start | bytes 4718596
  (174 other events, 1090.3 us)
Sparse Core Ops, SparseCore 0:
  281.6 45.3 all-gather.4
  369.8 43.3 reduce-scatter.4
  504.0 44.3 all-gather.8
  574.0 43.3 reduce-scatter.8
  713.2 44.3 all-gather.6
  800.3 43.3 reduce-scatter.6
  932.3 48.4 all-gather.10
  1006.1 43.3 reduce-scatter.10
  1443.2 195.6 all-reduce.3
where the time goes:
time: 1660 us; the launch traced here: 1650 us
  matrix products  599 us (36%)
  waiting for transfers between devices  528 us (32%)
  blocking collectives  180 us (11%)
  other arithmetic  169 us (10%)
  local copies, waits for them, and re-layouts  110 us (7%)
  starting transfers between devices  32.2 us (2%)
  loops' own time  19 us (1%)
    psum x1, waiting for transfers between devices, local(): lax.psum((acc_gain_one, acc_qkv, acc_wo, acc_gain_two, acc_route, acc_emb...  112 us
    dot_general x8, matrix products, one_block(): jnp.einsum('sqhd,skhd->shqk', query_block, keys_in, preferred_element_typ...  101 us
    all_gather x2, waiting for transfers between devices, local(): all_rows = lax.all_gather(arrived, 'narrow', axis=0, tiled=True)  89.9 us
    all_to_all x2, blocking collectives, local(): lax.all_to_all(sent_rows, 'wide', split_axis=0, concat_axis=0, tiled=True)  88.4 us
    reduce_scatter x2, waiting for transfers between devices, local(): lax.psum_scatter(partial_rows.astype(jnp.bfloat16), 'narrow', scatter_dim...  87 us
    convert_element_type x4, other arithmetic, one_block(): grad_scores = (soft_weights * (grad_soft - inner_term)).astype(jnp.bfloat16)  86.1 us
    dot_general x14, matrix products, contract_rows(): lax.dot_general(left, right, (((0,), (0,)), ((), ())), precision=precise,...  76.1 us
    all_gather x2, waiting for transfers between devices, local(): grad_all = lax.all_gather(grad_result, 'narrow', axis=0, tiled=True)  68.1 us
  transfers between devices with their start and end apart: 14, of which 13 were waited for; matrix products, arithmetic and copies ran while one was open for 17% of the time, Pallas kernels for 0%

commit v1 on v0

v1 whole, which is shorter than its diff:
```python
import functools

import jax
import jax.numpy as jnp
from jax import lax
from jax.experimental import pallas as pl
from jax.experimental.pallas import tpu as pltpu
from jax.sharding import PartitionSpec as P

D = 768
HEADS = 12
HEAD_DIM = 64
LENGTH = 1024
PAIR = 2 * HEAD_DIM
NN = (((1,), (0,)), ((), ()))
NT = (((1,), (1,)), ((), ()))
TN = (((0,), (0,)), ((), ()))
LOW = jnp.bfloat16
F32 = jnp.float32
VMEM_BYTES = 60 << 20


def dot(left, right, dims=NN, precise=None):
    return lax.dot_general(left, right, dims, precision=precise, preferred_element_type=F32)


def layer_norm(values, gain_vec):
    centred = values - jnp.mean(values, axis=-1, keepdims=True)
    spread_sq = jnp.mean(centred * centred, axis=-1, keepdims=True)
    return centred * lax.rsqrt(spread_sq + 1e-05) * gain_vec


def gate_from(projected, embed_rows, route_row):
    unit_rows = projected * lax.rsqrt(jnp.sum(projected * projected, axis=-1, keepdims=True) + 1.0)
    anchor = embed_rows * lax.rsqrt(jnp.sum(embed_rows * embed_rows, axis=-1, keepdims=True) + 1.0)
    logits = 3.0 * jnp.dot(
        unit_rows, anchor.T, precision=lax.Precision.HIGHEST, preferred_element_type=F32
    )
    soft_rows = jax.nn.softmax(logits, axis=-1)
    picked = route_row[:, None] == jnp.arange(soft_rows.shape[1], dtype=jnp.int32)[None, :]
    return jnp.sum(jnp.where(picked, soft_rows, 0.0), axis=-1)


def attention_forward_kernel(q_ref, k_ref, v_ref, mixed_ref, soft_ref, inv_ref, *, rows):
    lane = lax.broadcasted_iota(jnp.int32, (1, PAIR), 1)
    keys, values = k_ref[...], v_ref[...]
    none = jnp.zeros_like(keys)
    for block in range(LENGTH // rows):
        part = slice(block * rows, (block + 1) * rows)
        query = q_ref[part, :] * LOW(HEAD_DIM**-0.5)
        mixed, inverses = None, []
        for head in range(2):
            mine = (lane < HEAD_DIM) if head == 0 else (lane >= HEAD_DIM)
            scores = dot(query, jnp.where(mine, keys, none), NT)
            top = jnp.max(scores, axis=1, keepdims=True)
            weights = jnp.exp(scores - top)
            inverse = 1.0 / jnp.sum(weights, axis=1, keepdims=True)
            weights = weights.astype(LOW)
            soft_ref[head, part, :] = weights
            inverses.append(jnp.broadcast_to(inverse, (rows, PAIR)))
            term = dot(weights, jnp.where(mine, values, none)) * inverse
            mixed = term if mixed is None else mixed + term
        mixed_ref[part, :] = mixed.astype(LOW)
        inv_ref[part, :] = jnp.where(lane < HEAD_DIM, inverses[0], inverses[1])


def attention_forward(qkv_rows):
    pairs = D // PAIR
    columns = lambda first: pl.BlockSpec((LENGTH, PAIR), lambda i: (0, first + i))
    return pl.pallas_call(
        functools.partial(attention_forward_kernel, rows=512),
        grid=(pairs,),
        in_specs=[columns(0), columns(pairs), columns(2 * pairs)],
        out_specs=[columns(0), pl.BlockSpec((2, LENGTH, LENGTH), lambda i: (i, 0, 0)), columns(0)],
        out_shape=[
            jax.ShapeDtypeStruct((LENGTH, D), LOW),
            jax.ShapeDtypeStruct((HEADS, LENGTH, LENGTH), LOW),
            jax.ShapeDtypeStruct((LENGTH, D), F32),
        ],
        compiler_params=pltpu.CompilerParams(vmem_limit_bytes=VMEM_BYTES),
        cost_estimate=pl.CostEstimate(
            flops=20 * 10**9, bytes_accessed=30 * 2**20, transcendentals=HEADS * LENGTH * LENGTH
        ),
        name="attention_forward",
    )(qkv_rows, qkv_rows, qkv_rows)


def attention_backward_kernel(
    q_ref, k_ref, v_ref, grad_ref, mixed_ref, soft_ref, inv_ref, dq_ref, dk_ref, dv_ref, *, rows
):
    lane = lax.broadcasted_iota(jnp.int32, (1, PAIR), 1)
    scale = LOW(HEAD_DIM**-0.5)
    keys, values = k_ref[...], v_ref[...]
    none = jnp.zeros_like(keys)
    dk_parts, dv_parts = [None, None], [None, None]
    for block in range(LENGTH // rows):
        part = slice(block * rows, (block + 1) * rows)
        query_t = (q_ref[part, :] * scale).T
        scaled = grad_ref[part, :].astype(F32) * inv_ref[part, :]
        inner = scaled * mixed_ref[part, :].astype(F32)
        scaled = scaled.astype(LOW)
        scaled_t = scaled.T
        grad_query = None
        for head in range(2):
            mine = (lane < HEAD_DIM) if head == 0 else (lane >= HEAD_DIM)
            own = slice(head * HEAD_DIM, (head + 1) * HEAD_DIM)
            weights = soft_ref[head, part, :]
            grad_soft = dot(scaled, jnp.where(mine, values, none), NT)
            centre = jnp.sum(jnp.where(mine, inner, 0.0), axis=1, keepdims=True)
            grad_scores = (weights.astype(F32) * (grad_soft - centre)).astype(LOW)
            term = dot(grad_scores, jnp.where(mine, keys, none))
            grad_query = term if grad_query is None else grad_query + term
            dk = dot(query_t[own, :], grad_scores)
            dv = dot(scaled_t[own, :], weights)
            dk_parts[head] = dk if dk_parts[head] is None else dk_parts[head] + dk
            dv_parts[head] = dv if dv_parts[head] is None else dv_parts[head] + dv
        dq_ref[part, :] = (grad_query * HEAD_DIM**-0.5).astype(LOW)
    dk_ref[...] = jnp.concatenate(dk_parts, axis=0).T.astype(LOW)
    dv_ref[...] = jnp.concatenate(dv_parts, axis=0).T.astype(LOW)


def attention_backward(qkv_rows, grad_mixed, mixed_rows, soft, inverses):
    pairs = D // PAIR
    columns = lambda first: pl.BlockSpec((LENGTH, PAIR), lambda i: (0, first + i))
    return pl.pallas_call(
        functools.partial(attention_backward_kernel, rows=512),
        grid=(pairs,),
        in_specs=[
            columns(0),
            columns(pairs),
            columns(2 * pairs),
            columns(0),
            columns(0),
            pl.BlockSpec((2, LENGTH, LENGTH), lambda i: (i, 0, 0)),
            columns(0),
        ],
        out_specs=[columns(0)] * 3,
        out_shape=[jax.ShapeDtypeStruct((LENGTH, D), LOW)] * 3,
        compiler_params=pltpu.CompilerParams(vmem_limit_bytes=VMEM_BYTES),
        cost_estimate=pl.CostEstimate(
            flops=25 * 10**9, bytes_accessed=36 * 2**20, transcendentals=0
        ),
        name="attention_backward",
    )(qkv_rows, qkv_rows, qkv_rows, grad_mixed, mixed_rows, soft, inverses)


def gelu_and_slope(values):
    ratio = 1.0 / (1.0 + jnp.abs(values) * (0.3275911 * 0.7071067811865476))
    bell = jnp.exp(values * values * -0.5)
    series = 0.5 * 1.061405429
    for factor in (-1.453152027, 1.421413741, -0.284496736, 0.254829592):
        series = series * ratio + 0.5 * factor
    tail = series * ratio * bell
    below = jnp.where(values >= 0.0, 1.0 - tail, tail)
    return values * below, below + values * bell * 0.3989422804014327


def expert_kernel(rows_ref, cot_ref, gate_ref, in_ref, outer_ref, *rest, more, steps):
    if more:
        old_in, old_outer = rest[:2]
        rest = rest[2:]
    result_ref, sent_ref, din_ref, douter_ref, grad_sc, rows_t, acc_result, acc_sent = rest
    step = pl.program_id(0)

    @pl.when(step == 0)
    def _():
        grad_sc[...] = (cot_ref[...].astype(F32) * gate_ref[...]).astype(LOW)
        rows_t[...] = rows_ref[...].T
        acc_result[...] = jnp.zeros_like(acc_result)
        acc_sent[...] = jnp.zeros_like(acc_sent)

    first, second = in_ref[0], outer_ref[0]
    hidden, slope = gelu_and_slope(dot(rows_ref[...], first))
    hidden = hidden.astype(LOW)
    grad_rows = grad_sc[...]
    grad_pre = (dot(grad_rows, second, NT) * slope).astype(LOW)
    acc_result[...] += dot(hidden, second)
    acc_sent[...] += dot(grad_pre, first, NT)
    din = dot(rows_t[...], grad_pre)
    douter = dot(hidden, grad_rows, TN)
    if more:
        din += old_in[0]
        douter += old_outer[0]
    din_ref[0] = din
    douter_ref[0] = douter

    @pl.when(step == steps - 1)
    def _():
        result_ref[...] = acc_result[...].astype(LOW)
        sent_ref[...] = acc_sent[...].astype(LOW)


def expert_stage(rows, cot, gate, all_in, all_outer, old=()):
    count, width, units = all_in.shape
    height = rows.shape[0]
    tile = min(512, units)
    per = units // tile
    steps = count * per
    whole = lambda shape: pl.BlockSpec(shape, lambda i: (0,) * len(shape))
    in_spec = pl.BlockSpec((1, width, tile), lambda i: (i // per, 0, i % per))
    outer_spec = pl.BlockSpec((1, tile, width), lambda i: (i // per, i % per, 0))
    return pl.pallas_call(
        functools.partial(expert_kernel, more=bool(old), steps=steps),
        grid=(steps,),
        in_specs=[whole((height, width)), whole((height, width)), whole((height, 1)), in_spec, outer_spec]
        + ([in_spec, outer_spec] if old else []),
        out_specs=[whole((height, width)), whole((height, width)), in_spec, outer_spec],
        out_shape=[
            jax.ShapeDtypeStruct((height, width), LOW),
            jax.ShapeDtypeStruct((height, width), LOW),
            jax.ShapeDtypeStruct(all_in.shape, F32),
            jax.ShapeDtypeStruct(all_outer.shape, F32),
        ],
        scratch_shapes=[
            pltpu.VMEM((height, width), LOW),
            pltpu.VMEM((width, height), LOW),
            pltpu.VMEM((height, width), F32),
            pltpu.VMEM((height, width), F32),
        ],
        compiler_params=pltpu.CompilerParams(vmem_limit_bytes=VMEM_BYTES),
        cost_estimate=pl.CostEstimate(
            flops=12 * height * width * units * count, bytes_accessed=34 * 2**20, transcendentals=0
        ),
        name="expert_stage",
    )(rows, cot, gate, all_in, all_outer, *old)


def local(
    tokens,
    grad_out,
    route_ids,
    slot_ids,
    keep_ids,
    gain_one,
    w_query,
    w_key,
    w_value,
    w_out,
    gain_two,
    w_route,
    embed,
    w_in,
    w_outer,
):
    micro_count, tok_count, feat_width = tokens.shape
    narrow_count = lax.axis_size("narrow")
    expert_count = embed.shape[0]
    slot_cap = max(2, tok_count // expert_count)
    slots = expert_count * slot_cap
    w_qkv = jnp.concatenate([w_query, w_key, w_value], axis=1)
    route_float = w_route.astype(F32)
    all_in = lax.all_gather(w_in[0], "narrow", axis=0, tiled=False)
    all_outer = lax.all_gather(w_outer[0], "narrow", axis=0, tiled=False)
    slot_columns = jnp.arange(slots, dtype=jnp.int32)

    def exchange(rows):
        boxes = rows.reshape((expert_count, slot_cap) + rows.shape[1:])
        boxes = lax.all_to_all(boxes, "wide", split_axis=0, concat_axis=0, tiled=True)
        return boxes.reshape(rows.shape)

    tables, cots = [], []
    for m in range(micro_count):
        slot_index = jnp.where(keep_ids[m] > 0, route_ids[m] * slot_cap + slot_ids[m], -1)
        table = (slot_index[:, None] == slot_columns[None, :]).astype(LOW)
        tables.append(table)
        cots.append(exchange(dot(table, grad_out[m], TN).astype(LOW)))

    ahead = []
    for m in range(micro_count):
        inputs = tokens[m].astype(F32)
        normed_one, pull_one = jax.vjp(layer_norm, inputs, gain_one)
        normed_low = normed_one.astype(LOW)
        qkv_rows = dot(normed_low, w_qkv).astype(LOW)
        mixed_rows, soft, inverses = attention_forward(qkv_rows)
        first_sum = inputs + dot(mixed_rows, w_out)
        normed_two, pull_two = jax.vjp(layer_norm, first_sum, gain_two)
        second_low = normed_two.astype(LOW)
        projected = dot(second_low, w_route)
        gate_prob, pull_gate = jax.vjp(
            lambda proj_in, embed_in: gate_from(proj_in, embed_in, route_ids[m]), projected, embed
        )
        sent = exchange(dot(tables[m], second_low, TN).astype(LOW))
        gates = exchange(jnp.sum(tables[m].astype(F32) * gate_prob[:, None], axis=0)[:, None])
        ahead.append(
            (normed_low, pull_one, qkv_rows, mixed_rows, soft, inverses, first_sum, pull_two,
             second_low, gate_prob, pull_gate, sent, gates)
        )

    back = []
    expert_grads = ()
    for m in range(micro_count):
        sent, gates = ahead[m][-2:]
        result, grad_sent, *expert_grads = expert_stage(
            sent, cots[m], gates, all_in, all_outer, tuple(expert_grads)
        )
        back.append((exchange(result), exchange(grad_sent)))
    part_in, part_outer = expert_grads
    grad_in = lax.psum_scatter(part_in.astype(LOW), "narrow", scatter_dimension=0, tiled=False)
    grad_outer = lax.psum_scatter(part_outer.astype(LOW), "narrow", scatter_dimension=0, tiled=False)

    outputs, input_grads, sums = [], [], None
    for m in range(micro_count):
        (normed_low, pull_one, qkv_rows, mixed_rows, soft, inverses, first_sum, pull_two,
         second_low, gate_prob, pull_gate, _, _) = ahead[m]
        back_rows, back_grads = back[m]
        table = tables[m]
        returned = dot(table, back_rows)
        outputs.append((first_sum + gate_prob[:, None] * returned).astype(LOW))
        grad_sum = grad_out[m].astype(F32)
        grad_gate = jnp.sum(grad_sum * returned, axis=-1)
        grad_projected, grad_embed = pull_gate(grad_gate)
        grad_second = dot(table, back_grads) + dot(
            grad_projected, route_float, NT, lax.Precision.HIGHEST
        )
        grad_route = dot(second_low.astype(F32), grad_projected, TN, lax.Precision.HIGHEST)
        grad_first_norm, grad_gain_two = pull_two(grad_second)
        grad_first = grad_sum + grad_first_norm
        grad_branch = grad_first.astype(LOW)
        grad_wo = dot(mixed_rows, grad_branch, TN)
        grad_mixed = dot(grad_branch, w_out, NT).astype(LOW)
        grad_qkv = jnp.concatenate(
            attention_backward(qkv_rows, grad_mixed, mixed_rows, soft, inverses), axis=1
        )
        grad_wqkv = dot(normed_low, grad_qkv, TN)
        grad_input_norm, grad_gain_one = pull_one(dot(grad_qkv, w_qkv, NT))
        input_grads.append((grad_first + grad_input_norm).astype(LOW))
        terms = (grad_gain_one, grad_wqkv, grad_wo, grad_gain_two, grad_route, grad_embed)
        sums = terms if sums is None else tuple(a + b for a, b in zip(sums, terms))
    gain_one_sum, wqkv_sum, wo_sum, gain_two_sum, route_sum, embed_sum = sums
    wqkv_sum, wo_sum = lax.psum((wqkv_sum.astype(LOW), wo_sum.astype(LOW)), ("wide", "narrow"))
    gain_one_sum, gain_two_sum, route_sum, embed_sum = lax.psum(
        (gain_one_sum, gain_two_sum, route_sum, embed_sum), ("wide", "narrow")
    )
    wqkv_sum = wqkv_sum.astype(F32)
    return (
        jnp.stack(outputs),
        jnp.stack(input_grads),
        gain_one_sum,
        wqkv_sum[:, :feat_width],
        wqkv_sum[:, feat_width : 2 * feat_width],
        wqkv_sum[:, 2 * feat_width :],
        wo_sum.astype(F32),
        gain_two_sum,
        route_sum,
        embed_sum,
        grad_in.astype(F32)[None],
        grad_outer.astype(F32)[None],
    )


def solution(mesh):
    tokens_spec = P(None, ("wide", "narrow"), None)
    ids_spec = P(None, ("wide", "narrow"))
    in_spec, outer_spec = P("wide", None, "narrow"), P("wide", "narrow", None)
    return jax.shard_map(
        local,
        mesh=mesh,
        in_specs=(tokens_spec,) * 2 + (ids_spec,) * 3 + (P(),) * 8 + (in_spec, outer_spec),
        out_specs=(tokens_spec,) * 2 + (P(),) * 8 + (in_spec, outer_spec),
        check_vma=False,
    )
```

time: 1660 us -> 895 us (0.54)
  matrix products: 599 us -> 108 us
  waiting for transfers between devices: 528 us -> 314 us
  Pallas kernels: 0 us -> 189 us
  other arithmetic: 169 us -> 50.7 us
  blocking collectives: 180 us -> 87.1 us
  local copies, waits for them, and re-layouts: 110 us -> 52.9 us
  starting transfers between devices: 32.2 us -> 67.5 us
  loops' own time: 19 us -> 0 us
    dot_general x66 -> x26, matrix products: 597 us -> 106 us  [dot(): lax.dot_general(left, right, dims, precision=precise, preferred_element_t...]
    pallas_call x0 -> x6, Pallas kernels: none -> 189 us  [the longest x2 84.9 us: expert_stage(): pl.pallas_call(functools.partial(expert_kernel, more=bool(old), steps=ste...]
    all_gather x4 -> x2, waiting for transfers between devices: 158 us -> 0.01 us  [the longest x1 0.01 us: local(): all_in = lax.all_gather(w_in[0], 'narrow', axis=0, tiled=False)]
    all_to_all x3 -> x1, blocking collectives: 134 us -> 45.3 us  [exchange(): lax.all_to_all(boxes, 'wide', split_axis=0, concat_axis=0, tiled=True)]
    psum x1, waiting for transfers between devices: 112 us -> 48.1 us  [local(): lax.psum((wqkv_sum.astype(LOW), wo_sum.astype(LOW)), ('wide', 'narrow'))]
    convert_element_type x7 -> x8, other arithmetic: 87.7 us -> 28.1 us  [the longest x1 6.56 us: local(): part_outer.astype(LOW)]
    reduce_sum x4, other arithmetic: 44.9 us -> 1.37 us  [the longest x2 1.3 us: local(): jnp.sum(tables[m].astype(F32) * gate_prob[:, None], axis=0)[:, None]]
    all_to_all x5 -> x9, starting transfers between devices: 31.8 us -> 67.3 us  [exchange(): lax.all_to_all(boxes, 'wide', split_axis=0, concat_axis=0, tiled=True)]
  transfers between devices with their start and end apart: 14 -> 14, of which waited for: 13 -> 11; matrix products, arithmetic and copies ran while one was open for 17% -> 19% of each run, Pallas kernels for 0% -> 9%
where the time goes in v1:
time: 895 us; the launch traced here: 885 us
  waiting for transfers between devices  314 us (35%)
  Pallas kernels  189 us (21%)
  matrix products  108 us (12%)
  blocking collectives  87.1 us (10%)
  starting transfers between devices  67.5 us (8%)
  local copies, waits for them, and re-layouts  52.9 us (6%)
  other arithmetic  50.7 us (6%)
  between operations  15.6 us (2%)
    all_to_all x9, waiting for transfers between devices, exchange(): lax.all_to_all(boxes, 'wide', split_axis=0, concat_axis=0, tiled=True)  152 us
    dot_general x26, matrix products, dot(): lax.dot_general(left, right, dims, precision=precise, preferred_element_t...  106 us
    pallas_call x2, Pallas kernels, expert_stage(): pl.pallas_call(functools.partial(expert_kernel, more=bool(old), steps=ste...  84.9 us
    all_to_all x9, starting transfers between devices, exchange(): lax.all_to_all(boxes, 'wide', split_axis=0, concat_axis=0, tiled=True)  67.3 us
    reduce_scatter x1, waiting for transfers between devices, local(): lax.psum_scatter(part_outer.astype(LOW), 'narrow', scatter_dimension=0, t...  57.7 us
    reduce_scatter x1, waiting for transfers between devices, local(): lax.psum_scatter(part_in.astype(LOW), 'narrow', scatter_dimension=0, tile...  55 us
    pallas_call x2, Pallas kernels, attention_backward(): pl.pallas_call(functools.partial(attention_backward_kernel, rows=512), gr...  54.7 us
    pallas_call x2, Pallas kernels, attention_forward(): pl.pallas_call(functools.partial(attention_forward_kernel, rows=512), gri...  49.6 us
  transfers between devices with their start and end apart: 14, of which 11 were waited for; matrix products, arithmetic and copies ran while one was open for 19% of the time, Pallas kernels for 9%

profile of v1, /device:TPU:0, one launch (start us, length us, event | category | flops | bytes accessed | tf_op | source)
XLA Modules:
  0.0 885.2 jit_solution(141640824355962542)
XLA Ops:
  32.8 24.7 %attention_forward.2 = (bf16[1024,768]{1,0:T(8,128)(2,1)}, bf16[12,1024,1024]{2,1,0:T(8,128)(2,1)}, f32[1024,768]{1,0:T(8,128)}) custom-call(bf16[1024,2304]{1,0:T(8,128)(2,1)} %convolution_convert_fusion.1.q_ref.k_ref.v_ref, bf16[1024,2304]{1,0:T(8,128)(2,1)} %convolution_convert_fusion.1.q_ref.k_ref.v_ref, ...), custom_call_target="tpu_custom_call" | custom-call | flops 20000000000 | bytes 31457280 | tf_op jit(solution)/shard_map/attention_forward/pallas_call | solution.py:70
  62.4 24.9 %attention_forward.3 = (bf16[1024,768]{1,0:T(8,128)(2,1)}, bf16[12,1024,1024]{2,1,0:T(8,128)(2,1)}, f32[1024,768]{1,0:T(8,128)}) custom-call(bf16[1024,2304]{1,0:T(8,128)(2,1)} %convolution_convert_fusion.q_ref.k_ref.v_ref, bf16[1024,2304]{1,0:T(8,128)(2,1)} %convolution_convert_fusion.q_ref.k_ref.v_ref, ...), custom_call_target="tpu_custom_call" | custom-call | flops 20000000000 | bytes 31457280 | tf_op jit(solution)/shard_map/attention_forward/pallas_call | solution.py:70
  120.7 28.0 %all-to-all-done.1 = bf16[16,64,768]{2,1,0:T(8,128)(2,1)} async-done(((bf16[16,64,768]{2,1,0:T(8,128)(2,1)}), bf16[16,64,768]{2,1,0:T(8,128)(2,1)}, u32[]{:S(2)}, u32[]{:S(2)}) %all-to-all-start.1) | async-done | bytes 1572896 | tf_op jit(solution)/shard_map/all_to_all | solution.py:258
  148.7 9.1 %all-to-all-start = ((bf16[16,64,768]{2,1,0:T(8,128)(2,1)}), bf16[16,64,768]{2,1,0:T(8,128)(2,1)S(1)}, u32[]{:S(2)}, u32[]{:S(2)}) async-start(bf16[16,64,768]{2,1,0:T(8,128)(2,1)} %bitcast.152), calls=%async_computation | async-start | bytes 3145728 | tf_op jit(solution)/shard_map/all_to_all | solution.py:258
  160.4 29.4 %all-to-all-done = bf16[16,64,768]{2,1,0:T(8,128)(2,1)S(1)} async-done(((bf16[16,64,768]{2,1,0:T(8,128)(2,1)}), bf16[16,64,768]{2,1,0:T(8,128)(2,1)S(1)}, u32[]{:S(2)}, u32[]{:S(2)}) %all-to-all-start) | async-done | bytes 1572896 | tf_op jit(solution)/shard_map/all_to_all | solution.py:258
  190.9 41.8 %expert_stage.2 = (bf16[1024,768]{1,0:T(8,128)(2,1)}, bf16[1024,768]{1,0:T(8,128)(2,1)}, f32[2,768,1536]{2,1,0:T(8,128)}, f32[2,1536,768]{2,1,0:T(8,128)}) custom-call(bf16[1024,768]{1,0:T(8,128)(2,1)} %bitcast.147, bf16[1024,768]{1,0:T(8,128)(2,1)} %bitcast.7.cot_ref, f32[1024,1]{1,0:T(8,128)} %reshape.316.gate_ref, ...), custom_call_target="tpu_custom_call" | custom-call | flops 28991029248 | bytes 35651584 | tf_op jit(solution)/shard_map/expert_stage/pallas_call | solution.py:202
  232.8 45.3 %all_to_all.50 = bf16[16,64,768]{2,1,0:T(8,128)(2,1)} all-to-all(bf16[16,64,768]{2,1,0:T(8,128)(2,1)} %bitcast.154), channel_id=1, replica_groups=mesh['wide'=16,'narrow'=2] {'wide'}, dimensions={0} | all-to-all | bytes 3145728 | tf_op jit(solution)/shard_map/all_to_all | solution.py:258
  298.1 17.3 %all-to-all-done.8 = bf16[16,64,768]{2,1,0:T(8,128)(2,1)} async-done(((bf16[16,64,768]{2,1,0:T(8,128)(2,1)}), bf16[16,64,768]{2,1,0:T(8,128)(2,1)}, u32[]{:S(2)}, u32[]{:S(2)}) %all-to-all-start.8) | async-done | bytes 1572896 | tf_op jit(solution)/shard_map/all_to_all | solution.py:258
  315.4 9.1 %all-to-all-start.5 = ((bf16[16,64,768]{2,1,0:T(8,128)(2,1)}), bf16[16,64,768]{2,1,0:T(8,128)(2,1)}, u32[]{:S(2)}, u32[]{:S(2)}) async-start(bf16[16,64,768]{2,1,0:T(8,128)(2,1)} %bitcast.146), calls=%async_computation.5 | async-start | bytes 3145728 | tf_op jit(solution)/shard_map/all_to_all | solution.py:258
  337.1 19.5 %all-to-all-done.5 = bf16[16,64,768]{2,1,0:T(8,128)(2,1)} async-done(((bf16[16,64,768]{2,1,0:T(8,128)(2,1)}), bf16[16,64,768]{2,1,0:T(8,128)(2,1)}, u32[]{:S(2)}, u32[]{:S(2)}) %all-to-all-start.5) | async-done | bytes 1572896 | tf_op jit(solution)/shard_map/all_to_all | solution.py:258
  356.5 9.3 %all-to-all-start.6 = ((f32[16,64,1]{1,2,0:T(1,128)}), f32[16,64,1]{1,2,0:T(1,128)S(1)}, u32[]{:S(2)}, u32[]{:S(2)}) async-start(f32[16,64,1]{1,2,0:T(1,128)} %reshape_broadcast_in_dim.7), calls=%async_computation.6 | async-start | bytes 16384 | tf_op jit(solution)/shard_map/all_to_all | solution.py:258
  377.9 29.9 %all-to-all-done.4 = bf16[16,64,768]{2,1,0:T(8,128)(2,1)S(1)} async-done(((bf16[16,64,768]{2,1,0:T(8,128)(2,1)}), bf16[16,64,768]{2,1,0:T(8,128)(2,1)S(1)}, u32[]{:S(2)}, u32[]{:S(2)}) %all-to-all-start.4) | async-done | bytes 1572896 | tf_op jit(solution)/shard_map/all_to_all | solution.py:258
  409.0 43.1 %expert_stage.3 = (bf16[1024,768]{1,0:T(8,128)(2,1)}, bf16[1024,768]{1,0:T(8,128)(2,1)}, f32[2,768,1536]{2,1,0:T(8,128)}, f32[2,1536,768]{2,1,0:T(8,128)}) custom-call(bf16[1024,768]{1,0:T(8,128)(2,1)} %bitcast.148, bf16[1024,768]{1,0:T(8,128)(2,1)} %bitcast.18.cot_ref, f32[1024,1]{1,0:T(8,128)} %reshape.317.gate_ref, ...), custom_call_target="tpu_custom_call" | custom-call | flops 28991029248 | bytes 35651584 | tf_op jit(solution)/shard_map/expert_stage/pallas_call | solution.py:202
  452.1 9.3 %all-to-all-start.9 = ((bf16[16,64,768]{2,1,0:T(8,128)(2,1)}), bf16[16,64,768]{2,1,0:T(8,128)(2,1)}, u32[]{:S(2)}, u32[]{:S(2)}) async-start(bf16[16,64,768]{2,1,0:T(8,128)(2,1)} %bitcast.149), calls=%async_computation.9 | async-start | bytes 3145728 | tf_op jit(solution)/shard_map/all_to_all | solution.py:258
  470.2 23.2 %all-to-all-done.9 = bf16[16,64,768]{2,1,0:T(8,128)(2,1)} async-done(((bf16[16,64,768]{2,1,0:T(8,128)(2,1)}), bf16[16,64,768]{2,1,0:T(8,128)(2,1)}, u32[]{:S(2)}, u32[]{:S(2)}) %all-to-all-start.9) | async-done | bytes 1572896 | tf_op jit(solution)/shard_map/all_to_all | solution.py:258
  493.4 9.6 %all-to-all-start.7 = ((bf16[16,64,768]{2,1,0:T(8,128)(2,1)}), bf16[16,64,768]{2,1,0:T(8,128)(2,1)}, u32[]{:S(2)}, u32[]{:S(2)}) async-start(bf16[16,64,768]{2,1,0:T(8,128)(2,1)} %bitcast.19), calls=%async_computation.7 | async-start | bytes 3145728 | tf_op jit(solution)/shard_map/all_to_all | solution.py:258
  503.0 27.3 %attention_backward.2 = (bf16[1024,768]{1,0:T(8,128)(2,1)}, bf16[1024,768]{1,0:T(8,128)(2,1)}, bf16[1024,768]{1,0:T(8,128)(2,1)}) custom-call(bf16[1024,2304]{1,0:T(8,128)(2,1)} %convolution_convert_fusion.1.q_ref.k_ref.v_ref, bf16[1024,2304]{1,0:T(8,128)(2,1)} %convolution_convert_fusion.1.q_ref.k_ref.v_ref, ...), custom_call_target="tpu_custom_call" | custom-call | flops 24999999488 | bytes 37748736 | tf_op jit(solution)/shard_map/attention_backward/pallas_call | solution.py:125
  564.7 27.4 %attention_backward.3 = (bf16[1024,768]{1,0:T(8,128)(2,1)}, bf16[1024,768]{1,0:T(8,128)(2,1)}, bf16[1024,768]{1,0:T(8,128)(2,1)}) custom-call(bf16[1024,2304]{1,0:T(8,128)(2,1)} %convolution_convert_fusion.q_ref.k_ref.v_ref, bf16[1024,2304]{1,0:T(8,128)(2,1)} %convolution_convert_fusion.q_ref.k_ref.v_ref, ...), custom_call_target="tpu_custom_call" | custom-call | flops 24999999488 | bytes 37748736 | tf_op jit(solution)/shard_map/attention_backward/pallas_call | solution.py:125
  617.6 9.5 %fusion.35 = (f32[1024]{0:T(1024)S(1)}, f32[1024,768]{0,1:T(8,128)}) fusion(bf16[1,1024,768]{1,2,0:T(8,128)(2,1)} %copy-done.11, f32[768]{0:T(1024)S(1)} %copy-done.78, f32[1024]{0:T(1024)S(1)} %copy-done.72, bf16[1024,2304]{1,0:T(8,128)(2,1)} %copy-done.46, bf16[768,2304]{1,0:T(8,128)(2,1)} %copy-done.48), kind=kOutput, calls=%fused_computation.50 | convolution fusion | flops 3627809792 | bytes 12987392 | tf_op jit(solution)/shard_map/dot_general | solution.py:24
  635.4 10.2 %fusion.33 = (f32[768]{0:T(1024)S(1)}, f32[1024]{0:T(1024)S(1)}, f32[1024]{0:T(1024)S(1)}, f32[1024,768]{0,1:T(8,128)S(1)}) fusion(f32[1024,768]{0,1:T(8,128)} %get-tuple-element.164, bf16[1,1024,768]{1,2,0:T(8,128)(2,1)} %copy-done.11, f32[1024]{0:T(1024)S(1)} %copy-done.80, f32[1024]{0:T(1024)S(1)} %copy-done.72, f32[1024]{0:T(1024)S(1)} %multiply_multiply_fusion.3, ...), kind=kOutput, calls=%fused_computation.48 | convolution fusion | flops 3636458752 | bytes 17725440 | tf_op jit(solution)/shard_map/dot_general | solution.py:24
  660.1 41.8 %all-reduce = (f32[768]{0:T(1024)}, f32[768]{0:T(1024)}, f32[768,16]{0,1:T(8,128)}, f32[16,16]{0,1:T(8,128)S(1)}) all-reduce(f32[768]{0:T(1024)S(1)} %add.170, f32[768]{0:T(1024)S(1)} %add.173, f32[768,16]{0,1:T(8,128)S(1)} %convolution_add_fusion.2, f32[16,16]{0,1:T(8,128)S(1)} %fusion.98), channel_id=1, replica_groups=mesh['wide'=16,'narrow'=2] {'wide','narrow'}, use_global_device_ids=true, to_apply=%region_35.36 | all-reduce | flops 14080 | bytes 112640 | tf_op jit(solution)/shard_map/psum | solution.py:331
  702.6 48.1 %all-reduce.4.cloned.1.call-done = (bf16[768,2304]{1,0:T(8,128)(2,1)}, bf16[768,768]{1,0:T(8,128)(2,1)}) async-done(((bf16[768,2304]{1,0:T(8,128)(2,1)}, bf16[768,768]{1,0:T(8,128)(2,1)}), (bf16[768,2304]{1,0:T(8,128)(2,1)}, bf16[768,768]{1,0:T(8,128)(2,1)})) %all-reduce.4.cloned.1.call-update) | async-done | bytes 4718608 | tf_op jit(solution)/shard_map/psum | solution.py:330
  756.9 55.0 %reduce-scatter.3.cloned.1.call-done = bf16[1,768,1536]{2,1,0:T(8,128)(2,1)} async-done(((bf16[2,768,1536]{2,1,0:T(8,128)(2,1)}), bf16[1,768,1536]{2,1,0:T(8,128)(2,1)}) %reduce-scatter.3.cloned.1.call-update) | async-done | bytes 2359312 | tf_op jit(solution)/shard_map/reduce_scatter | solution.py:298
  816.4 57.7 %reduce-scatter.5.cloned.1.call-done = bf16[1,1536,768]{2,1,0:T(8,128)(2,1)} async-done(((bf16[2,1536,768]{2,1,0:T(8,128)(2,1)}), bf16[1,1536,768]{2,1,0:T(8,128)(2,1)}) %reduce-scatter.5.cloned.1.call-update) | async-done | bytes 2359312 | tf_op jit(solution)/shard_map/reduce_scatter | solution.py:299
  (324 shorter events, 219.2 us)
Async XLA Ops:
  7.2 50.3 %copy-start = (bf16[768,768]{1,0:T(8,128)(2,1)S(1)}, bf16[768,768]{1,0:T(8,128)(2,1)}, u32[]{:S(2)}) copy-start(bf16[768,768]{1,0:T(8,128)(2,1)} %param.24) | copy-start | bytes 3538948
  7.2 182.6 %all-gather.3.cloned.1.call-start = ((), (), s32[]{:S(2)}) async-start(), calls=%async_computation.12 | async-start | bytes 7077888 | tf_op jit(solution)/shard_map/all_gather | solution.py:252
  17.9 69.5 %copy-start.6 = (bf16[1,1024,768]{1,2,0:T(8,128)(2,1)}, bf16[1,1024,768]{1,2,0:T(8,128)(2,1)S(1)}, u32[]{:S(2)}) copy-start(bf16[1,1024,768]{1,2,0:T(8,128)(2,1)S(1)} %copy.83) | copy-start | bytes 4718596
  96.6 231.6 %copy-start.42 = (f32[1024,16]{0,1:T(8,128)}, f32[1024,16]{0,1:T(8,128)S(1)}, u32[]{:S(2)}) copy-start(f32[1024,16]{0,1:T(8,128)S(1)} %get-tuple-element.144) | copy-start | bytes 196612
  96.6 231.6 %copy-start.53 = (f32[1024]{0:T(1024)}, f32[1024]{0:T(1024)S(1)}, u32[]{:S(2)}) copy-start(f32[1024]{0:T(1024)S(1)} %add_rsqrt_fusion.1) | copy-start | bytes 12292
  96.9 200.9 %copy-start.44 = (f32[1024,16]{0,1:T(8,128)}, f32[1024,16]{0,1:T(8,128)S(1)}, u32[]{:S(2)}) copy-start(f32[1024,16]{0,1:T(8,128)S(1)} %get-tuple-element.146) | copy-start | bytes 196612
  96.9 200.9 %copy-start.55 = (f32[1024]{0:T(1024)}, f32[1024]{0:T(1024)S(1)}, u32[]{:S(2)}) copy-start(f32[1024]{0:T(1024)S(1)} %get-tuple-element.145) | copy-start | bytes 12292
  97.0 200.8 %copy-start.69 = (f32[1024]{0:T(1024)}, f32[1024]{0:T(1024)S(1)}, u32[]{:S(2)}) copy-start(f32[1024]{0:T(1024)S(1)} %fusion.91) | copy-start | bytes 12292
  97.0 200.8 %copy-start.57 = (s32[1,1024]{1,0:T(1,128)}, s32[1,1024]{1,0:T(1,128)S(1)}, u32[]{:S(2)}) copy-start(s32[1,1024]{1,0:T(1,128)S(1)} %get-tuple-element.134) | copy-start | bytes 12292
  98.4 13.9 %all-to-all-start.2 = ((f32[16,64,1]{1,2,0:T(1,128)}), f32[16,64,1]{1,2,0:T(1,128)S(1)}, u32[]{:S(2)}, u32[]{:S(2)}) async-start(f32[16,64,1]{1,2,0:T(1,128)} %reshape_broadcast_in_dim.6), calls=%async_computation.2 | async-start | bytes 16384 | tf_op jit(solution)/shard_map/all_to_all | solution.py:258
  112.4 36.4 %all-to-all-start.1 = ((bf16[16,64,768]{2,1,0:T(8,128)(2,1)}), bf16[16,64,768]{2,1,0:T(8,128)(2,1)}, u32[]{:S(2)}, u32[]{:S(2)}) async-start(bf16[16,64,768]{2,1,0:T(8,128)(2,1)} %bitcast.150), calls=%async_computation.1 | async-start | bytes 3145728 | tf_op jit(solution)/shard_map/all_to_all | solution.py:258
  116.8 73.0 %all-gather.5.cloned.1.call-start = ((), (), s32[]{:S(2)}) async-start(), calls=%async_computation.13 | async-start | bytes 7077888 | tf_op jit(solution)/shard_map/all_gather | solution.py:253
  148.7 41.1 %all-to-all-start = ((bf16[16,64,768]{2,1,0:T(8,128)(2,1)}), bf16[16,64,768]{2,1,0:T(8,128)(2,1)S(1)}, u32[]{:S(2)}, u32[]{:S(2)}) async-start(bf16[16,64,768]{2,1,0:T(8,128)(2,1)} %bitcast.152), calls=%async_computation | async-start | bytes 3145728 | tf_op jit(solution)/shard_map/all_to_all | solution.py:258
  278.1 37.3 %all-to-all-start.8 = ((bf16[16,64,768]{2,1,0:T(8,128)(2,1)}), bf16[16,64,768]{2,1,0:T(8,128)(2,1)}, u32[]{:S(2)}, u32[]{:S(2)}) async-start(bf16[16,64,768]{2,1,0:T(8,128)(2,1)} %bitcast.22), calls=%async_computation.8 | async-start | bytes 3145728 | tf_op jit(solution)/shard_map/all_to_all | solution.py:258
  297.8 30.4 %copy-start.86 = (f32[1024]{0:T(1024)}, f32[1024]{0:T(1024)S(1)}, u32[]{:S(2)}) copy-start(f32[1024]{0:T(1024)S(1)} %get-tuple-element.147) | copy-start | bytes 12292
  315.4 41.2 %all-to-all-start.5 = ((bf16[16,64,768]{2,1,0:T(8,128)(2,1)}), bf16[16,64,768]{2,1,0:T(8,128)(2,1)}, u32[]{:S(2)}, u32[]{:S(2)}) async-start(bf16[16,64,768]{2,1,0:T(8,128)(2,1)} %bitcast.146), calls=%async_computation.5 | async-start | bytes 3145728 | tf_op jit(solution)/shard_map/all_to_all | solution.py:258
  335.0 34.0 %copy-start.16 = (bf16[1024,768]{0,1:T(8,128)(2,1)}, bf16[1024,768]{0,1:T(8,128)(2,1)S(1)}, u32[]{:S(2)}) copy-start(bf16[1024,768]{0,1:T(8,128)(2,1)S(1)} %get-tuple-element.140) | copy-start | bytes 4718596
  356.5 15.7 %all-to-all-start.6 = ((f32[16,64,1]{1,2,0:T(1,128)}), f32[16,64,1]{1,2,0:T(1,128)S(1)}, u32[]{:S(2)}, u32[]{:S(2)}) async-start(f32[16,64,1]{1,2,0:T(1,128)} %reshape_broadcast_in_dim.7), calls=%async_computation.6 | async-start | bytes 16384 | tf_op jit(solution)/shard_map/all_to_all | solution.py:258
  372.2 35.6 %all-to-all-start.4 = ((bf16[16,64,768]{2,1,0:T(8,128)(2,1)}), bf16[16,64,768]{2,1,0:T(8,128)(2,1)S(1)}, u32[]{:S(2)}, u32[]{:S(2)}) async-start(bf16[16,64,768]{2,1,0:T(8,128)(2,1)} %bitcast.153), calls=%async_computation.4 | async-start | bytes 3145728 | tf_op jit(solution)/shard_map/all_to_all | solution.py:258
  452.1 41.3 %all-to-all-start.9 = ((bf16[16,64,768]{2,1,0:T(8,128)(2,1)}), bf16[16,64,768]{2,1,0:T(8,128)(2,1)}, u32[]{:S(2)}, u32[]{:S(2)}) async-start(bf16[16,64,768]{2,1,0:T(8,128)(2,1)} %bitcast.149), calls=%async_computation.9 | async-start | bytes 3145728 | tf_op jit(solution)/shard_map/all_to_all | solution.py:258
  493.4 56.0 %all-to-all-start.7 = ((bf16[16,64,768]{2,1,0:T(8,128)(2,1)}), bf16[16,64,768]{2,1,0:T(8,128)(2,1)}, u32[]{:S(2)}, u32[]{:S(2)}) async-start(bf16[16,64,768]{2,1,0:T(8,128)(2,1)} %bitcast.19), calls=%async_computation.7 | async-start | bytes 3145728 | tf_op jit(solution)/shard_map/all_to_all | solution.py:258
  503.0 247.8 %all-reduce.4.cloned.1.call-start = ((), (), s32[]{:S(2)}) async-start(), calls=%async_computation.16 | async-start | bytes 9437184 | tf_op jit(solution)/shard_map/psum | solution.py:330
  604.4 207.4 %reduce-scatter.3.cloned.1.call-start = ((), (), s32[]{:S(2)}) async-start(), calls=%async_computation.14 | async-start | bytes 7077888 | tf_op jit(solution)/shard_map/reduce_scatter | solution.py:298
  610.9 263.2 %reduce-scatter.5.cloned.1.call-start = ((), (), s32[]{:S(2)}) async-start(), calls=%async_computation.15 | async-start | bytes 7077888 | tf_op jit(solution)/shard_map/reduce_scatter | solution.py:299
  (83 other events, 447.9 us)
Sparse Core Ops, SparseCore 0:
  9.6 65.3 all-gather.2
  119.2 63.9 all-gather.4
  604.5 146.1 all-reduce.3
  753.0 58.8 reduce-scatter.2
  814.0 59.9 reduce-scatter.4

commit v2 on v1

--- a/solution.py
+++ b/solution.py
@@ -39,6 +39,82 @@
     soft_rows = jax.nn.softmax(logits, axis=-1)
     picked = route_row[:, None] == jnp.arange(soft_rows.shape[1], dtype=jnp.int32)[None, :]
     return jnp.sum(jnp.where(picked, soft_rows, 0.0), axis=-1)
+
+
+MESH = pl.DeviceIdType.MESH
+
+
+def call_with_moves(body, moves, cid, *, grid, in_specs, out_specs, out_shape, scratch_shapes=(), cost, name, args):
+    members = lax.axis_size("wide")
+    n_in, n_out, n_moves, n_scratch = len(in_specs), len(out_specs), len(moves), len(scratch_shapes)
+
+    def kernel(*refs):
+        ins, refs = refs[:n_in], refs[n_in:]
+        sources, refs = refs[:n_moves], refs[n_moves:]
+        outs, refs = refs[:n_out], refs[n_out:]
+        targets, refs = refs[:n_moves], refs[n_moves:]
+        scratch, refs = refs[:n_scratch], refs[n_scratch:]
+        stages, (send_sem, recv_sem, own_sem) = refs[:n_moves], refs[n_moves:]
+        me = lax.axis_index("wide")
+        step = pl.program_id(0)
+
+        def remote(i, d):
+            peer = lax.rem(me + d, members)
+            return pltpu.make_async_remote_copy(
+                src_ref=sources[i].at[peer],
+                dst_ref=targets[i].at[me],
+                send_sem=send_sem.at[i, d],
+                recv_sem=recv_sem.at[i, d],
+                device_id={"wide": peer},
+                device_id_type=MESH,
+            )
+
+        @pl.when(step == 0)
+        def _():
+            barrier = pltpu.get_barrier_semaphore()
+            for d in range(1, members):
+                pl.semaphore_signal(
+                    barrier, inc=1, device_id={"wide": lax.rem(me + d, members)}, device_id_type=MESH
+                )
+            pl.semaphore_wait(barrier, members - 1)
+            for i in range(n_moves):
+                for d in range(1, members):
+                    remote(i, d).start()
+                pltpu.make_async_copy(sources[i].at[me], stages[i], own_sem.at[i]).start()
+
+        body(*ins, *outs, *scratch)
+
+        @pl.when(step == grid[0] - 1)
+        def _():
+            for i in range(n_moves):
+                pltpu.make_async_copy(sources[i].at[me], stages[i], own_sem.at[i]).wait()
+                pltpu.make_async_copy(stages[i], targets[i].at[me], own_sem.at[i]).start()
+            for i in range(n_moves):
+                pltpu.make_async_copy(stages[i], targets[i].at[me], own_sem.at[i]).wait()
+                for d in range(1, members):
+                    remote(i, d).wait()
+
+    anywhere = pl.BlockSpec(memory_space=pl.ANY)
+    results = pl.pallas_call(
+        kernel,
+        grid=grid,
+        in_specs=list(in_specs) + [anywhere] * n_moves,
+        out_specs=list(out_specs) + [anywhere] * n_moves,
+        out_shape=list(out_shape) + [jax.ShapeDtypeStruct(a.shape, a.dtype) for a in moves],
+        scratch_shapes=list(scratch_shapes)
+        + [pltpu.VMEM(a.shape[1:], a.dtype) for a in moves]
+        + [
+            pltpu.SemaphoreType.DMA((n_moves, members)),
+            pltpu.SemaphoreType.DMA((n_moves, members)),
+            pltpu.SemaphoreType.DMA((n_moves,)),
+        ],
+        compiler_params=pltpu.CompilerParams(
+            vmem_limit_bytes=VMEM_BYTES, collective_id=cid, has_side_effects=True
+        ),
+        cost_estimate=cost,
+        name=name,
+    )(*args, *moves)
+    return results[:n_out], results[n_out:]
 
 
 def attention_forward_kernel(q_ref, k_ref, v_ref, mixed_ref, soft_ref, inv_ref, *, rows):
@@ -64,11 +140,13 @@
         inv_ref[part, :] = jnp.where(lane < HEAD_DIM, inverses[0], inverses[1])
 
 
-def attention_forward(qkv_rows):
+def attention_forward(qkv_rows, moves, cid):
     pairs = D // PAIR
     columns = lambda first: pl.BlockSpec((LENGTH, PAIR), lambda i: (0, first + i))
-    return pl.pallas_call(
+    return call_with_moves(
         functools.partial(attention_forward_kernel, rows=512),
+        moves,
+        cid,
         grid=(pairs,),
         in_specs=[columns(0), columns(pairs), columns(2 * pairs)],
         out_specs=[columns(0), pl.BlockSpec((2, LENGTH, LENGTH), lambda i: (i, 0, 0)), columns(0)],
@@ -77,12 +155,12 @@
             jax.ShapeDtypeStruct((HEADS, LENGTH, LENGTH), LOW),
             jax.ShapeDtypeStruct((LENGTH, D), F32),
         ],
-        compiler_params=pltpu.CompilerParams(vmem_limit_bytes=VMEM_BYTES),
-        cost_estimate=pl.CostEstimate(
+        cost=pl.CostEstimate(
             flops=20 * 10**9, bytes_accessed=30 * 2**20, transcendentals=HEADS * LENGTH * LENGTH
         ),
         name="attention_forward",
-    )(qkv_rows, qkv_rows, qkv_rows)
+        args=(qkv_rows, qkv_rows, qkv_rows),
+    )
 
 
 def attention_backward_kernel(
@@ -119,11 +197,13 @@
     dv_ref[...] = jnp.concatenate(dv_parts, axis=0).T.astype(LOW)
 
 
-def attention_backward(qkv_rows, grad_mixed, mixed_rows, soft, inverses):
+def attention_backward(qkv_rows, grad_mixed, mixed_rows, soft, inverses, moves, cid):
     pairs = D // PAIR
     columns = lambda first: pl.BlockSpec((LENGTH, PAIR), lambda i: (0, first + i))
-    return pl.pallas_call(
+    return call_with_moves(
         functools.partial(attention_backward_kernel, rows=512),
+        moves,
+        cid,
         grid=(pairs,),
         in_specs=[
             columns(0),
@@ -136,12 +216,10 @@
         ],
         out_specs=[columns(0)] * 3,
         out_shape=[jax.ShapeDtypeStruct((LENGTH, D), LOW)] * 3,
-        compiler_params=pltpu.CompilerParams(vmem_limit_bytes=VMEM_BYTES),
-        cost_estimate=pl.CostEstimate(
-            flops=25 * 10**9, bytes_accessed=36 * 2**20, transcendentals=0
-        ),
+        cost=pl.CostEstimate(flops=25 * 10**9, bytes_accessed=36 * 2**20, transcendentals=0),
         name="attention_backward",
-    )(qkv_rows, qkv_rows, qkv_rows, grad_mixed, mixed_rows, soft, inverses)
+        args=(qkv_rows, qkv_rows, qkv_rows, grad_mixed, mixed_rows, soft, inverses),
+    )
 
 
 def gelu_and_slope(values):
@@ -155,16 +233,25 @@
     return values * below, below + values * bell * 0.3989422804014327
 
 
-def expert_kernel(rows_ref, cot_ref, gate_ref, in_ref, outer_ref, *rest, more, steps):
+def diagonal(slot_cap):
+    shape = (slot_cap, 128)
+    return lax.broadcasted_iota(jnp.int32, shape, 0) == lax.broadcasted_iota(jnp.int32, shape, 1)
+
+
+def expert_kernel(rows_ref, cot_ref, gate_ref, in_ref, outer_ref, *rest, more, steps, slot_cap):
     if more:
         old_in, old_outer = rest[:2]
         rest = rest[2:]
-    result_ref, sent_ref, din_ref, douter_ref, grad_sc, rows_t, acc_result, acc_sent = rest
+    result_ref, sent_ref, dots_ref, din_ref, douter_ref, grad_sc, rows_t, acc_result, acc_sent = rest
     step = pl.program_id(0)
+    sources = rows_ref.shape[0] // slot_cap
 
     @pl.when(step == 0)
     def _():
-        grad_sc[...] = (cot_ref[...].astype(F32) * gate_ref[...]).astype(LOW)
+        for w in range(sources):
+            part = slice(w * slot_cap, (w + 1) * slot_cap)
+            gate = jnp.sum(jnp.where(diagonal(slot_cap), gate_ref[w, 0:1, :], 0.0), axis=1, keepdims=True)
+            grad_sc[part, :] = (cot_ref[part, :].astype(F32) * gate).astype(LOW)
         rows_t[...] = rows_ref[...].T
         acc_result[...] = jnp.zeros_like(acc_result)
         acc_sent[...] = jnp.zeros_like(acc_sent)
@@ -186,11 +273,18 @@
 
     @pl.when(step == steps - 1)
     def _():
-        result_ref[...] = acc_result[...].astype(LOW)
+        result = acc_result[...].astype(LOW)
+        result_ref[...] = result
         sent_ref[...] = acc_sent[...].astype(LOW)
-
-
-def expert_stage(rows, cot, gate, all_in, all_outer, old=()):
+        for w in range(sources):
+            part = slice(w * slot_cap, (w + 1) * slot_cap)
+            products = cot_ref[part, :].astype(F32) * result[part, :].astype(F32)
+            column = jnp.sum(products, axis=1, keepdims=True)
+            row = jnp.sum(jnp.where(diagonal(slot_cap), column, 0.0), axis=0, keepdims=True)
+            dots_ref[w] = jnp.broadcast_to(row, (8, 128))
+
+
+def expert_stage(rows, cot, gates, all_in, all_outer, old, slot_cap, moves, cid):
     count, width, units = all_in.shape
     height = rows.shape[0]
     tile = min(512, units)
@@ -199,15 +293,18 @@
     whole = lambda shape: pl.BlockSpec(shape, lambda i: (0,) * len(shape))
     in_spec = pl.BlockSpec((1, width, tile), lambda i: (i // per, 0, i % per))
     outer_spec = pl.BlockSpec((1, tile, width), lambda i: (i // per, i % per, 0))
-    return pl.pallas_call(
-        functools.partial(expert_kernel, more=bool(old), steps=steps),
+    return call_with_moves(
+        functools.partial(expert_kernel, more=bool(old), steps=steps, slot_cap=slot_cap),
+        moves,
+        cid,
         grid=(steps,),
-        in_specs=[whole((height, width)), whole((height, width)), whole((height, 1)), in_spec, outer_spec]
+        in_specs=[whole((height, width)), whole((height, width)), whole(gates.shape), in_spec, outer_spec]
         + ([in_spec, outer_spec] if old else []),
-        out_specs=[whole((height, width)), whole((height, width)), in_spec, outer_spec],
+        out_specs=[whole((height, width)), whole((height, width)), whole(gates.shape), in_spec, outer_spec],
         out_shape=[
             jax.ShapeDtypeStruct((height, width), LOW),
             jax.ShapeDtypeStruct((height, width), LOW),
+            jax.ShapeDtypeStruct(gates.shape, F32),
             jax.ShapeDtypeStruct(all_in.shape, F32),
             jax.ShapeDtypeStruct(all_outer.shape, F32),
         ],
@@ -217,12 +314,12 @@
             pltpu.VMEM((height, width), F32),
             pltpu.VMEM((height, width), F32),
         ],
-        compiler_params=pltpu.CompilerParams(vmem_limit_bytes=VMEM_BYTES),
-        cost_estimate=pl.CostEstimate(
+        cost=pl.CostEstimate(
             flops=12 * height * width * units * count, bytes_accessed=34 * 2**20, transcendentals=0
         ),
         name="expert_stage",
-    )(rows, cot, gate, all_in, all_outer, *old)
+        args=(rows, cot, gates, all_in, all_outer, *old),
+    )
 
 
 def local(
@@ -253,25 +350,31 @@
     all_outer = lax.all_gather(w_outer[0], "narrow", axis=0, tiled=False)
     slot_columns = jnp.arange(slots, dtype=jnp.int32)
 
-    def exchange(rows):
-        boxes = rows.reshape((expert_count, slot_cap) + rows.shape[1:])
-        boxes = lax.all_to_all(boxes, "wide", split_axis=0, concat_axis=0, tiled=True)
-        return boxes.reshape(rows.shape)
-
-    tables, cots = [], []
+    def boxes(rows):
+        return rows.reshape((expert_count, slot_cap) + rows.shape[1:])
+
+    def flat(boxed):
+        return boxed.reshape((expert_count * slot_cap,) + boxed.shape[2:])
+
+    tables, cot_boxes = [], []
     for m in range(micro_count):
         slot_index = jnp.where(keep_ids[m] > 0, route_ids[m] * slot_cap + slot_ids[m], -1)
         table = (slot_index[:, None] == slot_columns[None, :]).astype(LOW)
         tables.append(table)
-        cots.append(exchange(dot(table, grad_out[m], TN).astype(LOW)))
-
-    ahead = []
+        cot_boxes.append(boxes(dot(table, grad_out[m], TN).astype(LOW)))
+
+    ahead, send = [], []
     for m in range(micro_count):
         inputs = tokens[m].astype(F32)
         normed_one, pull_one = jax.vjp(layer_norm, inputs, gain_one)
         normed_low = normed_one.astype(LOW)
         qkv_rows = dot(normed_low, w_qkv).astype(LOW)
-        mixed_rows, soft, inverses = attention_forward(qkv_rows)
+        if m == 0:
+            (mixed_rows, soft, inverses), (cot_0,) = attention_forward(qkv_rows, (cot_boxes[0],), 1)
+        else:
+            (mixed_rows, soft, inverses), (sent_0, gates_0, cot_1) = attention_forward(
+                qkv_rows, (*send[0], cot_boxes[1]), 2
+            )
         first_sum = inputs + dot(mixed_rows, w_out)
         normed_two, pull_two = jax.vjp(layer_norm, first_sum, gain_two)
         second_low = normed_two.astype(LOW)
@@ -279,37 +382,35 @@
         gate_prob, pull_gate = jax.vjp(
             lambda proj_in, embed_in: gate_from(proj_in, embed_in, route_ids[m]), projected, embed
         )
-        sent = exchange(dot(tables[m], second_low, TN).astype(LOW))
-        gates = exchange(jnp.sum(tables[m].astype(F32) * gate_prob[:, None], axis=0)[:, None])
+        gates = jnp.sum(tables[m].astype(F32) * gate_prob[:, None], axis=0)
+        gates = jnp.pad(gates.reshape(expert_count, 1, slot_cap), ((0, 0), (0, 7), (0, 128 - slot_cap)))
+        send.append((boxes(dot(tables[m], second_low, TN).astype(LOW)), gates))
         ahead.append(
             (normed_low, pull_one, qkv_rows, mixed_rows, soft, inverses, first_sum, pull_two,
-             second_low, gate_prob, pull_gate, sent, gates)
+             second_low, gate_prob, pull_gate)
         )
 
-    back = []
-    expert_grads = ()
-    for m in range(micro_count):
-        sent, gates = ahead[m][-2:]
-        result, grad_sent, *expert_grads = expert_stage(
-            sent, cots[m], gates, all_in, all_outer, tuple(expert_grads)
-        )
-        back.append((exchange(result), exchange(grad_sent)))
-    part_in, part_outer = expert_grads
+    (result_0, grad_0, dots_0, *expert_grads), (sent_1, gates_1) = expert_stage(
+        flat(sent_0), flat(cot_0), gates_0, all_in, all_outer, (), slot_cap, send[1], 3
+    )
+    (result_1, grad_1, dots_1, part_in, part_outer), (home_grad_0, home_dots_0) = expert_stage(
+        flat(sent_1), flat(cot_1), gates_1, all_in, all_outer, tuple(expert_grads), slot_cap,
+        (boxes(grad_0), dots_0), 4
+    )
     grad_in = lax.psum_scatter(part_in.astype(LOW), "narrow", scatter_dimension=0, tiled=False)
     grad_outer = lax.psum_scatter(part_outer.astype(LOW), "narrow", scatter_dimension=0, tiled=False)
 
-    outputs, input_grads, sums = [], [], None
+    input_grads, sums = [], None
     for m in range(micro_count):
         (normed_low, pull_one, qkv_rows, mixed_rows, soft, inverses, first_sum, pull_two,
-         second_low, gate_prob, pull_gate, _, _) = ahead[m]
-        back_rows, back_grads = back[m]
+         second_low, gate_prob, pull_gate) = ahead[m]
+        home_grad, home_dots = (home_grad_0, home_dots_0) if m == 0 else (home_grad_1, home_dots_1)
         table = tables[m]
-        returned = dot(table, back_rows)
-        outputs.append((first_sum + gate_prob[:, None] * returned).astype(LOW))
         grad_sum = grad_out[m].astype(F32)
-        grad_gate = jnp.sum(grad_sum * returned, axis=-1)
+        slot_dots = home_dots[:, 0, :slot_cap].reshape(slots)
+        grad_gate = jnp.sum(table.astype(F32) * slot_dots[None, :], axis=-1)
         grad_projected, grad_embed = pull_gate(grad_gate)
-        grad_second = dot(table, back_grads) + dot(
+        grad_second = dot(table, flat(home_grad)) + dot(
             grad_projected, route_float, NT, lax.Precision.HIGHEST
         )
         grad_route = dot(second_low.astype(F32), grad_projected, TN, lax.Precision.HIGHEST)
@@ -318,14 +419,25 @@
         grad_branch = grad_first.astype(LOW)
         grad_wo = dot(mixed_rows, grad_branch, TN)
         grad_mixed = dot(grad_branch, w_out, NT).astype(LOW)
-        grad_qkv = jnp.concatenate(
-            attention_backward(qkv_rows, grad_mixed, mixed_rows, soft, inverses), axis=1
-        )
+        if m == 0:
+            grads, (home_grad_1, home_dots_1, home_result_0) = attention_backward(
+                qkv_rows, grad_mixed, mixed_rows, soft, inverses, (boxes(grad_1), dots_1, boxes(result_0)), 5
+            )
+        else:
+            grads, (home_result_1,) = attention_backward(
+                qkv_rows, grad_mixed, mixed_rows, soft, inverses, (boxes(result_1),), 6
+            )
+        grad_qkv = jnp.concatenate(grads, axis=1)
         grad_wqkv = dot(normed_low, grad_qkv, TN)
         grad_input_norm, grad_gain_one = pull_one(dot(grad_qkv, w_qkv, NT))
         input_grads.append((grad_first + grad_input_norm).astype(LOW))
         terms = (grad_gain_one, grad_wqkv, grad_wo, grad_gain_two, grad_route, grad_embed)
         sums = terms if sums is None else tuple(a + b for a, b in zip(sums, terms))
+    outputs = []
+    for m, home_result in enumerate((home_result_0, home_result_1)):
+        first_sum, gate_prob = ahead[m][6], ahead[m][9]
+        returned = dot(tables[m], flat(home_result))
+        outputs.append((first_sum + gate_prob[:, None] * returned).astype(LOW))
     gain_one_sum, wqkv_sum, wo_sum, gain_two_sum, route_sum, embed_sum = sums
     wqkv_sum, wo_sum = lax.psum((wqkv_sum.astype(LOW), wo_sum.astype(LOW)), ("wide", "narrow"))
     gain_one_sum, gain_two_sum, route_sum, embed_sum = lax.psum(

time: 895 us -> 755 us (0.84)
  waiting for transfers between devices: 314 us -> 158 us
  Pallas kernels: 189 us -> 331 us
  starting transfers between devices: 67.5 us -> 0.37 us
  blocking collectives: 87.1 us -> 48.7 us
  matrix products: 108 us -> 95.3 us
    all_to_all x9 -> x0, waiting for transfers between devices: 152 us -> none  [exchange(): lax.all_to_all(boxes, 'wide', split_axis=0, concat_axis=0, tiled=True)]
    pallas_call x6, Pallas kernels: 189 us -> 331 us  [call_with_moves(): pl.pallas_call(kernel, grid=grid, in_specs=list(in_specs) + [anywhere] *...]
    all_to_all x9 -> x0, starting transfers between devices: 67.3 us -> none  [exchange(): lax.all_to_all(boxes, 'wide', split_axis=0, concat_axis=0, tiled=True)]
    all_to_all x1 -> x0, blocking collectives: 45.3 us -> none  [exchange(): lax.all_to_all(boxes, 'wide', split_axis=0, concat_axis=0, tiled=True)]
    dot_general x26, matrix products: 106 us -> 93.9 us  [dot(): lax.dot_general(left, right, dims, precision=precise, preferred_element_t...]
    unnamed x200 -> x152, local copies, waits for them, and re-layouts: 37.4 us -> 37.5 us
  transfers between devices with their start and end apart: 14 -> 5, of which waited for: 11 -> 3; matrix products, arithmetic and copies ran while one was open for 19% -> 17% of each run, Pallas kernels for 9% -> 15%
where the time goes in v2:
time: 755 us; the launch traced here: 747 us
  Pallas kernels  331 us (44%)
  waiting for transfers between devices  158 us (21%)
  matrix products  95.3 us (13%)
  local copies, waits for them, and re-layouts  51.7 us (7%)
  blocking collectives  48.7 us (6%)
  other arithmetic  46.7 us (6%)
  between operations  15.1 us (2%)
    pallas_call x6, Pallas kernels, call_with_moves(): pl.pallas_call(kernel, grid=grid, in_specs=list(in_specs) + [anywhere] *...  331 us
    dot_general x26, matrix products, dot(): lax.dot_general(left, right, dims, precision=precise, preferred_element_t...  93.9 us
    reduce_scatter x1, waiting for transfers between devices, local(): lax.psum_scatter(part_outer.astype(LOW), 'narrow', scatter_dimension=0, t...  57.7 us
    reduce_scatter x1, waiting for transfers between devices, local(): lax.psum_scatter(part_in.astype(LOW), 'narrow', scatter_dimension=0, tile...  55 us
    psum x1, blocking collectives, local(): lax.psum((gain_one_sum, gain_two_sum, route_sum, embed_sum), ('wide', 'na...  48.7 us
    psum x1, waiting for transfers between devices, local(): lax.psum((wqkv_sum.astype(LOW), wo_sum.astype(LOW)), ('wide', 'narrow'))  44.2 us
    unnamed x152, local copies, waits for them, and re-layouts  37.5 us
  transfers between devices with their start and end apart: 5, of which 3 were waited for; matrix products, arithmetic and copies ran while one was open for 17% of the time, Pallas kernels for 15%

profile of v2, /device:TPU:0, one launch (start us, length us, event | category | flops | bytes accessed | tf_op | source)
XLA Modules:
  0.0 746.9 jit_solution(11519896316566854936)
XLA Ops:
  25.5 5.9 convolution_convert_fusion.1.refs_0_.refs_1_.refs_2_
  31.4 35.9 %attention_forward.2 = (bf16[1024,768]{1,0:T(8,128)(2,1)}, bf16[12,1024,1024]{2,1,0:T(8,128)(2,1)}, f32[1024,768]{1,0:T(8,128)}, bf16[16,64,768]{2,1,0:T(8,128)(2,1)}) custom-call(bf16[1024,2304]{1,0:T(8,128)(2,1)} %convolution_convert_fusion.1.refs_0_.refs_1_.refs_2_, bf16[1024,2304]{1,0:T(8,128)(2,1)} %convolution_convert_fusion.1.refs_0_.refs_1_.refs_2_, ...), custom_call_target="tpu_custom_call" | custom-call | flops 20000000000 | bytes 31457280 | tf_op jit(solution)/shard_map/attention_forward/pallas_call | solution.py:98
  77.6 7.9 %convolution_convert_fusion.refs_0_.refs_1_.refs_2_ = bf16[1024,2304]{1,0:T(8,128)(2,1)} fusion(bf16[768,2304]{1,0:T(8,128)(2,1)} %copy-done.34, bf16[1,1024,768]{1,2,0:T(8,128)(2,1)S(1)} %copy.73, f32[1024]{0:T(1024)S(1)} %fusion.113, f32[1024]{0:T(1024)S(1)} %get-tuple-element.179, f32[768]{0:T(1024)S(1)} %copy-done.49), kind=kOutput, calls=%fused_computation.1 | convolution fusion | flops 3630170112 | bytes 9841664 | tf_op jit(solution)/shard_map/dot_general | solution.py:24
  89.3 73.1 %attention_forward.3 = (bf16[1024,768]{1,0:T(8,128)(2,1)}, bf16[12,1024,1024]{2,1,0:T(8,128)(2,1)}, f32[1024,768]{1,0:T(8,128)}, bf16[16,64,768]{2,1,0:T(8,128)(...) custom-call(bf16[1024,2304]{1,0:T(8,128)(2,1)} %convolution_convert_fusion.refs_0_.refs_1_.refs_2_, ...), custom_call_target="tpu_custom_call" | custom-call | flops 20000000000 | bytes 31457280 | tf_op jit(solution)/shard_map/attention_forward/pallas_call | solution.py:98
  178.5 4.6 fusion.61
  183.2 61.7 %expert_stage.2 = (bf16[1024,768]{1,0:T(8,128)(2,1)}, bf16[1024,768]{1,0:T(8,128)(2,1)}, f32[16,8,128]{2,1,0:T(8,128)}, f32[2,768,1536]{2,1,0:T(8,128)}, f32[2,1...) custom-call(bf16[1024,768]{1,0:T(8,128)(2,1)} %bitcast.163, bf16[1024,768]{1,0:T(8,128)(2,1)} %bitcast.159, ...), custom_call_target="tpu_custom_call" | custom-call | flops 28991029248 | bytes 35651584 | tf_op jit(solution)/shard_map/expert_stage/pallas_call | solution.py:98
  244.9 48.0 %expert_stage.3 = (bf16[1024,768]{1,0:T(8,128)(2,1)}, bf16[1024,768]{1,0:T(8,128)(2,1)}, f32[16,8,128]{2,1,0:T(8,128)}, f32[2,768,1536]{2,1,0:T(8,128)}, f32[2,1...) custom-call(bf16[1024,768]{1,0:T(8,128)(2,1)} %bitcast.168, bf16[1024,768]{1,0:T(8,128)(2,1)} %bitcast.161, ...), custom_call_target="tpu_custom_call" | custom-call | flops 28991029248 | bytes 35651584 | tf_op jit(solution)/shard_map/expert_stage/pallas_call | solution.py:98
  309.9 64.6 %attention_backward.2 = (bf16[1024,768]{1,0:T(8,128)(2,1)}, bf16[1024,768]{1,0:T(8,128)(2,1)}, bf16[1024,768]{1,0:T(8,128)(2,1)}, bf16[16,64,768]{2,1,0:T(8,128)...) custom-call(bf16[1024,2304]{1,0:T(8,128)(2,1)} %convolution_convert_fusion.1.refs_0_.refs_1_.refs_2_, ...), custom_call_target="tpu_custom_call" | custom-call | flops 24999999488 | bytes 37748736 | tf_op jit(solution)/shard_map/attention_backward/pallas_call | solution.py:98
  393.2 6.1 fusion.72
  399.3 47.3 %attention_backward.3 = (bf16[1024,768]{1,0:T(8,128)(2,1)}, bf16[1024,768]{1,0:T(8,128)(2,1)}, bf16[1024,768]{1,0:T(8,128)(2,1)}, bf16[16,64,768]{2,1,0:T(8,128)(2,1)}) custom-call(bf16[1024,2304]{1,0:T(8,128)(2,1)} %convolution_convert_fusion.refs_0_.refs_1_.refs_2_, bf16[1024,2304]{1,0:T(8,128)(2,1)} %convolution_convert_fusion.refs_0_.refs_1_.refs_2_, ...), custom_call_target="tpu_custom_call" | custom-call | flops 24999999488 | bytes 37748736 | tf_op jit(solution)/shard_map/attention_backward/pallas_call | solution.py:98
  451.3 7.6 %add_convert_fusion = bf16[768,2304]{1,0:T(8,128)(2,1)} fusion(f32[768,2304]{1,0:T(8,128)} %fusion.72, bf16[1024,2304]{1,0:T(8,128)(2,1)S(1)} %constant_dynamic-update-slice_fusion.6, bf16[1,1024,768]{1,2,0:T(8,128)(2,1)S(1)} %copy-done.7, f32[1024]{0:T(1024)S(1)} %copy-done.47, f32[1024]{0:T(1024)S(1)} %copy-done.39, f32[768]{0:T(1024)S(1)} %copy-done.50), kind=kOutput, calls=%fused_computation | convolution fusion | flops 3631349760 | bytes 16919552 | tf_op jit(solution)/shard_map/dot_general | solution.py:24
  459.0 6.4 convert_element_type.150
  465.6 6.3 convert_element_type.152
  472.6 8.7 %fusion.39 = (f32[1024]{0:T(1024)S(1)}, f32[1024,768]{0,1:T(8,128)S(1)}) fusion(bf16[1,1024,768]{1,2,0:T(8,128)(2,1)} %copy-done.10, f32[768]{0:T(1024)S(1)} %copy-done.50, f32[1024]{0:T(1024)S(1)} %copy-done.45, bf16[1024,2304]{1,0:T(8,128)(2,1)} %copy-done.32, bf16[768,2304]{1,0:T(8,128)(2,1)} %copy-done.34), kind=kOutput, calls=%fused_computation.52 | convolution fusion | flops 3627809792 | bytes 12987392 | tf_op jit(solution)/shard_map/dot_general | solution.py:24
  481.4 5.1 fusion.37
  491.8 48.7 %all-reduce.2 = (f32[768]{0:T(1024)}, f32[768]{0:T(1024)}, f32[768,16]{0,1:T(8,128)}, f32[16,16]{0,1:T(8,128)S(1)}) all-reduce(f32[768]{0:T(1024)S(1)} %add.174, f32[768]{0:T(1024)S(1)} %add.177, f32[768,16]{0,1:T(8,128)S(1)} %convolution_add_fusion.2, f32[16,16]{0,1:T(8,128)S(1)} %fusion.100), channel_id=1, replica_groups=mesh['wide'=16,'narrow'=2] {'wide','narrow'}, use_global_device_ids=true, to_apply=%region_35.36 | all-reduce | flops 14080 | bytes 112640 | tf_op jit(solution)/shard_map/psum | solution.py:443
  541.2 7.7 %fusion.66 = (bf16[1,1024,768]{1,2,0:T(8,128)(2,1)S(1)}, bf16[1,1024,768]{1,2,0:T(8,128)(2,1)S(1)}) fusion(f32[1024,768]{0,1:T(8,128)} %copy-done.8, bf16[1,1024,768]{1,2,0:T(8,128)(2,1)} %copy-done.17, f32[1024]{0:T(1024)S(1)} %negate_multiply_fusion.1, f32[1024]{0:T(1024)S(1)} %negate_multiply_fusion.3, f32[1024]{0:T(1024)S(1)} %multiply_multiply_fusion.1, ...), kind=kLoop, calls=%fused_computation.92 | loop fusion | flops 20447232 | bytes 22064128 | tf_op jit(solution)/shard_map/stack | solution.py:449
  550.8 4.8 copy.67
  563.8 4.7 copy.66
  568.4 44.2 %all-reduce.6.cloned.1.call-done = (bf16[768,2304]{1,0:T(8,128)(2,1)}, bf16[768,768]{1,0:T(8,128)(2,1)}) async-done(((bf16[768,2304]{1,0:T(8,128)(2,1)}, bf16[768,768]{1,0:T(8,128)(2,1)}), (bf16[768,2304]{1,0:T(8,128)(2,1)}, bf16[768,768]{1,0:T(8,128)(2,1)})) %all-reduce.6.cloned.1.call-update) | async-done | bytes 4718608 | tf_op jit(solution)/shard_map/psum | solution.py:442
  618.8 55.0 %reduce-scatter.3.cloned.1.call-done = bf16[1,768,1536]{2,1,0:T(8,128)(2,1)} async-done(((bf16[2,768,1536]{2,1,0:T(8,128)(2,1)}), bf16[1,768,1536]{2,1,0:T(8,128)(2,1)}) %reduce-scatter.3.cloned.1.call-update) | async-done | bytes 2359312 | tf_op jit(solution)/shard_map/reduce_scatter | solution.py:400
  673.8 4.5 convert_element_type.151
  678.3 57.7 %reduce-scatter.5.cloned.1.call-done = bf16[1,1536,768]{2,1,0:T(8,128)(2,1)} async-done(((bf16[2,1536,768]{2,1,0:T(8,128)(2,1)}), bf16[1,1536,768]{2,1,0:T(8,128)(2,1)}) %reduce-scatter.5.cloned.1.call-update) | async-done | bytes 2359312 | tf_op jit(solution)/shard_map/reduce_scatter | solution.py:401
  736.0 4.2 convert_element_type.153
  (262 shorter events, 111.2 us)
Async XLA Ops:
  7.2 60.2 %copy-start = (bf16[768,768]{1,0:T(8,128)(2,1)S(1)}, bf16[768,768]{1,0:T(8,128)(2,1)}, u32[]{:S(2)}) copy-start(bf16[768,768]{1,0:T(8,128)(2,1)} %param.24) | copy-start | bytes 3538948
  7.2 175.9 %all-gather.3.cloned.1.call-start = ((), (), s32[]{:S(2)}) async-start(), calls=%async_computation.2 | async-start | bytes 7077888 | tf_op jit(solution)/shard_map/all_gather | solution.py:349
  7.9 175.2 %all-gather.5.cloned.1.call-start = ((), (), s32[]{:S(2)}) async-start(), calls=%async_computation.3 | async-start | bytes 7077888 | tf_op jit(solution)/shard_map/all_gather | solution.py:350
  8.7 604.0 %all-reduce.6.cloned.1.call-start = ((), (), s32[]{:S(2)}) async-start(), calls=%async_computation.6 | async-start | bytes 9437184 | tf_op jit(solution)/shard_map/psum | solution.py:442
  8.9 67.0 %copy-start.60 = (f32[16]{0:T(128)}, f32[16]{0:T(128)S(1)}, u32[]{:S(2)}) copy-start(f32[16]{0:T(128)S(1)} %multiply_reduce_fusion.12) | copy-start | bytes 196
  14.7 10.8 %copy-start.44 = (f32[1024]{0:T(1024)}, f32[1024]{0:T(1024)S(1)}, u32[]{:S(2)}) copy-start(f32[1024]{0:T(1024)S(1)} %broadcast_multiply_fusion.3) | copy-start | bytes 12292
  17.3 145.0 %copy-start.6 = (bf16[1,1024,768]{1,2,0:T(8,128)(2,1)}, bf16[1,1024,768]{1,2,0:T(8,128)(2,1)S(1)}, u32[]{:S(2)}) copy-start(bf16[1,1024,768]{1,2,0:T(8,128)(2,1)S(1)} %copy.73) | copy-start | bytes 4718596
  20.1 5.4 copy-start.51
  20.1 57.4 %copy-start.38 = (f32[1024]{0:T(1024)}, f32[1024]{0:T(1024)S(1)}, u32[]{:S(2)}) copy-start(f32[1024]{0:T(1024)S(1)} %get-tuple-element.179) | copy-start | bytes 12292
  20.4 5.1 copy-start.34
  77.5 8.0 %copy-start.40 = (f32[1024]{0:T(1024)}, f32[1024]{0:T(1024)S(1)}, u32[]{:S(2)}) copy-start(f32[1024]{0:T(1024)S(1)} %fusion.40) | copy-start | bytes 12292
  77.6 7.9 %copy-start.46 = (f32[1024]{0:T(1024)}, f32[1024]{0:T(1024)S(1)}, u32[]{:S(2)}) copy-start(f32[1024]{0:T(1024)S(1)} %fusion.113) | copy-start | bytes 12292
  77.6 7.9 %copy-start.23 = (bf16[2,1024,768]{2,1,0:T(8,128)(2,1)S(1)}, bf16[2,1024,768]{2,1,0:T(8,128)(2,1)}, u32[]{:S(2)}) copy-start(bf16[2,1024,768]{2,1,0:T(8,128)(2,1)} %param.16) | copy-start | bytes 9437188
  175.3 126.6 %copy-start.17 = (bf16[1,1024,768]{1,2,0:T(8,128)(2,1)}, bf16[1,1024,768]{1,2,0:T(8,128)(2,1)S(1)}, u32[]{:S(2)}) copy-start(bf16[1,1024,768]{1,2,0:T(8,128)(2,1)S(1)} %copy.72) | copy-start | bytes 4718596
  393.2 6.1 copy-start.32
  458.9 214.9 %reduce-scatter.3.cloned.1.call-start = ((), (), s32[]{:S(2)}) async-start(), calls=%async_computation.4 | async-start | bytes 7077888 | tf_op jit(solution)/shard_map/reduce_scatter | solution.py:400
  465.4 270.6 %reduce-scatter.5.cloned.1.call-start = ((), (), s32[]{:S(2)}) async-start(), calls=%async_computation.5 | async-start | bytes 7077888 | tf_op jit(solution)/shard_map/reduce_scatter | solution.py:401
  471.9 9.4 %slice-start = ((s8[4718592]{0:T(1024)(128)(4,1)}), s8[4194304]{0:T(1024)(128)(4,1)S(1)}, s32[]{:S(2)}) async-start(s8[4718592]{0:T(1024)(128)(4,1)} %bitcast.142), calls=%async_computation.7 | async-start | bytes 8388608
  472.6 8.8 %copy-start.43 = (f32[1024]{0:T(1024)S(1)}, f32[1024]{0:T(1024)}, u32[]{:S(2)}) copy-start(f32[1024]{0:T(1024)} %copy-done.42) | copy-start | bytes 12292
  472.6 8.8 %copy-start.13 = (bf16[1,1024,768]{1,2,0:T(8,128)(2,1)S(1)}, bf16[1,1024,768]{1,2,0:T(8,128)(2,1)}, u32[]{:S(2)}) copy-start(bf16[1,1024,768]{1,2,0:T(8,128)(2,1)} %copy-done.10) | copy-start | bytes 4718596
  472.6 8.8 %slice-start.1 = ((s8[4718592]{0:T(1024)(128)(4,1)}), s8[524288]{0:T(1024)(128)(4,1)S(1)}, s32[]{:S(2)}) async-start(s8[4718592]{0:T(1024)(128)(4,1)} %bitcast.142), calls=%async_computation.8 | async-start | bytes 1048576
  472.6 8.8 %copy-start.35 = (bf16[768,2304]{1,0:T(8,128)(2,1)S(1)}, bf16[768,2304]{1,0:T(8,128)(2,1)}, u32[]{:S(2)}) copy-start(bf16[768,2304]{1,0:T(8,128)(2,1)} %copy-done.34) | copy-start | bytes 10616836
  481.3 5.2 copy-start.24
  481.4 5.1 copy-start.41
  (50 other events, 137.2 us)
Sparse Core Ops, SparseCore 0:
  9.6 65.3 all-gather.2
  76.5 62.6 all-gather.4
  459.0 153.5 all-reduce.5
  614.9 58.8 reduce-scatter.2
  675.9 59.9 reduce-scatter.4

commit v3 on v2

--- a/solution.py
+++ b/solution.py
@@ -44,18 +44,29 @@
 MESH = pl.DeviceIdType.MESH
 
 
-def call_with_moves(body, moves, cid, *, grid, in_specs, out_specs, out_shape, scratch_shapes=(), cost, name, args):
-    members = lax.axis_size("wide")
+def call_with_moves(
+    body, moves, pushes, cid, *, grid, in_specs, out_specs, out_shape, scratch_shapes=(), cost, name, args
+):
+    members, spread = lax.axis_size("wide"), lax.axis_size("narrow")
     n_in, n_out, n_moves, n_scratch = len(in_specs), len(out_specs), len(moves), len(scratch_shapes)
+    arrays = []
+    for array, _, _ in pushes:
+        if not any(array is known for known in arrays):
+            arrays.append(array)
+    which = [next(k for k, known in enumerate(arrays) if known is array) for array, _, _ in pushes]
+    n_arrays, n_pushes = len(arrays), len(pushes)
 
     def kernel(*refs):
         ins, refs = refs[:n_in], refs[n_in:]
         sources, refs = refs[:n_moves], refs[n_moves:]
+        pushed, refs = refs[:n_arrays], refs[n_arrays:]
         outs, refs = refs[:n_out], refs[n_out:]
         targets, refs = refs[:n_moves], refs[n_moves:]
+        landings, refs = refs[:n_pushes], refs[n_pushes:]
         scratch, refs = refs[:n_scratch], refs[n_scratch:]
-        stages, (send_sem, recv_sem, own_sem) = refs[:n_moves], refs[n_moves:]
-        me = lax.axis_index("wide")
+        stages, refs = refs[:n_moves], refs[n_moves:]
+        send_sem, recv_sem, own_sem, push_send, push_recv = refs
+        me, side = lax.axis_index("wide"), lax.axis_index("narrow")
         step = pl.program_id(0)
 
         def remote(i, d):
@@ -69,14 +80,36 @@
                 device_id_type=MESH,
             )
 
+        def push(k, j):
+            return pltpu.make_async_remote_copy(
+                src_ref=pushes[k][1](pushed[which[k]], j),
+                dst_ref=landings[k].at[j],
+                send_sem=push_send.at[k, j],
+                recv_sem=push_recv.at[k, j],
+                device_id={"narrow": lax.rem(side + j + 1, spread)},
+                device_id_type=MESH,
+            )
+
         @pl.when(step == 0)
         def _():
             barrier = pltpu.get_barrier_semaphore()
-            for d in range(1, members):
-                pl.semaphore_signal(
-                    barrier, inc=1, device_id={"wide": lax.rem(me + d, members)}, device_id_type=MESH
-                )
-            pl.semaphore_wait(barrier, members - 1)
+            count = 0
+            if n_moves:
+                for d in range(1, members):
+                    pl.semaphore_signal(
+                        barrier, inc=1, device_id={"wide": lax.rem(me + d, members)}, device_id_type=MESH
+                    )
+                count += members - 1
+            if n_pushes:
+                for j in range(spread - 1):
+                    pl.semaphore_signal(
+                        barrier, inc=1, device_id={"narrow": lax.rem(side + j + 1, spread)}, device_id_type=MESH
+                    )
+                count += spread - 1
+            pl.semaphore_wait(barrier, count)
+            for k in range(n_pushes):
+                for j in range(spread - 1):
+                    push(k, j).start()
             for i in range(n_moves):
                 for d in range(1, members):
                     remote(i, d).start()
@@ -93,28 +126,254 @@
                 pltpu.make_async_copy(stages[i], targets[i].at[me], own_sem.at[i]).wait()
                 for d in range(1, members):
                     remote(i, d).wait()
+            for k in range(n_pushes):
+                for j in range(spread - 1):
+                    push(k, j).wait()
 
     anywhere = pl.BlockSpec(memory_space=pl.ANY)
     results = pl.pallas_call(
         kernel,
         grid=grid,
-        in_specs=list(in_specs) + [anywhere] * n_moves,
-        out_specs=list(out_specs) + [anywhere] * n_moves,
-        out_shape=list(out_shape) + [jax.ShapeDtypeStruct(a.shape, a.dtype) for a in moves],
+        in_specs=list(in_specs) + [anywhere] * (n_moves + n_arrays),
+        out_specs=list(out_specs) + [anywhere] * (n_moves + n_pushes),
+        out_shape=list(out_shape)
+        + [jax.ShapeDtypeStruct(a.shape, a.dtype) for a in moves]
+        + [jax.ShapeDtypeStruct((spread - 1, *shape), a.dtype) for a, _, shape in pushes],
         scratch_shapes=list(scratch_shapes)
         + [pltpu.VMEM(a.shape[1:], a.dtype) for a in moves]
         + [
-            pltpu.SemaphoreType.DMA((n_moves, members)),
-            pltpu.SemaphoreType.DMA((n_moves, members)),
-            pltpu.SemaphoreType.DMA((n_moves,)),
+            pltpu.SemaphoreType.DMA((max(1, n_moves), members)),
+            pltpu.SemaphoreType.DMA((max(1, n_moves), members)),
+            pltpu.SemaphoreType.DMA((max(1, n_moves),)),
+            pltpu.SemaphoreType.DMA((max(1, n_pushes), spread)),
+            pltpu.SemaphoreType.DMA((max(1, n_pushes), spread)),
         ],
         compiler_params=pltpu.CompilerParams(
             vmem_limit_bytes=VMEM_BYTES, collective_id=cid, has_side_effects=True
         ),
         cost_estimate=cost,
         name=name,
-    )(*args, *moves)
-    return results[:n_out], results[n_out:]
+    )(*args, *moves, *arrays)
+    return results[:n_out], results[n_out : n_out + n_moves], results[n_out + n_moves :]
+
+
+def reduce_orders(wide_count, narrow_count):
+    bits = lambda axis, count: [(axis, 1 << k) for k in range(count.bit_length() - 1)]
+    wide, narrow = bits("wide", wide_count), bits("narrow", narrow_count)
+    core, x_bits, z_bits = wide[:1], wide[1:2], wide[2:]
+    return (
+        core + x_bits + narrow + z_bits,
+        core + narrow + x_bits + z_bits,
+        core + z_bits + x_bits + narrow,
+    )
+
+
+def halvings(order, rows, columns):
+    plan = []
+    for _ in order:
+        if columns % 256 == 0:
+            columns //= 2
+            plan.append("columns")
+        elif rows % 32 == 0:
+            rows //= 2
+            plan.append("rows")
+        else:
+            plan.append("whole")
+    return plan
+
+
+def reduce_kernel(*refs, orders, width, places):
+    n_in = len(places)
+    ins, refs = refs[:n_in], refs[n_in:]
+    small_ref, out_ref, small_out, total, result, small_send, small_recv = refs[:7]
+    refs = refs[7:]
+    parts, stages = len(orders), len(orders[0])
+    outgoing = [refs[p * stages : (p + 1) * stages] for p in range(parts)]
+    incoming = [refs[(parts + p) * stages : (parts + p + 1) * stages] for p in range(parts)]
+    send_sem, recv_sem, back_send, back_recv, small_sems, small_rsems = refs[2 * parts * stages :]
+    index = {axis: lax.axis_index(axis) for axis in ("wide", "narrow")}
+    rows = total.shape[0]
+
+    def own_bit(axis, bit):
+        return lax.rem(index[axis] // bit, 2)
+
+    def partner(axis, bit):
+        return {axis: index[axis] + bit - 2 * bit * own_bit(axis, bit)}
+
+    barrier = pltpu.get_barrier_semaphore()
+    for axis, bit in orders[0]:
+        pl.semaphore_signal(barrier, inc=1, device_id=partner(axis, bit), device_id_type=MESH)
+    pl.semaphore_wait(barrier, stages)
+
+    for ref, place in zip(ins, places):
+        total[:, place : place + ref.shape[1]] = ref[...]
+    small_send[0] = small_ref[...]
+
+    regions = [[(0, rows, p * width, width)] for p in range(parts)]
+
+    def take(region):
+        row, height, column, span = region
+        if not isinstance(row, int):
+            row = pl.multiple_of(row, 16)
+        if not isinstance(column, int):
+            column = pl.multiple_of(column, 128)
+        return pl.ds(row, height), pl.ds(column, span)
+
+    def half(region, how, pick):
+        row, height, column, span = region
+        if how == "columns":
+            return row, height, column + pick * (span // 2), span // 2
+        if how == "rows":
+            return row + pick * (height // 2), height // 2, column, span
+        return region
+
+    plans = [halvings(order, rows, width) for order in orders]
+
+    def there(p, s):
+        axis, bit = orders[p][s]
+        return pltpu.make_async_remote_copy(
+            src_ref=outgoing[p][s],
+            dst_ref=incoming[p][s],
+            send_sem=send_sem.at[p, s],
+            recv_sem=recv_sem.at[p, s],
+            device_id=partner(axis, bit),
+            device_id_type=MESH,
+        )
+
+    def small_there(s):
+        axis, bit = orders[0][s]
+        return pltpu.make_async_remote_copy(
+            src_ref=small_send.at[s],
+            dst_ref=small_recv.at[s],
+            send_sem=small_sems.at[s],
+            recv_sem=small_rsems.at[s],
+            device_id=partner(axis, bit),
+            device_id_type=MESH,
+        )
+
+    def launch(p, s):
+        axis, bit = orders[p][s]
+        mine = own_bit(axis, bit)
+        region, how = regions[p][-1], plans[p][s]
+        outgoing[p][s][...] = total[take(half(region, how, 1 - mine))].astype(LOW)
+        there(p, s).start()
+        regions[p].append(half(region, how, mine))
+
+    for p in range(parts):
+        launch(p, 0)
+    small_there(0).start()
+    for s in range(stages):
+        for p in range(parts):
+            there(p, s).wait()
+            kept = take(regions[p][-1])
+            base = outgoing[p][s][...].astype(F32) if plans[p][s] == "whole" else total[kept]
+            value = base + incoming[p][s][...].astype(F32)
+            if s + 1 < stages:
+                total[kept] = value
+                launch(p, s + 1)
+            else:
+                result[kept] = value.astype(LOW)
+        small_there(s).wait()
+        fresh = small_send[s] + small_recv[s]
+        if s + 1 < stages:
+            small_send[s + 1] = fresh
+            small_there(s + 1).start()
+        else:
+            small_out[...] = fresh
+
+    def back(p, s):
+        axis, bit = orders[p][s]
+        spot = take(regions[p][s + 1])
+        return pltpu.make_async_remote_copy(
+            src_ref=result.at[spot],
+            dst_ref=result.at[spot],
+            send_sem=back_send.at[p, s],
+            recv_sem=back_recv.at[p, s],
+            device_id=partner(axis, bit),
+            device_id_type=MESH,
+        )
+
+    for s in reversed(range(stages)):
+        for p in range(parts):
+            if plans[p][s] != "whole":
+                back(p, s).start()
+        for p in range(parts):
+            if plans[p][s] != "whole":
+                back(p, s).wait()
+    out_ref[...] = result[...]
+
+
+def reduce_everywhere(big, small, cid):
+    orders = reduce_orders(lax.axis_size("wide"), lax.axis_size("narrow"))
+    places, columns = [], 0
+    for array in big:
+        places.append(columns)
+        columns += array.shape[1]
+    rows = big[0].shape[0]
+    width, parts, stages = columns // len(orders), len(orders), len(orders[0])
+    buffers = []
+    for order in orders:
+        height, span = rows, width
+        for how in halvings(order, rows, width):
+            height, span = (height // 2 if how == "rows" else height), (span // 2 if how == "columns" else span)
+            buffers.append(pltpu.VMEM((height, span), LOW))
+    vmem = pl.BlockSpec(memory_space=pltpu.VMEM)
+    return pl.pallas_call(
+        functools.partial(reduce_kernel, orders=orders, width=width, places=places),
+        in_specs=[vmem] * (len(big) + 1),
+        out_specs=[vmem, vmem],
+        out_shape=[jax.ShapeDtypeStruct((rows, columns), LOW), jax.ShapeDtypeStruct(small.shape, F32)],
+        scratch_shapes=[
+            pltpu.VMEM((rows, columns), F32),
+            pltpu.VMEM((rows, columns), LOW),
+            pltpu.VMEM((stages, *small.shape), F32),
+            pltpu.VMEM((stages, *small.shape), F32),
+        ]
+        + buffers
+        + buffers
+        + [pltpu.SemaphoreType.DMA((parts, stages))] * 4
+        + [pltpu.SemaphoreType.DMA((stages,))] * 2,
+        compiler_params=pltpu.CompilerParams(
+            vmem_limit_bytes=VMEM_BYTES, collective_id=cid, has_side_effects=True
+        ),
+        cost_estimate=pl.CostEstimate(flops=10**9, bytes_accessed=20 * 2**20, transcendentals=0),
+        name="reduce_everywhere",
+    )(*big, small)
+
+
+def join_kernel(own_ref, far_ref, out_ref):
+    value = own_ref[...]
+    for j in range(far_ref.shape[0]):
+        value += far_ref[j].astype(F32)
+    out_ref[0] = value
+
+
+def join(own, fars, along):
+    tiles = len(fars)
+    spread = fars[0].shape[0]
+    shape = list(own.shape)
+    shape[along] //= tiles
+
+    def kernel(own_ref, *rest):
+        far_refs, out_ref = rest[:tiles], rest[tiles]
+        for t in range(tiles):
+
+            @pl.when(pl.program_id(0) == t)
+            def _():
+                join_kernel(own_ref, far_refs[t], out_ref)
+
+    place = (lambda t: (0, t)) if along == 1 else (lambda t: (t, 0))
+    return pl.pallas_call(
+        kernel,
+        grid=(tiles,),
+        in_specs=[pl.BlockSpec(tuple(shape), place)]
+        + [pl.BlockSpec((spread, *shape), lambda t: (0, 0, 0), pipeline_mode=pl.Buffered(1))] * tiles,
+        out_specs=pl.BlockSpec((1, *shape), lambda t: (0, *place(t))),
+        out_shape=jax.ShapeDtypeStruct((1, *own.shape), F32),
+        compiler_params=pltpu.CompilerParams(vmem_limit_bytes=VMEM_BYTES),
+        cost_estimate=pl.CostEstimate(flops=10**7, bytes_accessed=12 * 2**20, transcendentals=0),
+        name="join",
+    )(own, *fars)
 
 
 def attention_forward_kernel(q_ref, k_ref, v_ref, mixed_ref, soft_ref, inv_ref, *, rows):
@@ -140,12 +399,13 @@
         inv_ref[part, :] = jnp.where(lane < HEAD_DIM, inverses[0], inverses[1])
 
 
-def attention_forward(qkv_rows, moves, cid):
+def attention_forward(qkv_rows, moves, pushes, cid):
     pairs = D // PAIR
     columns = lambda first: pl.BlockSpec((LENGTH, PAIR), lambda i: (0, first + i))
     return call_with_moves(
         functools.partial(attention_forward_kernel, rows=512),
         moves,
+        pushes,
         cid,
         grid=(pairs,),
         in_specs=[columns(0), columns(pairs), columns(2 * pairs)],
@@ -197,12 +457,13 @@
     dv_ref[...] = jnp.concatenate(dv_parts, axis=0).T.astype(LOW)
 
 
-def attention_backward(qkv_rows, grad_mixed, mixed_rows, soft, inverses, moves, cid):
+def attention_backward(qkv_rows, grad_mixed, mixed_rows, soft, inverses, moves, pushes, cid):
     pairs = D // PAIR
     columns = lambda first: pl.BlockSpec((LENGTH, PAIR), lambda i: (0, first + i))
     return call_with_moves(
         functools.partial(attention_backward_kernel, rows=512),
         moves,
+        pushes,
         cid,
         grid=(pairs,),
         in_specs=[
@@ -238,16 +499,39 @@
     return lax.broadcasted_iota(jnp.int32, shape, 0) == lax.broadcasted_iota(jnp.int32, shape, 1)
 
 
-def expert_kernel(rows_ref, cot_ref, gate_ref, in_ref, outer_ref, *rest, more, steps, slot_cap):
+def expert_kernel(*refs, more, last, per, steps, slot_cap):
+    rows_ref, cot_ref, gate_ref, own_in, own_outer = refs[:5]
+    far_in, far_outer = refs[5 : 5 + per], refs[5 + per : 5 + 2 * per]
+    refs = refs[5 + 2 * per :]
     if more:
-        old_in, old_outer = rest[:2]
-        rest = rest[2:]
-    result_ref, sent_ref, dots_ref, din_ref, douter_ref, grad_sc, rows_t, acc_result, acc_sent = rest
+        old_in, old_outer = refs[:2]
+        refs = refs[2:]
+    result_ref, sent_ref, dots_ref, din_ref, douter_ref = refs[:5]
+    refs = refs[5:]
+    if last:
+        far_din, far_douter = refs[:2]
+        refs = refs[2:]
+    grad_sc, rows_t, acc_result, acc_sent, first_buf, second_buf, sems = refs
     step = pl.program_id(0)
+    slot = lax.rem(step, 2)
     sources = rows_ref.shape[0] // slot_cap
+    tile = first_buf.shape[2]
+
+    def fetch(i):
+        if i < per:
+            first = own_in.at[:, i * tile : (i + 1) * tile]
+            second = own_outer.at[i * tile : (i + 1) * tile, :]
+        else:
+            first, second = far_in[i % per].at[i // per - 1], far_outer[i % per].at[i // per - 1]
+        return (
+            pltpu.make_async_copy(first, first_buf.at[i % 2], sems.at[0, i % 2]),
+            pltpu.make_async_copy(second, second_buf.at[i % 2], sems.at[1, i % 2]),
+        )
 
     @pl.when(step == 0)
     def _():
+        for copy in fetch(0):
+            copy.start()
         for w in range(sources):
             part = slice(w * slot_cap, (w + 1) * slot_cap)
             gate = jnp.sum(jnp.where(diagonal(slot_cap), gate_ref[w, 0:1, :], 0.0), axis=1, keepdims=True)
@@ -256,7 +540,17 @@
         acc_result[...] = jnp.zeros_like(acc_result)
         acc_sent[...] = jnp.zeros_like(acc_sent)
 
-    first, second = in_ref[0], outer_ref[0]
+    for i in range(steps):
+
+        @pl.when(step == i)
+        def _():
+            for copy in fetch(i):
+                copy.wait()
+            if i + 1 < steps:
+                for copy in fetch(i + 1):
+                    copy.start()
+
+    first, second = first_buf[slot], second_buf[slot]
     hidden, slope = gelu_and_slope(dot(rows_ref[...], first))
     hidden = hidden.astype(LOW)
     grad_rows = grad_sc[...]
@@ -266,10 +560,22 @@
     din = dot(rows_t[...], grad_pre)
     douter = dot(hidden, grad_rows, TN)
     if more:
-        din += old_in[0]
-        douter += old_outer[0]
-    din_ref[0] = din
-    douter_ref[0] = douter
+        din += old_in[...]
+        douter += old_outer[...]
+    if not last:
+        din_ref[...] = din
+        douter_ref[...] = douter
+    else:
+
+        @pl.when(step < per)
+        def _():
+            din_ref[...] = din
+            douter_ref[...] = douter
+
+        @pl.when(step >= per)
+        def _():
+            far_din[...] = din.astype(LOW)
+            far_douter[...] = douter.astype(LOW)
 
     @pl.when(step == steps - 1)
     def _():
@@ -284,41 +590,76 @@
             dots_ref[w] = jnp.broadcast_to(row, (8, 128))
 
 
-def expert_stage(rows, cot, gates, all_in, all_outer, old, slot_cap, moves, cid):
-    count, width, units = all_in.shape
+def tile_of(units):
+    return min(512, units)
+
+
+def expert_stage(rows, cot, gates, weights, old, last, slot_cap, moves, pushes, cid):
+    own_in, own_outer, far_in, far_outer = weights
+    width, units = own_in.shape
+    count = lax.axis_size("narrow")
     height = rows.shape[0]
-    tile = min(512, units)
+    tile = tile_of(units)
     per = units // tile
     steps = count * per
     whole = lambda shape: pl.BlockSpec(shape, lambda i: (0,) * len(shape))
-    in_spec = pl.BlockSpec((1, width, tile), lambda i: (i // per, 0, i % per))
-    outer_spec = pl.BlockSpec((1, tile, width), lambda i: (i // per, i % per, 0))
+    anywhere = pl.BlockSpec(memory_space=pl.ANY)
+    din_spec = pl.BlockSpec((None, width, tile), lambda i: (i, 0, 0))
+    douter_spec = pl.BlockSpec((None, tile, width), lambda i: (i, 0, 0))
+    out_specs = [whole((height, width)), whole((height, width)), whole(gates.shape)]
+    out_shape = [
+        jax.ShapeDtypeStruct((height, width), LOW),
+        jax.ShapeDtypeStruct((height, width), LOW),
+        jax.ShapeDtypeStruct(gates.shape, F32),
+    ]
+    if last:
+        near = lambda i: jnp.minimum(i, per - 1)
+        away = lambda i: jnp.maximum(i - per, 0)
+        out_specs += [
+            pl.BlockSpec((width, tile), lambda i: (0, near(i))),
+            pl.BlockSpec((tile, width), lambda i: (near(i), 0)),
+            pl.BlockSpec((None, width, tile), lambda i: (away(i), 0, 0)),
+            pl.BlockSpec((None, tile, width), lambda i: (away(i), 0, 0)),
+        ]
+        out_shape += [
+            jax.ShapeDtypeStruct((width, units), F32),
+            jax.ShapeDtypeStruct((units, width), F32),
+            jax.ShapeDtypeStruct((steps - per, width, tile), LOW),
+            jax.ShapeDtypeStruct((steps - per, tile, width), LOW),
+        ]
+    else:
+        out_specs += [din_spec, douter_spec]
+        out_shape += [
+            jax.ShapeDtypeStruct((steps, width, tile), F32),
+            jax.ShapeDtypeStruct((steps, tile, width), F32),
+        ]
     return call_with_moves(
-        functools.partial(expert_kernel, more=bool(old), steps=steps, slot_cap=slot_cap),
+        functools.partial(
+            expert_kernel, more=bool(old), last=last, per=per, steps=steps, slot_cap=slot_cap
+        ),
         moves,
+        pushes,
         cid,
         grid=(steps,),
-        in_specs=[whole((height, width)), whole((height, width)), whole(gates.shape), in_spec, outer_spec]
-        + ([in_spec, outer_spec] if old else []),
-        out_specs=[whole((height, width)), whole((height, width)), whole(gates.shape), in_spec, outer_spec],
-        out_shape=[
-            jax.ShapeDtypeStruct((height, width), LOW),
-            jax.ShapeDtypeStruct((height, width), LOW),
-            jax.ShapeDtypeStruct(gates.shape, F32),
-            jax.ShapeDtypeStruct(all_in.shape, F32),
-            jax.ShapeDtypeStruct(all_outer.shape, F32),
-        ],
+        in_specs=[whole((height, width)), whole((height, width)), whole(gates.shape)]
+        + [anywhere] * (2 + 2 * per)
+        + ([din_spec, douter_spec] if old else []),
+        out_specs=out_specs,
+        out_shape=out_shape,
         scratch_shapes=[
             pltpu.VMEM((height, width), LOW),
             pltpu.VMEM((width, height), LOW),
             pltpu.VMEM((height, width), F32),
             pltpu.VMEM((height, width), F32),
+            pltpu.VMEM((2, width, tile), LOW),
+            pltpu.VMEM((2, tile, width), LOW),
+            pltpu.SemaphoreType.DMA((2, 2)),
         ],
         cost=pl.CostEstimate(
             flops=12 * height * width * units * count, bytes_accessed=34 * 2**20, transcendentals=0
         ),
         name="expert_stage",
-        args=(rows, cot, gates, all_in, all_outer, *old),
+        args=(rows, cot, gates, own_in, own_outer, *far_in, *far_outer, *old),
     )
 
 
@@ -346,8 +687,16 @@
     slots = expert_count * slot_cap
     w_qkv = jnp.concatenate([w_query, w_key, w_value], axis=1)
     route_float = w_route.astype(F32)
-    all_in = lax.all_gather(w_in[0], "narrow", axis=0, tiled=False)
-    all_outer = lax.all_gather(w_outer[0], "narrow", axis=0, tiled=False)
+    own_in, own_outer = w_in[0], w_outer[0]
+    units = own_in.shape[1]
+    tile = tile_of(units)
+    per = units // tile
+    weight_pushes = [
+        (own_in, lambda ref, j, t=t: ref.at[:, t * tile : (t + 1) * tile], (feat_width, tile)) for t in range(per)
+    ] + [
+        (own_outer, lambda ref, j, t=t: ref.at[t * tile : (t + 1) * tile, :], (tile, feat_width)) for t in range(per)
+    ]
+    early = len(weight_pushes) // 3
     slot_columns = jnp.arange(slots, dtype=jnp.int32)
 
     def boxes(rows):
@@ -370,10 +719,12 @@
         normed_low = normed_one.astype(LOW)
         qkv_rows = dot(normed_low, w_qkv).astype(LOW)
         if m == 0:
-            (mixed_rows, soft, inverses), (cot_0,) = attention_forward(qkv_rows, (cot_boxes[0],), 1)
+            (mixed_rows, soft, inverses), (cot_0,), far_a = attention_forward(
+                qkv_rows, (cot_boxes[0],), weight_pushes[:early], 1
+            )
         else:
-            (mixed_rows, soft, inverses), (sent_0, gates_0, cot_1) = attention_forward(
-                qkv_rows, (*send[0], cot_boxes[1]), 2
+            (mixed_rows, soft, inverses), (sent_0, gates_0, cot_1), far_b = attention_forward(
+                qkv_rows, (*send[0], cot_boxes[1]), weight_pushes[early:], 2
             )
         first_sum = inputs + dot(mixed_rows, w_out)
         normed_two, pull_two = jax.vjp(layer_norm, first_sum, gain_two)
@@ -390,15 +741,20 @@
              second_low, gate_prob, pull_gate)
         )
 
-    (result_0, grad_0, dots_0, *expert_grads), (sent_1, gates_1) = expert_stage(
-        flat(sent_0), flat(cot_0), gates_0, all_in, all_outer, (), slot_cap, send[1], 3
-    )
-    (result_1, grad_1, dots_1, part_in, part_outer), (home_grad_0, home_dots_0) = expert_stage(
-        flat(sent_1), flat(cot_1), gates_1, all_in, all_outer, tuple(expert_grads), slot_cap,
-        (boxes(grad_0), dots_0), 4
-    )
-    grad_in = lax.psum_scatter(part_in.astype(LOW), "narrow", scatter_dimension=0, tiled=False)
-    grad_outer = lax.psum_scatter(part_outer.astype(LOW), "narrow", scatter_dimension=0, tiled=False)
+    far = [*far_a, *far_b]
+    weights = (own_in, own_outer, far[:per], far[per:])
+    (result_0, grad_0, dots_0, *old), (sent_1, gates_1), _ = expert_stage(
+        flat(sent_0), flat(cot_0), gates_0, weights, (), False, slot_cap, send[1], (), 3
+    )
+    (result_1, grad_1, dots_1, near_din, near_douter, far_din, far_douter), (home_grad_0, home_dots_0), _ = expert_stage(
+        flat(sent_1), flat(cot_1), gates_1, weights, tuple(old), True, slot_cap, (boxes(grad_0), dots_0), (), 4
+    )
+    grad_pushes = [
+        (far_din, lambda ref, j, t=t: ref.at[j * per + t], (feat_width, tile)) for t in range(per)
+    ] + [
+        (far_douter, lambda ref, j, t=t: ref.at[j * per + t], (tile, feat_width)) for t in range(per)
+    ]
+    later = len(grad_pushes) - early
 
     input_grads, sums = [], None
     for m in range(micro_count):
@@ -420,12 +776,13 @@
         grad_wo = dot(mixed_rows, grad_branch, TN)
         grad_mixed = dot(grad_branch, w_out, NT).astype(LOW)
         if m == 0:
-            grads, (home_grad_1, home_dots_1, home_result_0) = attention_backward(
-                qkv_rows, grad_mixed, mixed_rows, soft, inverses, (boxes(grad_1), dots_1, boxes(result_0)), 5
+            grads, (home_grad_1, home_dots_1, home_result_0), got_a = attention_backward(
+                qkv_rows, grad_mixed, mixed_rows, soft, inverses,
+                (boxes(grad_1), dots_1, boxes(result_0)), grad_pushes[:later], 5
             )
         else:
-            grads, (home_result_1,) = attention_backward(
-                qkv_rows, grad_mixed, mixed_rows, soft, inverses, (boxes(result_1),), 6
+            grads, (home_result_1,), got_b = attention_backward(
+                qkv_rows, grad_mixed, mixed_rows, soft, inverses, (boxes(result_1),), grad_pushes[later:], 6
             )
         grad_qkv = jnp.concatenate(grads, axis=1)
         grad_wqkv = dot(normed_low, grad_qkv, TN)
@@ -439,24 +796,30 @@
         returned = dot(tables[m], flat(home_result))
         outputs.append((first_sum + gate_prob[:, None] * returned).astype(LOW))
     gain_one_sum, wqkv_sum, wo_sum, gain_two_sum, route_sum, embed_sum = sums
-    wqkv_sum, wo_sum = lax.psum((wqkv_sum.astype(LOW), wo_sum.astype(LOW)), ("wide", "narrow"))
-    gain_one_sum, gain_two_sum, route_sum, embed_sum = lax.psum(
-        (gain_one_sum, gain_two_sum, route_sum, embed_sum), ("wide", "narrow")
-    )
-    wqkv_sum = wqkv_sum.astype(F32)
+    router_dim = route_sum.shape[1]
+    small = jnp.concatenate(
+        [
+            route_sum.T,
+            gain_one_sum[None],
+            gain_two_sum[None],
+            jnp.pad(embed_sum.reshape(1, -1), ((0, 0), (0, feat_width - embed_sum.size))),
+            jnp.zeros((-(router_dim + 3) % 8, feat_width), F32),
+        ],
+        axis=0,
+    )
+    big, small = reduce_everywhere((wqkv_sum, wo_sum), small, 7)
+    big = [big[:, k * feat_width : (k + 1) * feat_width].astype(F32) for k in range(4)]
+    got = [*got_a, *got_b]
     return (
         jnp.stack(outputs),
         jnp.stack(input_grads),
-        gain_one_sum,
-        wqkv_sum[:, :feat_width],
-        wqkv_sum[:, feat_width : 2 * feat_width],
-        wqkv_sum[:, 2 * feat_width :],
-        wo_sum.astype(F32),
-        gain_two_sum,
-        route_sum,
-        embed_sum,
-        grad_in.astype(F32)[None],
-        grad_outer.astype(F32)[None],
+        small[router_dim],
+        *big,
+        small[router_dim + 1],
+        small[:router_dim].T,
+        small[router_dim + 2, : embed.size].reshape(embed.shape),
+        join(near_din, got[:per], 1),
+        join(near_douter, got[per:], 0),
     )
 
 

time: 755 us -> 607 us (0.80)
  waiting for transfers between devices: 158 us -> 0 us
  Pallas kernels: 331 us -> 430 us
  blocking collectives: 48.7 us -> 0 us
  between operations: 15.1 us -> 2.45 us
  other arithmetic: 46.7 us -> 36.6 us
  matrix products: 95.3 us -> 86.4 us
  local copies, waits for them, and re-layouts: 51.7 us -> 43.5 us
    reduce_scatter x2 -> x0, waiting for transfers between devices: 113 us -> none  [the longest x1 57.7 us: local(): lax.psum_scatter(part_outer.astype(LOW), 'narrow', scatter_dimension=0, t...]
    pallas_call x0 -> x3, Pallas kernels: none -> 87.9 us  [the longest x1 75.4 us: reduce_everywhere(): pl.pallas_call(functools.partial(reduce_kernel, orders=orders, width=widt...]
    psum x1 -> x0, blocking collectives: 48.7 us -> none  [local(): lax.psum((gain_one_sum, gain_two_sum, route_sum, embed_sum), ('wide', 'na...]
    psum x1 -> x0, waiting for transfers between devices: 44.2 us -> none  [local(): lax.psum((wqkv_sum.astype(LOW), wo_sum.astype(LOW)), ('wide', 'narrow'))]
    convert_element_type x5 -> x1, other arithmetic: 24.4 us -> 6.23 us  [local(): big[:, k * feat_width:(k + 1) * feat_width].astype(F32)]
    pallas_call x6, Pallas kernels: 331 us -> 342 us  [call_with_moves(): pl.pallas_call(kernel, grid=grid, in_specs=list(in_specs) + [anywhere] *...]
    dot_general x26, matrix products: 93.9 us -> 84.9 us  [dot(): lax.dot_general(left, right, dims, precision=precise, preferred_element_t...]
    unnamed x152 -> x157, local copies, waits for them, and re-layouts: 37.5 us -> 30.9 us
  transfers between devices with their start and end apart: 5 -> 0, of which waited for: 3 -> 0; matrix products, arithmetic and copies ran while one was open for 17% -> 0% of each run, Pallas kernels for 15% -> 0%
where the time goes in v3:
time: 607 us; the launch traced here: 598 us
  Pallas kernels  430 us (71%)
  matrix products  86.4 us (14%)
  local copies, waits for them, and re-layouts  43.5 us (7%)
  other arithmetic  36.6 us (6%)
    pallas_call x6, Pallas kernels, call_with_moves(): pl.pallas_call(kernel, grid=grid, in_specs=list(in_specs) + [anywhere] *...  342 us
    dot_general x26, matrix products, dot(): lax.dot_general(left, right, dims, precision=precise, preferred_element_t...  84.9 us
    pallas_call x1, Pallas kernels, reduce_everywhere(): pl.pallas_call(functools.partial(reduce_kernel, orders=orders, width=widt...  75.4 us
    unnamed x157, local copies, waits for them, and re-layouts  30.9 us
    pallas_call x2, Pallas kernels, join(): pl.pallas_call(kernel, grid=(tiles,), in_specs=[pl.BlockSpec(tuple(shape)...  12.5 us

profile of v3, /device:TPU:0, one launch (start us, length us, event | category | flops | bytes accessed | tf_op | source)
XLA Modules:
  0.0 598.5 jit_solution(12631396171475556249)
XLA Ops:
  0.7 3.8 fusion.125
  12.3 5.9 convolution_convert_fusion.1.refs_0_.refs_1_.refs_2_
  21.4 46.4 %attention_forward.2 = (bf16[1024,768]{1,0:T(8,128)(2,1)}, bf16[12,1024,1024]{2,1,0:T(8,128)(2,1)}, f32[1024,768]{1,0:T(8,128)}, bf16[16,64,768]{2,1,0:T(8,128)(...) custom-call(bf16[1024,2304]{1,0:T(8,128)(2,1)} %convolution_convert_fusion.1.refs_0_.refs_1_.refs_2_, ...), custom_call_target="tpu_custom_call" | custom-call | flops 20000000000 | bytes 31457280 | tf_op jit(solution)/shard_map/attention_forward/pallas_call | solution.py:134
  76.1 4.7 fusion.55
  81.3 5.9 convolution_convert_fusion.refs_0_.refs_1_.refs_2_
  90.3 76.9 %attention_forward.3 = (bf16[1024,768]{1,0:T(8,128)(2,1)}, bf16[12,1024,1024]{2,1,0:T(8,128)(2,1)}, f32[1024,768]{1,0:T(8,128)}, bf16[16,64,768]{2,1,0:T(8,128)(...) custom-call(bf16[1024,2304]{1,0:T(8,128)(2,1)} %convolution_convert_, ...), custom_call_target="tpu_custom_call" | custom-call | flops 20000000000 | bytes 31457280 | tf_op jit(solution)/shard_map/attention_forward/pallas_call | solution.py:134
  177.2 47.1 %expert_stage.2 = (bf16[1024,768]{1,0:T(8,128)(2,1)}, bf16[1024,768]{1,0:T(8,128)(2,1)}, f32[16,8,128]{2,1,0:T(8,128)}, f32[6,768,512]{2,1,0:T(8,128)}, f32[6,51...) custom-call(bf16[1024,768]{1,0:T(8,128)(2,1)} %bitcast.176, bf16[1024,768]{1,0:T(8,128)(2,1)} %bitcast.172, ...), custom_call_target="tpu_custom_call" | custom-call | flops 28991029248 | bytes 35651584 | tf_op jit(solution)/shard_map/expert_stage/pallas_call | solution.py:134
  224.2 49.0 %expert_stage.3 = (bf16[1024,768]{1,0:T(8,128)(2,1)}, bf16[1024,768]{1,0:T(8,128)(2,1)}, f32[16,8,128]{2,1,0:T(8,128)}, f32[768,1536]{1,0:T(8,128)}, f32[1536,76...) custom-call(bf16[1024,768]{1,0:T(8,128)(2,1)} %bitcast.180, ...), custom_call_target="tpu_custom_call" | custom-call | flops 28991029248 | bytes 35651584 | tf_op jit(solution)/shard_map/expert_stage/pallas_call | solution.py:134
  275.3 3.6 fusion.11
  293.1 78.4 %attention_backward.2 = (bf16[1024,768]{1,0:T(8,128)(2,1)}, bf16[1024,768]{1,0:T(8,128)(2,1)}, bf16[1024,768]{1,0:T(8,128)(2,1)}, bf16[16,64,768]{2,1,0:T(8,128)...) custom-call(bf16[1024,2304]{1,0:T(8,128)(2,1)} %convolution_convert_, ...), custom_call_target="tpu_custom_call" | custom-call | flops 24999999488 | bytes 37748736 | tf_op jit(solution)/shard_map/attention_backward/pallas_call | solution.py:134
  373.7 3.6 fusion.4
  390.0 43.8 %attention_backward.3 = (bf16[1024,768]{1,0:T(8,128)(2,1)}, bf16[1024,768]{1,0:T(8,128)(2,1)}, bf16[1024,768]{1,0:T(8,128)(2,1)}, bf16[16,64,768]{2,1,0:T(8,128)...) custom-call(bf16[1024,2304]{1,0:T(8,128)(2,1)} %convolution_convert_fusion.refs_0_.refs_1_.refs_2_, ...), custom_call_target="tpu_custom_call" | custom-call | flops 24999999488 | bytes 37748736 | tf_op jit(solution)/shard_map/attention_backward/pallas_call | solution.py:134
  433.8 6.2 %join.3 = f32[1,1536,768]{2,1,0:T(8,128)} custom-call(f32[1536,768]{1,0:T(8,128)} %get-tuple-element.108.own_ref, bf16[1,512,768]{2,1,0:T(8,128)(2,1)} %get-tuple-element.109.rest_0_, bf16[1,512,768]{2,1,0:T(8,128)(2,1)} %get-tuple-element.110.rest_1_, bf16[1,512,768]{2,1,0:T(8,128)(2,1)} %get-tuple-element.111.rest_2_), custom_call_target="tpu_custom_call" | custom-call | flops 10000000 | bytes 12582912 | tf_op jit(solution)/shard_map/join/pallas_call | solution.py:366
  439.9 6.3 %join.2 = f32[1,768,1536]{2,1,0:T(8,128)} custom-call(f32[768,1536]{1,0:T(8,128)} %get-tuple-element.104.own_ref, bf16[1,768,512]{2,1,0:T(8,128)(2,1)} %get-tuple-element.105.rest_0_, bf16[1,768,512]{2,1,0:T(8,128)(2,1)} %get-tuple-element.106.rest_1_, bf16[1,768,512]{2,1,0:T(8,128)(2,1)} %get-tuple-element.107.rest_2_), custom_call_target="tpu_custom_call" | custom-call | flops 10000000 | bytes 12582912 | tf_op jit(solution)/shard_map/join/pallas_call | solution.py:366
  454.5 3.9 fusion.39
  458.5 5.1 fusion.37
  476.8 3.9 fusion.72
  480.8 6.2 %convolution_add_fusion.refs_0_ = f32[768,2304]{1,0:T(8,128)} fusion(f32[768,2304]{1,0:T(8,128)S(1)} %fusion.72, bf16[1024,2304]{1,0:T(8,128)(2,1)S(1)} %bitcast.147, bf16[1,1024,768]{1,2,0:T(8,128)(2,1)S(1)} %copy-done.7, f32[1024]{0:T(1024)S(1)} %copy-done.50, f32[1024]{0:T(1024)S(1)} %copy-done.41, f32[768]{0:T(1024)S(1)} %copy-done.53), kind=kOutput, calls=%fused_computation.2 | convolution fusion | flops 3629580288 | bytes 20458496 | tf_op jit(solution)/shard_map/dot_general | solution.py:24
  487.0 75.4 %reduce_everywhere.1 = (bf16[768,3072]{1,0:T(8,128)(2,1)}, f32[24,768]{1,0:T(8,128)}) custom-call(f32[768,2304]{1,0:T(8,128)} %convolution_add_fusion.refs_0_, f32[768,768]{1,0:T(8,128)} %convolution_add_fusion.3.refs_1_, f32[24,768]{1,0:T(8,128)} %concatenate.15.refs_2_), custom_call_target="tpu_custom_call" | custom-call | flops 1000000000 | bytes 20971520 | tf_op jit(solution)/shard_map/reduce_everywhere/pallas_call | solution.py:321
  562.5 6.2 %slice_convert_fusion = (f32[768,768]{1,0:T(8,128)}, f32[768,768]{1,0:T(8,128)}, f32[768,768]{1,0:T(8,128)}, f32[768,768]{1,0:T(8,128)}) fusion(bf16[768,3072]{1,0:T(8,128)(2,1)} %get-tuple-element.103), kind=kLoop, calls=%fused_computation.96 | loop fusion | flops 2359296 | bytes 14155776 | tf_op jit(solution)/shard_map/convert_element_type | solution.py:811
  570.6 7.5 %fusion.66 = (bf16[1,1024,768]{1,2,0:T(8,128)(2,1)S(1)}, bf16[1,1024,768]{1,2,0:T(8,128)(2,1)S(1)}) fusion(f32[1024,768]{0,1:T(8,128)} %get-tuple-element.156, bf16[1,1024,768]{1,2,0:T(8,128)(2,1)} %copy-done.16, f32[1024]{0:T(1024)S(1)} %negate_multiply_fusion.1, f32[1024]{0:T(1024)S(1)} %negate_multiply_fusion.3, f32[1024]{0:T(1024)S(1)} %multiply_multiply_fusion.1, ...), kind=kLoop, calls=%fused_computation.91 | loop fusion | flops 20447232 | bytes 22064128 | tf_op jit(solution)/shard_map/stack | solution.py:815
  580.1 5.0 copy.54
  585.1 4.1 fusion.64
  593.3 4.6 copy.53
  (261 shorter events, 92.3 us)
Async XLA Ops:
  0.6 67.2 %copy-start = (bf16[768,768]{1,0:T(8,128)(2,1)S(1)}, bf16[768,768]{1,0:T(8,128)(2,1)}, u32[]{:S(2)}) copy-start(bf16[768,768]{1,0:T(8,128)(2,1)} %param.24) | copy-start | bytes 3538948
  6.5 5.4 copy-start.47
  9.2 158.0 %copy-start.6 = (bf16[1,1024,768]{1,2,0:T(8,128)(2,1)}, bf16[1,1024,768]{1,2,0:T(8,128)(2,1)S(1)}, u32[]{:S(2)}) copy-start(bf16[1,1024,768]{1,2,0:T(8,128)(2,1)S(1)} %copy.59) | copy-start | bytes 4718596
  9.5 71.8 %copy-start.40 = (f32[1024]{0:T(1024)}, f32[1024]{0:T(1024)S(1)}, u32[]{:S(2)}) copy-start(f32[1024]{0:T(1024)S(1)} %get-tuple-element.196) | copy-start | bytes 12292
  12.3 5.9 copy-start.35
  12.3 5.9 copy-start.57
  12.3 5.9 copy-start.58
  12.3 5.9 copy-start.56
  12.3 6.0 %copy-start.19 = (bf16[2,1024,768]{2,1,0:T(8,128)(2,1)S(1)}, bf16[2,1024,768]{2,1,0:T(8,128)(2,1)}, u32[]{:S(2)}) copy-start(bf16[2,1024,768]{2,1,0:T(8,128)(2,1)} %param.16) | copy-start | bytes 9437188
  74.3 6.5 %copy-start.63 = (f32[16]{0:T(128)}, f32[16]{0:T(128)S(1)}, u32[]{:S(2)}) copy-start(f32[16]{0:T(128)S(1)} %multiply_reduce_fusion.12) | copy-start | bytes 196
  74.7 6.1 %copy-start.59 = (f32[1024]{0:T(1024)}, f32[1024]{0:T(1024)S(1)}, u32[]{:S(2)}) copy-start(f32[1024]{0:T(1024)S(1)} %select_reduce_fusion.1) | copy-start | bytes 12292
  76.1 5.2 copy-start.36
  81.3 5.9 copy-start.43
  81.3 5.9 copy-start.49
  81.3 5.9 copy-start.20
  175.8 48.5 %copy-start.61 = (f32[1024]{0:T(1024)}, f32[1024]{0:T(1024)S(1)}, u32[]{:S(2)}) copy-start(f32[1024]{0:T(1024)S(1)} %select_reduce_fusion) | copy-start | bytes 12292
  439.9 6.8 %copy-start.64 = (f32[16]{0:T(128)S(1)}, f32[16]{0:T(128)}, u32[]{:S(2)}) copy-start(f32[16]{0:T(128)} %copy-done.63) | copy-start | bytes 196
  449.1 9.4 %copy-start.33 = (bf16[1024,2304]{1,0:T(8,128)(2,1)}, bf16[1024,2304]{1,0:T(8,128)(2,1)S(1)}, u32[]{:S(2)}) copy-start(bf16[1024,2304]{1,0:T(8,128)(2,1)S(1)} %constant_dynamic-update-slice_fusion.6) | copy-start | bytes 14155780
  458.4 5.2 copy-start.22
  458.5 5.1 copy-start.44
  458.5 5.2 copy-start.50
  470.2 6.6 %slice-start.2 = ((s8[4718592]{0:T(1024)(128)(4,1)}), s8[4194304]{0:T(1024)(128)(4,1)S(1)}, s32[]{:S(2)}) async-start(s8[4718592]{0:T(1024)(128)(4,1)} %bitcast.148), calls=%async_computation.2 | async-start | bytes 8388608
  473.7 7.1 %slice-start = ((s8[4718592]{0:T(1024)(128)(4,1)}), s8[4194304]{0:T(1024)(128)(4,1)S(1)}, s32[]{:S(2)}) async-start(s8[4718592]{0:T(1024)(128)(4,1)} %bitcast.146), calls=%async_computation | async-start | bytes 8388608
  562.5 6.2 %copy-start.42 = (f32[24,768]{1,0:T(8,128)S(1)}, f32[24,768]{1,0:T(8,128)}, u32[]{:S(2)}) copy-start(f32[24,768]{1,0:T(8,128)} %get-tuple-element.102) | copy-start | bytes 221188
  (48 other events, 141.8 us)

commit v4 on v3

--- a/solution.py
+++ b/solution.py
@@ -12,6 +12,7 @@
 HEAD_DIM = 64
 LENGTH = 1024
 PAIR = 2 * HEAD_DIM
+GROUP = 4
 NN = (((1,), (0,)), ((), ()))
 NT = (((1,), (1,)), ((), ()))
 TN = (((0,), (0,)), ((), ()))
@@ -24,21 +25,71 @@
     return lax.dot_general(left, right, dims, precision=precise, preferred_element_type=F32)
 
 
-def layer_norm(values, gain_vec):
+def normalise(values):
     centred = values - jnp.mean(values, axis=-1, keepdims=True)
-    spread_sq = jnp.mean(centred * centred, axis=-1, keepdims=True)
-    return centred * lax.rsqrt(spread_sq + 1e-05) * gain_vec
-
-
-def gate_from(projected, embed_rows, route_row):
-    unit_rows = projected * lax.rsqrt(jnp.sum(projected * projected, axis=-1, keepdims=True) + 1.0)
-    anchor = embed_rows * lax.rsqrt(jnp.sum(embed_rows * embed_rows, axis=-1, keepdims=True) + 1.0)
-    logits = 3.0 * jnp.dot(
-        unit_rows, anchor.T, precision=lax.Precision.HIGHEST, preferred_element_type=F32
-    )
-    soft_rows = jax.nn.softmax(logits, axis=-1)
-    picked = route_row[:, None] == jnp.arange(soft_rows.shape[1], dtype=jnp.int32)[None, :]
-    return jnp.sum(jnp.where(picked, soft_rows, 0.0), axis=-1)
+    inverse = lax.rsqrt(jnp.mean(centred * centred, axis=-1, keepdims=True) + 1e-05)
+    return centred * inverse, inverse
+
+
+def normalise_back(grad, normed, inverse):
+    return inverse * (
+        grad
+        - jnp.mean(grad, axis=-1, keepdims=True)
+        - normed * jnp.mean(grad * normed, axis=-1, keepdims=True)
+    )
+
+
+def three_parts(values):
+    high = values.astype(LOW)
+    rest = values - high.astype(F32)
+    middle = rest.astype(LOW)
+    return high, middle, (rest - middle.astype(F32)).astype(LOW)
+
+
+def spread_parts(column):
+    lane = lax.broadcasted_iota(jnp.int32, (1, 128), 1)
+    high, middle, low = (part.astype(F32) for part in three_parts(column))
+    return jnp.where(lane == 0, high, jnp.where(lane == 1, middle, jnp.where(lane == 2, low, 0.0))).astype(LOW)
+
+
+def diagonal(rows):
+    shape = (rows, 128)
+    return lax.broadcasted_iota(jnp.int32, shape, 0) == lax.broadcasted_iota(jnp.int32, shape, 1)
+
+
+def to_column(row):
+    pieces = [
+        jnp.sum(jnp.where(diagonal(128), row[:, first : first + 128], 0.0), axis=1, keepdims=True)
+        for first in range(0, row.shape[1], 128)
+    ]
+    return jnp.concatenate(pieces, axis=0)
+
+
+def unit_length(rows):
+    inverse = lax.rsqrt(jnp.sum(rows * rows, axis=-1, keepdims=True) + 1.0)
+    return rows * inverse, inverse
+
+
+def route_probs(projected, embed_rows, route_column):
+    unit, inverse = unit_length(projected)
+    anchor, anchor_inverse = unit_length(embed_rows)
+    logits = 3.0 * dot(unit, anchor, NT, lax.Precision.HIGHEST)
+    weights = jnp.exp(logits - jnp.max(logits, axis=-1, keepdims=True))
+    probs = weights / jnp.sum(weights, axis=-1, keepdims=True)
+    lane = lax.broadcasted_iota(jnp.int32, (1, probs.shape[1]), 1)
+    picked = route_column == lane
+    gate = jnp.sum(jnp.where(picked, probs, 0.0), axis=-1, keepdims=True)
+    return unit, inverse, anchor, anchor_inverse, probs, picked, gate
+
+
+def slot_rows(slot_row, first, count):
+    slot = lax.broadcasted_iota(jnp.int32, (count, slot_row.shape[1]), 0) + first
+    return jnp.where(slot == slot_row, 1.0, 0.0).astype(LOW)
+
+
+def token_rows(slot_column, slots):
+    lane = lax.broadcasted_iota(jnp.int32, (slot_column.shape[0], slots), 1)
+    return jnp.where(lane == slot_column, 1.0, 0.0).astype(LOW)
 
 
 MESH = pl.DeviceIdType.MESH
@@ -182,11 +233,12 @@
     return plan
 
 
-def reduce_kernel(*refs, orders, width, places):
-    n_in = len(places)
-    ins, refs = refs[:n_in], refs[n_in:]
-    small_ref, out_ref, small_out, total, result, small_send, small_recv = refs[:7]
-    refs = refs[7:]
+def reduce_kernel(*refs, orders, width, places, sets):
+    ins = [refs[k * sets : (k + 1) * sets] for k in range(len(places))]
+    refs = refs[len(places) * sets :]
+    smalls, refs = refs[:sets], refs[sets:]
+    out_ref, small_out, total, result, small_send, small_recv = refs[:6]
+    refs = refs[6:]
     parts, stages = len(orders), len(orders[0])
     outgoing = [refs[p * stages : (p + 1) * stages] for p in range(parts)]
     incoming = [refs[(parts + p) * stages : (parts + p + 1) * stages] for p in range(parts)]
@@ -205,9 +257,9 @@
         pl.semaphore_signal(barrier, inc=1, device_id=partner(axis, bit), device_id_type=MESH)
     pl.semaphore_wait(barrier, stages)
 
-    for ref, place in zip(ins, places):
-        total[:, place : place + ref.shape[1]] = ref[...]
-    small_send[0] = small_ref[...]
+    for group, place in zip(ins, places):
+        total[:, place : place + group[0].shape[1]] = sum(ref[...].astype(F32) for ref in group)
+    small_send[0] = sum(ref[...] for ref in smalls)
 
     regions = [[(0, rows, p * width, width)] for p in range(parts)]
 
@@ -306,10 +358,11 @@
 def reduce_everywhere(big, small, cid):
     orders = reduce_orders(lax.axis_size("wide"), lax.axis_size("narrow"))
     places, columns = [], 0
-    for array in big:
+    for group in big:
         places.append(columns)
-        columns += array.shape[1]
-    rows = big[0].shape[0]
+        columns += group[0].shape[1]
+    rows = big[0][0].shape[0]
+    sets = len(small)
     width, parts, stages = columns // len(orders), len(orders), len(orders[0])
     buffers = []
     for order in orders:
@@ -319,15 +372,15 @@
             buffers.append(pltpu.VMEM((height, span), LOW))
     vmem = pl.BlockSpec(memory_space=pltpu.VMEM)
     return pl.pallas_call(
-        functools.partial(reduce_kernel, orders=orders, width=width, places=places),
-        in_specs=[vmem] * (len(big) + 1),
+        functools.partial(reduce_kernel, orders=orders, width=width, places=places, sets=sets),
+        in_specs=[vmem] * ((len(big) + 1) * sets),
         out_specs=[vmem, vmem],
-        out_shape=[jax.ShapeDtypeStruct((rows, columns), LOW), jax.ShapeDtypeStruct(small.shape, F32)],
+        out_shape=[jax.ShapeDtypeStruct((rows, columns), LOW), jax.ShapeDtypeStruct(small[0].shape, F32)],
         scratch_shapes=[
             pltpu.VMEM((rows, columns), F32),
             pltpu.VMEM((rows, columns), LOW),
-            pltpu.VMEM((stages, *small.shape), F32),
-            pltpu.VMEM((stages, *small.shape), F32),
+            pltpu.VMEM((stages, *small[0].shape), F32),
+            pltpu.VMEM((stages, *small[0].shape), F32),
         ]
         + buffers
         + buffers
@@ -338,7 +391,7 @@
         ),
         cost_estimate=pl.CostEstimate(flops=10**9, bytes_accessed=20 * 2**20, transcendentals=0),
         name="reduce_everywhere",
-    )(*big, small)
+    )(*(array for group in big for array in group), *small)
 
 
 def join_kernel(own_ref, far_ref, out_ref):
@@ -376,73 +429,166 @@
     )(own, *fars)
 
 
-def attention_forward_kernel(q_ref, k_ref, v_ref, mixed_ref, soft_ref, inv_ref, *, rows):
+def attend_pair(query, keys, values, soft_ref, place, rows):
     lane = lax.broadcasted_iota(jnp.int32, (1, PAIR), 1)
-    keys, values = k_ref[...], v_ref[...]
     none = jnp.zeros_like(keys)
+    mixed_blocks, inverse_blocks = [], []
     for block in range(LENGTH // rows):
         part = slice(block * rows, (block + 1) * rows)
-        query = q_ref[part, :] * LOW(HEAD_DIM**-0.5)
+        scaled = query[part, :] * LOW(HEAD_DIM**-0.5)
         mixed, inverses = None, []
         for head in range(2):
             mine = (lane < HEAD_DIM) if head == 0 else (lane >= HEAD_DIM)
-            scores = dot(query, jnp.where(mine, keys, none), NT)
+            scores = dot(scaled, jnp.where(mine, keys, none), NT)
             top = jnp.max(scores, axis=1, keepdims=True)
             weights = jnp.exp(scores - top)
             inverse = 1.0 / jnp.sum(weights, axis=1, keepdims=True)
             weights = weights.astype(LOW)
-            soft_ref[head, part, :] = weights
+            soft_ref[place + head, part, :] = weights
             inverses.append(jnp.broadcast_to(inverse, (rows, PAIR)))
             term = dot(weights, jnp.where(mine, values, none)) * inverse
             mixed = term if mixed is None else mixed + term
-        mixed_ref[part, :] = mixed.astype(LOW)
-        inv_ref[part, :] = jnp.where(lane < HEAD_DIM, inverses[0], inverses[1])
-
-
-def attention_forward(qkv_rows, moves, pushes, cid):
-    pairs = D // PAIR
-    columns = lambda first: pl.BlockSpec((LENGTH, PAIR), lambda i: (0, first + i))
+        mixed_blocks.append(mixed)
+        inverse_blocks.append(jnp.where(lane < HEAD_DIM, inverses[0], inverses[1]))
+    return jnp.concatenate(mixed_blocks, axis=0), jnp.concatenate(inverse_blocks, axis=0)
+
+
+def forward_kernel(
+    tokens_ref, gain_one_ref, wq_ref, wk_ref, wv_ref, wo_ref, gain_two_ref, route_ref, embed_ref, slot_ref, id_ref,
+    q_ref, k_ref, v_ref, soft_ref, inv_ref, mixed_ref, first_ref, sent_ref, gates_ref, projected_ref,
+    normed, total, *, steps, slots, slot_cap,
+):
+    step = pl.program_id(0)
+
+    @pl.when(step == 0)
+    def _():
+        values = tokens_ref[...].astype(F32)
+        normed[...] = (normalise(values)[0] * gain_one_ref[...]).astype(LOW)
+        total[...] = values
+
+    rows = normed[...]
+    q_ref[...] = dot(rows, wq_ref[...]).astype(LOW)
+    k_ref[...] = dot(rows, wk_ref[...]).astype(LOW)
+    v_ref[...] = dot(rows, wv_ref[...]).astype(LOW)
+    for pair in range(GROUP // 2):
+        lanes = slice(pair * PAIR, (pair + 1) * PAIR)
+        mixed, inverse = attend_pair(q_ref[:, lanes], k_ref[:, lanes], v_ref[:, lanes], soft_ref, 2 * pair, 512)
+        mixed_ref[:, lanes] = mixed.astype(LOW)
+        inv_ref[:, lanes] = inverse
+    total[...] += dot(mixed_ref[...], wo_ref[...])
+
+    @pl.when(step == steps - 1)
+    def _():
+        first = total[...]
+        first_ref[...] = first
+        second = (normalise(first)[0] * gain_two_ref[...]).astype(LOW)
+        projected = dot(second, route_ref[...])
+        projected_ref[...] = projected
+        route_column = to_column(id_ref[...].astype(F32)).astype(jnp.int32)
+        gate = route_probs(projected, embed_ref[...], route_column)[-1]
+        parts = spread_parts(gate)
+        slot_row = slot_ref[...]
+        block = 256
+        for begin in range(0, slots, block):
+            table = slot_rows(slot_row, begin, block)
+            sent_ref[begin : begin + block, :] = dot(table, second).astype(LOW)
+            gathered = jnp.sum(dot(table, parts), axis=1, keepdims=True)
+            for w in range(begin // slot_cap, (begin + block) // slot_cap):
+                column = gathered[w * slot_cap - begin : (w + 1) * slot_cap - begin, :]
+                row = jnp.sum(jnp.where(diagonal(slot_cap), column, 0.0), axis=0, keepdims=True)
+                gates_ref[w] = jnp.broadcast_to(row, (8, 128))
+
+
+def forward_stage(m, tokens, gains, weights, w_route, embed, slot_index, route_ids, slot_cap, moves, pushes, cid):
+    tok_count, width = tokens.shape[1:]
+    experts = embed.shape[0]
+    slots = experts * slot_cap
+    steps = HEADS // GROUP
+    span = GROUP * HEAD_DIM
+    one = pl.Buffered(1)
+    fixed = lambda shape: pl.BlockSpec(shape, lambda i: (0,) * len(shape), pipeline_mode=one)
+    of_m = lambda *shape: pl.BlockSpec((None, *shape), lambda i: (m, 0, 0), pipeline_mode=one)
+    columns = lambda height: pl.BlockSpec((height, span), lambda i: (0, i))
+    whole = lambda *shape: pl.BlockSpec(shape, lambda i: (0,) * len(shape))
+    gain_one, gain_two = gains
+    wq, wk, wv, wo = weights
+    low = lambda *shape: jax.ShapeDtypeStruct(shape, LOW)
+    full = lambda *shape: jax.ShapeDtypeStruct(shape, F32)
     return call_with_moves(
-        functools.partial(attention_forward_kernel, rows=512),
+        functools.partial(forward_kernel, steps=steps, slots=slots, slot_cap=slot_cap),
         moves,
         pushes,
         cid,
-        grid=(pairs,),
-        in_specs=[columns(0), columns(pairs), columns(2 * pairs)],
-        out_specs=[columns(0), pl.BlockSpec((2, LENGTH, LENGTH), lambda i: (i, 0, 0)), columns(0)],
+        grid=(steps,),
+        in_specs=[
+            of_m(tok_count, width), fixed((1, width)), columns(width), columns(width), columns(width),
+            pl.BlockSpec((span, width), lambda i: (i, 0)), fixed((1, width)), fixed(w_route.shape),
+            fixed(embed.shape), of_m(1, tok_count), of_m(1, tok_count),
+        ],
+        out_specs=[
+            columns(tok_count), columns(tok_count), columns(tok_count),
+            pl.BlockSpec((GROUP, LENGTH, LENGTH), lambda i: (i, 0, 0)),
+            columns(tok_count), columns(tok_count), whole(tok_count, width), whole(slots, width),
+            whole(experts, 8, 128), whole(tok_count, w_route.shape[1]),
+        ],
         out_shape=[
-            jax.ShapeDtypeStruct((LENGTH, D), LOW),
-            jax.ShapeDtypeStruct((HEADS, LENGTH, LENGTH), LOW),
-            jax.ShapeDtypeStruct((LENGTH, D), F32),
+            low(tok_count, width), low(tok_count, width), low(tok_count, width), low(HEADS, LENGTH, LENGTH),
+            full(tok_count, width), low(tok_count, width), full(tok_count, width), low(slots, width),
+            full(experts, 8, 128), full(tok_count, w_route.shape[1]),
         ],
+        scratch_shapes=[pltpu.VMEM((tok_count, width), LOW), pltpu.VMEM((tok_count, width), F32)],
         cost=pl.CostEstimate(
-            flops=20 * 10**9, bytes_accessed=30 * 2**20, transcendentals=HEADS * LENGTH * LENGTH
+            flops=30 * 10**9, bytes_accessed=50 * 2**20, transcendentals=HEADS * LENGTH * LENGTH
         ),
-        name="attention_forward",
-        args=(qkv_rows, qkv_rows, qkv_rows),
-    )
-
-
-def attention_backward_kernel(
-    q_ref, k_ref, v_ref, grad_ref, mixed_ref, soft_ref, inv_ref, dq_ref, dk_ref, dv_ref, *, rows
-):
+        name="forward_stage",
+        args=(tokens, gain_one, wq, wk, wv, wo, gain_two, w_route, embed, slot_index, route_ids),
+    )
+
+
+def dispatch_kernel(slot_ref, rows_ref, *out_refs, slots):
+    for m, out_ref in enumerate(out_refs):
+
+        @pl.when(pl.program_id(0) == m)
+        def _():
+            for begin in range(0, slots, 256):
+                table = slot_rows(slot_ref[...], begin, 256)
+                out_ref[begin : begin + 256, :] = dot(table, rows_ref[...]).astype(LOW)
+
+
+def dispatch(slot_index, rows, slots):
+    micro_count, tok_count, width = rows.shape
+    return pl.pallas_call(
+        functools.partial(dispatch_kernel, slots=slots),
+        grid=(micro_count,),
+        in_specs=[
+            pl.BlockSpec((None, 1, tok_count), lambda m: (m, 0, 0)),
+            pl.BlockSpec((None, tok_count, width), lambda m: (m, 0, 0)),
+        ],
+        out_specs=[pl.BlockSpec((slots, width), lambda m: (0, 0))] * micro_count,
+        out_shape=[jax.ShapeDtypeStruct((slots, width), LOW)] * micro_count,
+        compiler_params=pltpu.CompilerParams(vmem_limit_bytes=VMEM_BYTES),
+        cost_estimate=pl.CostEstimate(flops=3 * 10**9, bytes_accessed=6 * 2**20, transcendentals=0),
+        name="dispatch",
+    )(slot_index, rows)
+
+
+def attend_pair_back(query, keys, values, grad, mixed, soft_ref, place, inverses, rows):
     lane = lax.broadcasted_iota(jnp.int32, (1, PAIR), 1)
     scale = LOW(HEAD_DIM**-0.5)
-    keys, values = k_ref[...], v_ref[...]
     none = jnp.zeros_like(keys)
-    dk_parts, dv_parts = [None, None], [None, None]
+    dk_parts, dv_parts, dq_blocks = [None, None], [None, None], []
     for block in range(LENGTH // rows):
         part = slice(block * rows, (block + 1) * rows)
-        query_t = (q_ref[part, :] * scale).T
-        scaled = grad_ref[part, :].astype(F32) * inv_ref[part, :]
-        inner = scaled * mixed_ref[part, :].astype(F32)
+        query_t = (query[part, :] * scale).T
+        scaled = grad[part, :].astype(F32) * inverses[part, :]
+        inner = scaled * mixed[part, :].astype(F32)
         scaled = scaled.astype(LOW)
         scaled_t = scaled.T
         grad_query = None
         for head in range(2):
             mine = (lane < HEAD_DIM) if head == 0 else (lane >= HEAD_DIM)
             own = slice(head * HEAD_DIM, (head + 1) * HEAD_DIM)
-            weights = soft_ref[head, part, :]
+            weights = soft_ref[place + head, part, :]
             grad_soft = dot(scaled, jnp.where(mine, values, none), NT)
             centre = jnp.sum(jnp.where(mine, inner, 0.0), axis=1, keepdims=True)
             grad_scores = (weights.astype(F32) * (grad_soft - centre)).astype(LOW)
@@ -452,35 +598,213 @@
             dv = dot(scaled_t[own, :], weights)
             dk_parts[head] = dk if dk_parts[head] is None else dk_parts[head] + dk
             dv_parts[head] = dv if dv_parts[head] is None else dv_parts[head] + dv
-        dq_ref[part, :] = (grad_query * HEAD_DIM**-0.5).astype(LOW)
-    dk_ref[...] = jnp.concatenate(dk_parts, axis=0).T.astype(LOW)
-    dv_ref[...] = jnp.concatenate(dv_parts, axis=0).T.astype(LOW)
-
-
-def attention_backward(qkv_rows, grad_mixed, mixed_rows, soft, inverses, moves, pushes, cid):
-    pairs = D // PAIR
-    columns = lambda first: pl.BlockSpec((LENGTH, PAIR), lambda i: (0, first + i))
+        dq_blocks.append(grad_query * HEAD_DIM**-0.5)
+    return (
+        jnp.concatenate(dq_blocks, axis=0),
+        jnp.concatenate(dk_parts, axis=0).T,
+        jnp.concatenate(dv_parts, axis=0).T,
+    )
+
+
+def backward_kernel(
+    tokens_ref, cot_ref, gain_one_ref, wq_ref, wk_ref, wv_ref, wo_ref, gain_two_ref, route_ref, embed_ref, slot_ref,
+    id_ref, first_ref, projected_ref, home_ref, dots_ref, q_ref, k_ref, v_ref, mixed_ref, soft_ref, inv_ref,
+    dwq_ref, dwk_ref, dwv_ref, dwo_ref, gtok_ref, small_ref,
+    grad_first, branch, normed_t, total, mixed_grad, dq_sc, dk_sc, dv_sc, soft_buf, soft_sem,
+    *, steps, slots, slot_cap,
+):
+    step = pl.program_id(0)
+    width = tokens_ref.shape[1]
+    experts, router_dim = embed_ref.shape
+    pairs = GROUP // 2
+
+    def soft_pair(pair):
+        at = step * GROUP + 2 * pair
+        return pltpu.make_async_copy(soft_ref.at[pl.ds(at, 2)], soft_buf.at[pair % 2], soft_sem.at[pair % 2])
+
+    @pl.when(step == 0)
+    def _():
+        soft_pair(0).start()
+        normed_one = normalise(tokens_ref[...].astype(F32))[0]
+        normed_t[...] = (normed_one * gain_one_ref[...]).astype(LOW).T
+        slot_column = to_column(slot_ref[...].astype(F32)).astype(jnp.int32)
+        route_column = to_column(id_ref[...].astype(F32)).astype(jnp.int32)
+        columns = [
+            jnp.sum(jnp.where(diagonal(slot_cap), dots_ref[w, 0:1, :], 0.0), axis=1, keepdims=True)
+            for w in range(experts)
+        ]
+        dots = spread_parts(jnp.concatenate(columns, axis=0))
+        grads = []
+        block = 256
+        for begin in range(0, slot_column.shape[0], block):
+            table = token_rows(slot_column[begin : begin + block, :], slots)
+            grad_first[begin : begin + block, :] = dot(table, home_ref[...])
+            grads.append(jnp.sum(dot(table, dots), axis=1, keepdims=True))
+        grad_gate = jnp.concatenate(grads, axis=0)
+        projected, embed_rows = projected_ref[...], embed_ref[...]
+        unit, inverse, anchor, anchor_inverse, probs, picked, gate = route_probs(
+            projected, embed_rows, route_column
+        )
+        grad_logits = grad_gate * gate * (jnp.where(picked, 1.0, 0.0) - probs)
+        grad_unit = 3.0 * dot(grad_logits, anchor, NN, lax.Precision.HIGHEST)
+        grad_anchor = 3.0 * dot(grad_logits, unit, TN, lax.Precision.HIGHEST)
+        grad_projected = inverse * grad_unit - inverse**3 * projected * jnp.sum(
+            projected * grad_unit, axis=-1, keepdims=True
+        )
+        term_embed = anchor_inverse * grad_anchor - anchor_inverse**3 * embed_rows * jnp.sum(
+            embed_rows * grad_anchor, axis=-1, keepdims=True
+        )
+        normed_two, inverse_two = normalise(first_ref[...])
+        second = (normed_two * gain_two_ref[...]).astype(LOW)
+        grad_second = grad_first[...]
+        term_route = None
+        for part in three_parts(grad_projected):
+            grad_second += dot(part, route_ref[...], NT)
+            term = dot(part, second, TN)
+            term_route = term if term_route is None else term_route + term
+        small_ref[...] = jnp.zeros_like(small_ref)
+        small_ref[0:router_dim, 0:width] = term_route
+        small_ref[router_dim + 1 : router_dim + 2, 0:width] = jnp.sum(grad_second * normed_two, axis=0, keepdims=True)
+        small_ref[0:experts, width : width + router_dim] = term_embed
+        value = cot_ref[...].astype(F32) + normalise_back(grad_second * gain_two_ref[...], normed_two, inverse_two)
+        grad_first[...] = value
+        branch[...] = value.astype(LOW)
+        total[...] = jnp.zeros_like(total)
+
+    rows = branch[...]
+    dwo_ref[...] = dot(mixed_ref[...], rows, TN).astype(LOW)
+    mixed_grad[...] = dot(rows, wo_ref[...], NT).astype(LOW)
+    for pair in range(pairs):
+        lanes = slice(pair * PAIR, (pair + 1) * PAIR)
+        soft_pair(pair).wait()
+        if pair + 1 < pairs:
+            soft_pair(pair + 1).start()
+        else:
+
+            @pl.when(step + 1 < steps)
+            def _():
+                soft_pair(pairs).start()
+
+        dq, dk, dv = attend_pair_back(
+            q_ref[:, lanes], k_ref[:, lanes], v_ref[:, lanes], mixed_grad[:, lanes], mixed_ref[:, lanes],
+            soft_buf.at[pair % 2], 0, inv_ref[:, lanes], 512,
+        )
+        dq_sc[:, lanes] = dq.astype(LOW)
+        dk_sc[:, lanes] = dk.astype(LOW)
+        dv_sc[:, lanes] = dv.astype(LOW)
+    normed_rows = normed_t[...]
+    for grad_ref, weight_ref, out_ref in (
+        (dq_sc, wq_ref, dwq_ref), (dk_sc, wk_ref, dwk_ref), (dv_sc, wv_ref, dwv_ref)
+    ):
+        grad = grad_ref[...]
+        out_ref[...] = dot(normed_rows, grad).astype(LOW)
+        total[...] += dot(grad, weight_ref[...], NT)
+
+    @pl.when(step == steps - 1)
+    def _():
+        normed_one, inverse_one = normalise(tokens_ref[...].astype(F32))
+        grad = total[...]
+        small_ref[router_dim : router_dim + 1, 0:width] = jnp.sum(grad * normed_one, axis=0, keepdims=True)
+        gtok_ref[...] = (
+            grad_first[...] + normalise_back(grad * gain_one_ref[...], normed_one, inverse_one)
+        ).astype(LOW)
+
+
+def backward_stage(
+    m, tokens, grad_out, gains, weights, w_route, embed, slot_index, route_ids, kept, home, slot_cap, moves, pushes, cid
+):
+    tok_count, width = tokens.shape[1:]
+    experts, router_dim = embed.shape
+    slots = experts * slot_cap
+    steps = HEADS // GROUP
+    span = GROUP * HEAD_DIM
+    one = pl.Buffered(1)
+    fixed = lambda shape: pl.BlockSpec(shape, lambda i: (0,) * len(shape), pipeline_mode=one)
+    of_m = lambda *shape: pl.BlockSpec((None, *shape), lambda i: (m, 0, 0), pipeline_mode=one)
+    columns = lambda height: pl.BlockSpec((height, span), lambda i: (0, i))
+    lines = pl.BlockSpec((span, width), lambda i: (i, 0))
+    gain_one, gain_two = gains
+    wq, wk, wv, wo = weights
+    first, projected, q, k, v, mixed, soft, inverses = kept
+    low = lambda *shape: jax.ShapeDtypeStruct(shape, LOW)
+    small = (-(-max(experts, router_dim + 2) // 8) * 8, width + 128)
     return call_with_moves(
-        functools.partial(attention_backward_kernel, rows=512),
+        functools.partial(backward_kernel, steps=steps, slots=slots, slot_cap=slot_cap),
         moves,
         pushes,
         cid,
-        grid=(pairs,),
+        grid=(steps,),
         in_specs=[
-            columns(0),
-            columns(pairs),
-            columns(2 * pairs),
-            columns(0),
-            columns(0),
-            pl.BlockSpec((2, LENGTH, LENGTH), lambda i: (i, 0, 0)),
-            columns(0),
+            of_m(tok_count, width), of_m(tok_count, width), fixed((1, width)), columns(width), columns(width),
+            columns(width), lines, fixed((1, width)), fixed(w_route.shape), fixed(embed.shape), of_m(1, tok_count),
+            of_m(1, tok_count), fixed(first.shape), fixed(projected.shape), fixed(home[0].shape), fixed(home[1].shape),
+            columns(tok_count), columns(tok_count), columns(tok_count), columns(tok_count),
+            pl.BlockSpec(memory_space=pl.ANY), columns(tok_count),
         ],
-        out_specs=[columns(0)] * 3,
-        out_shape=[jax.ShapeDtypeStruct((LENGTH, D), LOW)] * 3,
-        cost=pl.CostEstimate(flops=25 * 10**9, bytes_accessed=36 * 2**20, transcendentals=0),
-        name="attention_backward",
-        args=(qkv_rows, qkv_rows, qkv_rows, grad_mixed, mixed_rows, soft, inverses),
-    )
+        out_specs=[
+            columns(width), columns(width), columns(width), lines, fixed((tok_count, width)), fixed(small),
+        ],
+        out_shape=[
+            low(width, width), low(width, width), low(width, width), low(width, width), low(tok_count, width),
+            jax.ShapeDtypeStruct(small, F32),
+        ],
+        scratch_shapes=[
+            pltpu.VMEM((tok_count, width), F32), pltpu.VMEM((tok_count, width), LOW),
+            pltpu.VMEM((width, tok_count), LOW), pltpu.VMEM((tok_count, width), F32),
+        ]
+        + [pltpu.VMEM((tok_count, span), LOW)] * 4
+        + [pltpu.VMEM((2, 2, LENGTH, LENGTH), LOW), pltpu.SemaphoreType.DMA((2,))],
+        cost=pl.CostEstimate(flops=40 * 10**9, bytes_accessed=50 * 2**20, transcendentals=0),
+        name="backward_stage",
+        args=(
+            tokens, grad_out, gain_one, wq, wk, wv, wo, gain_two, w_route, embed, slot_index, route_ids, first,
+            projected, *home, q, k, v, mixed, soft, inverses,
+        ),
+    )
+
+
+def finish_kernel(*refs, micro_count, slots):
+    slot_ref, id_ref, embed_ref = refs[:3]
+    ins, (out_ref, grad_ref) = refs[3:-2], refs[-2:]
+    for m in range(micro_count):
+        first_ref, projected_ref, home_ref, gtok_ref = ins[4 * m : 4 * m + 4]
+
+        @pl.when(pl.program_id(0) == m)
+        def _():
+            slot_column = to_column(slot_ref[...].astype(F32)).astype(jnp.int32)
+            route_column = to_column(id_ref[...].astype(F32)).astype(jnp.int32)
+            gate = route_probs(projected_ref[...], embed_ref[...], route_column)[-1]
+            returned = dot(token_rows(slot_column, slots), home_ref[...])
+            out_ref[...] = (first_ref[...] + gate * returned).astype(LOW)
+            grad_ref[...] = gtok_ref[...]
+
+
+def finish(slot_index, route_ids, embed, parts, slots):
+    micro_count, _, tok_count = slot_index.shape
+    width = parts[0][0].shape[1]
+    rows = 256
+    blocks = tok_count // rows
+    row = pl.BlockSpec((None, 1, rows), lambda m, i: (m, 0, i))
+    whole = lambda shape: pl.BlockSpec(shape, lambda m, i: (0, 0))
+    in_specs, args = [row, row, whole(embed.shape)], [slot_index, route_ids, embed]
+    for at, (first, projected, home, gtok) in enumerate(parts):
+        place = lambda m, i, at=at: (jnp.where(m == at, i, jnp.where(m < at, 0, blocks - 1)), 0)
+        in_specs += [
+            pl.BlockSpec((rows, width), place), pl.BlockSpec((rows, projected.shape[1]), place), whole(home.shape),
+            pl.BlockSpec((rows, width), place),
+        ]
+        args += [first, projected, home, gtok]
+    out = pl.BlockSpec((None, rows, width), lambda m, i: (m, i, 0))
+    return pl.pallas_call(
+        functools.partial(finish_kernel, micro_count=micro_count, slots=slots),
+        grid=(micro_count, blocks),
+        in_specs=in_specs,
+        out_specs=[out, out],
+        out_shape=[jax.ShapeDtypeStruct((micro_count, tok_count, width), LOW)] * 2,
+        compiler_params=pltpu.CompilerParams(vmem_limit_bytes=VMEM_BYTES),
+        cost_estimate=pl.CostEstimate(flops=3 * 10**9, bytes_accessed=18 * 2**20, transcendentals=0),
+        name="finish",
+    )(*args)
 
 
 def gelu_and_slope(values):
@@ -492,11 +816,6 @@
     tail = series * ratio * bell
     below = jnp.where(values >= 0.0, 1.0 - tail, tail)
     return values * below, below + values * bell * 0.3989422804014327
-
-
-def diagonal(slot_cap):
-    shape = (slot_cap, 128)
-    return lax.broadcasted_iota(jnp.int32, shape, 0) == lax.broadcasted_iota(jnp.int32, shape, 1)
 
 
 def expert_kernel(*refs, more, last, per, steps, slot_cap):
@@ -681,12 +1000,9 @@
     w_outer,
 ):
     micro_count, tok_count, feat_width = tokens.shape
-    narrow_count = lax.axis_size("narrow")
     expert_count = embed.shape[0]
     slot_cap = max(2, tok_count // expert_count)
     slots = expert_count * slot_cap
-    w_qkv = jnp.concatenate([w_query, w_key, w_value], axis=1)
-    route_float = w_route.astype(F32)
     own_in, own_outer = w_in[0], w_outer[0]
     units = own_in.shape[1]
     tile = tile_of(units)
@@ -697,7 +1013,11 @@
         (own_outer, lambda ref, j, t=t: ref.at[t * tile : (t + 1) * tile, :], (tile, feat_width)) for t in range(per)
     ]
     early = len(weight_pushes) // 3
-    slot_columns = jnp.arange(slots, dtype=jnp.int32)
+    slot_index = jnp.where(keep_ids > 0, route_ids * slot_cap + slot_ids, -1)[:, None, :]
+    route_rows = route_ids[:, None, :]
+    gains = (gain_one[None], gain_two[None])
+    mixers = (w_query, w_key, w_value, w_out)
+    router = (w_route, embed, slot_index, route_rows)
 
     def boxes(rows):
         return rows.reshape((expert_count, slot_cap) + rows.shape[1:])
@@ -705,46 +1025,20 @@
     def flat(boxed):
         return boxed.reshape((expert_count * slot_cap,) + boxed.shape[2:])
 
-    tables, cot_boxes = [], []
-    for m in range(micro_count):
-        slot_index = jnp.where(keep_ids[m] > 0, route_ids[m] * slot_cap + slot_ids[m], -1)
-        table = (slot_index[:, None] == slot_columns[None, :]).astype(LOW)
-        tables.append(table)
-        cot_boxes.append(boxes(dot(table, grad_out[m], TN).astype(LOW)))
-
-    ahead, send = [], []
-    for m in range(micro_count):
-        inputs = tokens[m].astype(F32)
-        normed_one, pull_one = jax.vjp(layer_norm, inputs, gain_one)
-        normed_low = normed_one.astype(LOW)
-        qkv_rows = dot(normed_low, w_qkv).astype(LOW)
-        if m == 0:
-            (mixed_rows, soft, inverses), (cot_0,), far_a = attention_forward(
-                qkv_rows, (cot_boxes[0],), weight_pushes[:early], 1
-            )
-        else:
-            (mixed_rows, soft, inverses), (sent_0, gates_0, cot_1), far_b = attention_forward(
-                qkv_rows, (*send[0], cot_boxes[1]), weight_pushes[early:], 2
-            )
-        first_sum = inputs + dot(mixed_rows, w_out)
-        normed_two, pull_two = jax.vjp(layer_norm, first_sum, gain_two)
-        second_low = normed_two.astype(LOW)
-        projected = dot(second_low, w_route)
-        gate_prob, pull_gate = jax.vjp(
-            lambda proj_in, embed_in: gate_from(proj_in, embed_in, route_ids[m]), projected, embed
-        )
-        gates = jnp.sum(tables[m].astype(F32) * gate_prob[:, None], axis=0)
-        gates = jnp.pad(gates.reshape(expert_count, 1, slot_cap), ((0, 0), (0, 7), (0, 128 - slot_cap)))
-        send.append((boxes(dot(tables[m], second_low, TN).astype(LOW)), gates))
-        ahead.append(
-            (normed_low, pull_one, qkv_rows, mixed_rows, soft, inverses, first_sum, pull_two,
-             second_low, gate_prob, pull_gate)
-        )
+    cot_boxes = [boxes(rows) for rows in dispatch(slot_index, grad_out, slots)]
+    (*ahead_0, sent, gates, projected), (cot_0,), far_a = forward_stage(
+        0, tokens, gains, mixers, *router, slot_cap, (cot_boxes[0],), weight_pushes[:early], 1
+    )
+    ahead_0.append(projected)
+    (*ahead_1, next_sent, next_gates, projected), (sent_0, gates_0, cot_1), far_b = forward_stage(
+        1, tokens, gains, mixers, *router, slot_cap, (boxes(sent), gates, cot_boxes[1]), weight_pushes[early:], 2
+    )
+    ahead_1.append(projected)
 
     far = [*far_a, *far_b]
     weights = (own_in, own_outer, far[:per], far[per:])
     (result_0, grad_0, dots_0, *old), (sent_1, gates_1), _ = expert_stage(
-        flat(sent_0), flat(cot_0), gates_0, weights, (), False, slot_cap, send[1], (), 3
+        flat(sent_0), flat(cot_0), gates_0, weights, (), False, slot_cap, (boxes(next_sent), next_gates), (), 3
     )
     (result_1, grad_1, dots_1, near_din, near_douter, far_din, far_douter), (home_grad_0, home_dots_0), _ = expert_stage(
         flat(sent_1), flat(cot_1), gates_1, weights, tuple(old), True, slot_cap, (boxes(grad_0), dots_0), (), 4
@@ -756,68 +1050,38 @@
     ]
     later = len(grad_pushes) - early
 
-    input_grads, sums = [], None
-    for m in range(micro_count):
-        (normed_low, pull_one, qkv_rows, mixed_rows, soft, inverses, first_sum, pull_two,
-         second_low, gate_prob, pull_gate) = ahead[m]
-        home_grad, home_dots = (home_grad_0, home_dots_0) if m == 0 else (home_grad_1, home_dots_1)
-        table = tables[m]
-        grad_sum = grad_out[m].astype(F32)
-        slot_dots = home_dots[:, 0, :slot_cap].reshape(slots)
-        grad_gate = jnp.sum(table.astype(F32) * slot_dots[None, :], axis=-1)
-        grad_projected, grad_embed = pull_gate(grad_gate)
-        grad_second = dot(table, flat(home_grad)) + dot(
-            grad_projected, route_float, NT, lax.Precision.HIGHEST
-        )
-        grad_route = dot(second_low.astype(F32), grad_projected, TN, lax.Precision.HIGHEST)
-        grad_first_norm, grad_gain_two = pull_two(grad_second)
-        grad_first = grad_sum + grad_first_norm
-        grad_branch = grad_first.astype(LOW)
-        grad_wo = dot(mixed_rows, grad_branch, TN)
-        grad_mixed = dot(grad_branch, w_out, NT).astype(LOW)
-        if m == 0:
-            grads, (home_grad_1, home_dots_1, home_result_0), got_a = attention_backward(
-                qkv_rows, grad_mixed, mixed_rows, soft, inverses,
-                (boxes(grad_1), dots_1, boxes(result_0)), grad_pushes[:later], 5
-            )
-        else:
-            grads, (home_result_1,), got_b = attention_backward(
-                qkv_rows, grad_mixed, mixed_rows, soft, inverses, (boxes(result_1),), grad_pushes[later:], 6
-            )
-        grad_qkv = jnp.concatenate(grads, axis=1)
-        grad_wqkv = dot(normed_low, grad_qkv, TN)
-        grad_input_norm, grad_gain_one = pull_one(dot(grad_qkv, w_qkv, NT))
-        input_grads.append((grad_first + grad_input_norm).astype(LOW))
-        terms = (grad_gain_one, grad_wqkv, grad_wo, grad_gain_two, grad_route, grad_embed)
-        sums = terms if sums is None else tuple(a + b for a, b in zip(sums, terms))
-    outputs = []
-    for m, home_result in enumerate((home_result_0, home_result_1)):
-        first_sum, gate_prob = ahead[m][6], ahead[m][9]
-        returned = dot(tables[m], flat(home_result))
-        outputs.append((first_sum + gate_prob[:, None] * returned).astype(LOW))
-    gain_one_sum, wqkv_sum, wo_sum, gain_two_sum, route_sum, embed_sum = sums
-    router_dim = route_sum.shape[1]
-    small = jnp.concatenate(
-        [
-            route_sum.T,
-            gain_one_sum[None],
-            gain_two_sum[None],
-            jnp.pad(embed_sum.reshape(1, -1), ((0, 0), (0, feat_width - embed_sum.size))),
-            jnp.zeros((-(router_dim + 3) % 8, feat_width), F32),
-        ],
-        axis=0,
-    )
-    big, small = reduce_everywhere((wqkv_sum, wo_sum), small, 7)
+    def kept(ahead):
+        q, k, v, soft, inverses, mixed, first, projected = ahead
+        return first, projected, q, k, v, mixed, soft, inverses
+
+    (*big_0, gtok_0, small_0), (home_grad_1, home_dots_1), got_a = backward_stage(
+        0, tokens, grad_out, gains, mixers, *router, kept(ahead_0), (flat(home_grad_0), home_dots_0), slot_cap,
+        (boxes(grad_1), dots_1), grad_pushes[:later], 5
+    )
+    (*big_1, gtok_1, small_1), (home_result_0, home_result_1), got_b = backward_stage(
+        1, tokens, grad_out, gains, mixers, *router, kept(ahead_1), (flat(home_grad_1), home_dots_1), slot_cap,
+        (boxes(result_0), boxes(result_1)), grad_pushes[later:], 6
+    )
+    block_out, grad_tokens = finish(
+        slot_index, route_rows, embed,
+        (
+            (ahead_0[6], ahead_0[7], flat(home_result_0), gtok_0),
+            (ahead_1[6], ahead_1[7], flat(home_result_1), gtok_1),
+        ),
+        slots,
+    )
+    big, small = reduce_everywhere(list(zip(big_0, big_1)), (small_0, small_1), 7)
     big = [big[:, k * feat_width : (k + 1) * feat_width].astype(F32) for k in range(4)]
+    router_dim = w_route.shape[1]
     got = [*got_a, *got_b]
     return (
-        jnp.stack(outputs),
-        jnp.stack(input_grads),
-        small[router_dim],
+        block_out,
+        grad_tokens,
+        small[router_dim, :feat_width],
         *big,
-        small[router_dim + 1],
-        small[:router_dim].T,
-        small[router_dim + 2, : embed.size].reshape(embed.shape),
+        small[router_dim + 1, :feat_width],
+        small[:router_dim, :feat_width].T,
+        small[:expert_count, feat_width : feat_width + router_dim],
         join(near_din, got[:per], 1),
         join(near_douter, got[per:], 0),
     )

time: 607 us -> 537 us (0.88)
  matrix products: 86.4 us -> 0 us
  Pallas kernels: 430 us -> 515 us
  local copies, waits for them, and re-layouts: 43.5 us -> 10.1 us
  other arithmetic: 36.6 us -> 6.94 us
    dot_general x32 -> x0, matrix products: 86.4 us -> none  [the longest x26 84.9 us: dot(): lax.dot_general(left, right, dims, precision=precise, preferred_element_t...]
    pallas_call x6, Pallas kernels: 342 us -> 393 us  [call_with_moves(): pl.pallas_call(kernel, grid=grid, in_specs=list(in_specs) + [anywhere] *...]
    unnamed x157 -> x1, local copies, waits for them, and re-layouts: 30.9 us -> 1.55 us
    pallas_call x0 -> x2, Pallas kernels: none -> 19.8 us  [the longest x1 13.1 us: finish(): pl.pallas_call(functools.partial(finish_kernel, micro_count=micro_count,...]
    pallas_call x1, Pallas kernels: 75.4 us -> 90.7 us  [reduce_everywhere(): pl.pallas_call(functools.partial(reduce_kernel, orders=orders, width=widt...]
    reduce_sum x20 -> x0, other arithmetic: 11.9 us -> none  [the longest x4 5.56 us: layer_norm(): centred = values - jnp.mean(values, axis=-1, keepdims=True)]
    another operation x3 -> x0, other arithmetic: 11.3 us -> none  [the longest x2 9.41 us: local(): jnp.stack(input_grads)]
    convert_element_type x4 -> x0, other arithmetic: 6.83 us -> none  [the longest x2 6.05 us: local(): grad_branch = grad_first.astype(LOW)]
where the time goes in v4:
time: 537 us; the launch traced here: 533 us
  Pallas kernels  515 us (96%)
  local copies, waits for them, and re-layouts  10.1 us (2%)
  other arithmetic  6.94 us (1%)
    pallas_call x6, Pallas kernels, call_with_moves(): pl.pallas_call(kernel, grid=grid, in_specs=list(in_specs) + [anywhere] *...  393 us
    pallas_call x1, Pallas kernels, reduce_everywhere(): pl.pallas_call(functools.partial(reduce_kernel, orders=orders, width=widt...  90.7 us
    pallas_call x1, Pallas kernels, finish(): pl.pallas_call(functools.partial(finish_kernel, micro_count=micro_count,...  13.1 us
    pallas_call x2, Pallas kernels, join(): pl.pallas_call(kernel, grid=(tiles,), in_specs=[pl.BlockSpec(tuple(shape)...  12.3 us

profile of v4, /device:TPU:0, one launch (start us, length us, event | category | flops | bytes accessed | tf_op | source)
XLA Modules:
  0.0 533.5 jit_solution(10623259650770488246)
XLA Ops:
  0.6 1.3 broadcast_in_dim.19.refs_1_.refs_2_
  1.9 1.3 broadcast_in_dim.20.refs_6_.refs_7_
  3.2 1.3 broadcast_in_dim.18.refs_10_.refs_11_.refs_1_
  4.5 0.7 compare_select_fusion
  5.2 0.6 broadcast_in_dim.17.slot_ref.refs_9_.refs_10_.refs_0_
  5.8 1.6 copy.27.refs_7_.refs_8_
  7.4 6.7 %dispatch.1 = (bf16[1024,768]{1,0:T(8,128)(2,1)}, bf16[1024,768]{1,0:T(8,128)(2,1)}) custom-call(s32[2,1,1024]{2,1,0:T(1,128)} %broadcast_in_dim.17.slot_ref.refs_9_.refs_10_.refs_0_, bf16[2,1024,768]{2,1,0:T(8,128)(2,1)} %refs_1_.3), custom_call_target="tpu_custom_call" | custom-call | flops 3000000000 | bytes 6291456 | tf_op jit(solution)/shard_map/dispatch/pallas_call | solution.py:560
  14.1 51.2 %forward_stage.2 = (bf16[1024,768]{1,0:T(8,128)(2,1)}, bf16[1024,768]{1,0:T(8,128)(2,1)}, bf16[1024,768]{1,0:T(8,128)(2,1)}, bf16[12,1024,1024]{2,1,0:T(8,128)(2...) custom-call(bf16[2,1024,768]{2,1,0:T(8,128)(2,1)} %refs_0_.7, ...), custom_call_target="tpu_custom_call" | custom-call | flops 30000001024 | bytes 52428800 | tf_op jit(solution)/shard_map/forward_stage/pallas_call | solution.py:185
  65.3 81.8 %forward_stage.3 = (bf16[1024,768]{1,0:T(8,128)(2,1)}, bf16[1024,768]{1,0:T(8,128)(2,1)}, bf16[1024,768]{1,0:T(8,128)(2,1)}, bf16[12,1024,1024]{2,1,0:T(8,128)(2...) custom-call(bf16[2,1024,768]{2,1,0:T(8,128)(2,1)} %refs_0_.7, ...), custom_call_target="tpu_custom_call" | custom-call | flops 30000001024 | bytes 52428800 | tf_op jit(solution)/shard_map/forward_stage/pallas_call | solution.py:185
  147.2 46.9 %expert_stage.2 = (bf16[1024,768]{1,0:T(8,128)(2,1)}, bf16[1024,768]{1,0:T(8,128)(2,1)}, f32[16,8,128]{2,1,0:T(8,128)}, f32[6,768,512]{2,1,0:T(8,128)}, f32[6,51...) custom-call(bf16[1024,768]{1,0:T(8,128)(2,1)} %bitcast.39, bf16[1024,768]{1,0:T(8,128)(2,1)} %bitcast.32, ...), custom_call_target="tpu_custom_call" | custom-call | flops 28991029248 | bytes 35651584 | tf_op jit(solution)/shard_map/expert_stage/pallas_call | solution.py:185
  194.1 48.7 %expert_stage.3 = (bf16[1024,768]{1,0:T(8,128)(2,1)}, bf16[1024,768]{1,0:T(8,128)(2,1)}, f32[16,8,128]{2,1,0:T(8,128)}, f32[768,1536]{1,0:T(8,128)}, f32[1536,76...) custom-call(bf16[1024,768]{1,0:T(8,128)(2,1)} %bitcast.41, ...), custom_call_target="tpu_custom_call" | custom-call | flops 28991029248 | bytes 35651584 | tf_op jit(solution)/shard_map/expert_stage/pallas_call | solution.py:185
  242.8 97.4 %backward_stage.2 = (bf16[768,768]{1,0:T(8,128)(2,1)}, bf16[768,768]{1,0:T(8,128)(2,1)}, bf16[768,768]{1,0:T(8,128)(2,1)}, bf16[768,768]{1,0:T(8,128)(2,1)}, bf1...) custom-call(bf16[2,1024,768]{2,1,0:T(8,128)(2,1)} %refs_0_.7, ...), custom_call_target="tpu_custom_call" | custom-call | flops 40000000000 | bytes 52428800 | tf_op jit(solution)/shard_map/backward_stage/pallas_call | solution.py:185
  340.2 6.2 %join.2 = f32[1,768,1536]{2,1,0:T(8,128)} custom-call(f32[768,1536]{1,0:T(8,128)} %get-tuple-element.152.own_ref, bf16[1,768,512]{2,1,0:T(8,128)(2,1)} %get-tuple-element.153.rest_0_, bf16[1,768,512]{2,1,0:T(8,128)(2,1)} %get-tuple-element.154.rest_1_, bf16[1,768,512]{2,1,0:T(8,128)(2,1)} %get-tuple-element.155.rest_2_), custom_call_target="tpu_custom_call" | custom-call | flops 10000000 | bytes 12582912 | tf_op jit(solution)/shard_map/join/pallas_call | solution.py:419
  346.3 66.6 %backward_stage.3 = (bf16[768,768]{1,0:T(8,128)(2,1)}, bf16[768,768]{1,0:T(8,128)(2,1)}, bf16[768,768]{1,0:T(8,128)(2,1)}, bf16[768,768]{1,0:T(8,128)(2,1)}, bf1...) custom-call(bf16[2,1024,768]{2,1,0:T(8,128)(2,1)} %refs_0_.7, ...), custom_call_target="tpu_custom_call" | custom-call | flops 40000000000 | bytes 52428800 | tf_op jit(solution)/shard_map/backward_stage/pallas_call | solution.py:185
  413.0 6.2 %join.3 = f32[1,1536,768]{2,1,0:T(8,128)} custom-call(f32[1536,768]{1,0:T(8,128)} %get-tuple-element.156.own_ref, bf16[1,512,768]{2,1,0:T(8,128)(2,1)} %get-tuple-element.157.rest_0_, bf16[1,512,768]{2,1,0:T(8,128)(2,1)} %get-tuple-element.158.rest_1_, bf16[1,512,768]{2,1,0:T(8,128)(2,1)} %get-tuple-element.159.rest_2_), custom_call_target="tpu_custom_call" | custom-call | flops 10000000 | bytes 12582912 | tf_op jit(solution)/shard_map/join/pallas_call | solution.py:419
  419.1 13.1 %finish.1 = (bf16[2,1024,768]{2,1,0:T(8,128)(2,1)}, bf16[2,1024,768]{2,1,0:T(8,128)(2,1)}) custom-call(s32[2,1,1024]{2,1,0:T(1,128)} %broadcast_in_dim.17.slot_ref.refs_9_.refs_10_.refs_0_, s32[2,1,1024]{2,1,0:T(1,128)} %broadcast_in_dim.18.refs_10_.refs_11_.refs_1_, f32[16,16]{1,0:T(8,128)} %refs_2_.5, f32[1024,768]{1,0:T(8,128)} %get-tuple-element.87.refs_12_.refs_3_, ...), custom_call_target="tpu_custom_call" | custom-call | flops 3000000000 | bytes 18874368 | tf_op jit(solution)/shard_map/finish/pallas_call | solution.py:798
  432.2 90.7 %reduce_everywhere.1 = (bf16[768,3072]{1,0:T(8,128)(2,1)}, f32[24,896]{1,0:T(8,128)}) custom-call(bf16[768,768]{1,0:T(8,128)(2,1)} %get-tuple-element.140.refs_0_, bf16[768,768]{1,0:T(8,128)(2,1)} %get-tuple-element.141.refs_1_, bf16[768,768]{1,0:T(8,128)(2,1)} %get-tuple-element.142.refs_2_, bf16[768,768]{1,0:T(8,128)(2,1)} %get-tuple-element.143.refs_3_, ...), custom_call_target="tpu_custom_call" | custom-call | flops 1000000000 | bytes 20971520 | tf_op jit(solution)/shard_map/reduce_everywhere/pallas_call | solution.py:374
  522.9 1.3 slice.31
  524.2 1.4 slice_reduce_fusion
  525.6 1.4 slice_bitcast_fusion
  527.0 6.2 %slice_convert_fusion = (f32[768,768]{1,0:T(8,128)}, f32[768,768]{1,0:T(8,128)}, f32[768,768]{1,0:T(8,128)}, f32[768,768]{1,0:T(8,128)}) fusion(bf16[768,3072]{1,0:T(8,128)(2,1)} %get-tuple-element.151), kind=kLoop, calls=%fused_computation | loop fusion | flops 2359296 | bytes 14155776 | tf_op jit(solution)/shard_map/convert_element_type | solution.py:1074

commit v5 on v4

--- a/solution.py
+++ b/solution.py
@@ -39,6 +39,16 @@
     )
 
 
+def by_rows(count, size, body, carry=None):
+    return lax.fori_loop(
+        0, count // size, lambda i, c: body(pl.ds(pl.multiple_of(i * size, size), size), c), carry, unroll=2
+    )
+
+
+def fold_rows(values):
+    return jnp.sum(values.reshape(values.shape[0] // 8, 8, values.shape[1]), axis=0)
+
+
 def three_parts(values):
     high = values.astype(LOW)
     rest = values - high.astype(F32)
@@ -80,6 +90,11 @@
     picked = route_column == lane
     gate = jnp.sum(jnp.where(picked, probs, 0.0), axis=-1, keepdims=True)
     return unit, inverse, anchor, anchor_inverse, probs, picked, gate
+
+
+def slot_line(m, route_ref, slot_ref, keep_ref, slot_cap):
+    line = slice(m, m + 1)
+    return jnp.where(keep_ref[line, :] > 0, route_ref[line, :] * slot_cap + slot_ref[line, :], -1)
 
 
 def slot_rows(slot_row, first, count):
@@ -216,7 +231,7 @@
         core + x_bits + narrow + z_bits,
         core + narrow + x_bits + z_bits,
         core + z_bits + x_bits + narrow,
-    )
+    ) * 2
 
 
 def halvings(order, rows, columns):
@@ -394,41 +409,6 @@
     )(*(array for group in big for array in group), *small)
 
 
-def join_kernel(own_ref, far_ref, out_ref):
-    value = own_ref[...]
-    for j in range(far_ref.shape[0]):
-        value += far_ref[j].astype(F32)
-    out_ref[0] = value
-
-
-def join(own, fars, along):
-    tiles = len(fars)
-    spread = fars[0].shape[0]
-    shape = list(own.shape)
-    shape[along] //= tiles
-
-    def kernel(own_ref, *rest):
-        far_refs, out_ref = rest[:tiles], rest[tiles]
-        for t in range(tiles):
-
-            @pl.when(pl.program_id(0) == t)
-            def _():
-                join_kernel(own_ref, far_refs[t], out_ref)
-
-    place = (lambda t: (0, t)) if along == 1 else (lambda t: (t, 0))
-    return pl.pallas_call(
-        kernel,
-        grid=(tiles,),
-        in_specs=[pl.BlockSpec(tuple(shape), place)]
-        + [pl.BlockSpec((spread, *shape), lambda t: (0, 0, 0), pipeline_mode=pl.Buffered(1))] * tiles,
-        out_specs=pl.BlockSpec((1, *shape), lambda t: (0, *place(t))),
-        out_shape=jax.ShapeDtypeStruct((1, *own.shape), F32),
-        compiler_params=pltpu.CompilerParams(vmem_limit_bytes=VMEM_BYTES),
-        cost_estimate=pl.CostEstimate(flops=10**7, bytes_accessed=12 * 2**20, transcendentals=0),
-        name="join",
-    )(own, *fars)
-
-
 def attend_pair(query, keys, values, soft_ref, place, rows):
     lane = lax.broadcasted_iota(jnp.int32, (1, PAIR), 1)
     none = jnp.zeros_like(keys)
@@ -454,17 +434,24 @@
 
 
 def forward_kernel(
-    tokens_ref, gain_one_ref, wq_ref, wk_ref, wv_ref, wo_ref, gain_two_ref, route_ref, embed_ref, slot_ref, id_ref,
-    q_ref, k_ref, v_ref, soft_ref, inv_ref, mixed_ref, first_ref, sent_ref, gates_ref, projected_ref,
-    normed, total, *, steps, slots, slot_cap,
+    tokens_ref, gain_one_ref, wq_ref, wk_ref, wv_ref, wo_ref, gain_two_ref, route_ref, embed_ref, *refs,
+    m, steps, slots, slot_cap,
 ):
+    ids_ref, slot_ids_ref, keep_ref = refs[:3]
+    q_ref, k_ref, v_ref, soft_ref, inv_ref, mixed_ref, first_ref, sent_ref, gates_ref, projected_ref, normed = refs[3:]
     step = pl.program_id(0)
+    height = tokens_ref.shape[0]
 
     @pl.when(step == 0)
     def _():
-        values = tokens_ref[...].astype(F32)
-        normed[...] = (normalise(values)[0] * gain_one_ref[...]).astype(LOW)
-        total[...] = values
+        gain = gain_one_ref[...]
+
+        def body(rows, _):
+            values = tokens_ref[rows, :].astype(F32)
+            normed[rows, :] = (normalise(values)[0] * gain).astype(LOW)
+            first_ref[rows, :] = values
+
+        by_rows(height, 32, body)
 
     rows = normed[...]
     q_ref[...] = dot(rows, wq_ref[...]).astype(LOW)
@@ -475,19 +462,23 @@
         mixed, inverse = attend_pair(q_ref[:, lanes], k_ref[:, lanes], v_ref[:, lanes], soft_ref, 2 * pair, 512)
         mixed_ref[:, lanes] = mixed.astype(LOW)
         inv_ref[:, lanes] = inverse
-    total[...] += dot(mixed_ref[...], wo_ref[...])
+    first_ref[...] += dot(mixed_ref[...], wo_ref[...])
 
     @pl.when(step == steps - 1)
     def _():
-        first = total[...]
-        first_ref[...] = first
-        second = (normalise(first)[0] * gain_two_ref[...]).astype(LOW)
-        projected = dot(second, route_ref[...])
+        gain = gain_two_ref[...]
+
+        def body(rows, _):
+            normed[rows, :] = (normalise(first_ref[rows, :])[0] * gain).astype(LOW)
+
+        by_rows(height, 32, body)
+        second = normed[...]
+        projected = dot(second, route_ref[...], NT)
         projected_ref[...] = projected
-        route_column = to_column(id_ref[...].astype(F32)).astype(jnp.int32)
+        route_column = to_column(ids_ref[m : m + 1, :].astype(F32)).astype(jnp.int32)
         gate = route_probs(projected, embed_ref[...], route_column)[-1]
         parts = spread_parts(gate)
-        slot_row = slot_ref[...]
+        slot_row = slot_line(m, ids_ref, slot_ids_ref, keep_ref, slot_cap)
         block = 256
         for begin in range(0, slots, block):
             table = slot_rows(slot_row, begin, block)
@@ -499,7 +490,7 @@
                 gates_ref[w] = jnp.broadcast_to(row, (8, 128))
 
 
-def forward_stage(m, tokens, gains, weights, w_route, embed, slot_index, route_ids, slot_cap, moves, pushes, cid):
+def forward_stage(m, tokens, gains, weights, w_route, embed, ids, slot_cap, moves, pushes, cid):
     tok_count, width = tokens.shape[1:]
     experts = embed.shape[0]
     slots = experts * slot_cap
@@ -515,7 +506,7 @@
     low = lambda *shape: jax.ShapeDtypeStruct(shape, LOW)
     full = lambda *shape: jax.ShapeDtypeStruct(shape, F32)
     return call_with_moves(
-        functools.partial(forward_kernel, steps=steps, slots=slots, slot_cap=slot_cap),
+        functools.partial(forward_kernel, m=m, steps=steps, slots=slots, slot_cap=slot_cap),
         moves,
         pushes,
         cid,
@@ -523,53 +514,53 @@
         in_specs=[
             of_m(tok_count, width), fixed((1, width)), columns(width), columns(width), columns(width),
             pl.BlockSpec((span, width), lambda i: (i, 0)), fixed((1, width)), fixed(w_route.shape),
-            fixed(embed.shape), of_m(1, tok_count), of_m(1, tok_count),
-        ],
+            fixed(embed.shape),
+        ]
+        + [fixed(ids[0].shape)] * 3,
         out_specs=[
             columns(tok_count), columns(tok_count), columns(tok_count),
             pl.BlockSpec((GROUP, LENGTH, LENGTH), lambda i: (i, 0, 0)),
             columns(tok_count), columns(tok_count), whole(tok_count, width), whole(slots, width),
-            whole(experts, 8, 128), whole(tok_count, w_route.shape[1]),
+            whole(experts, 8, 128), whole(tok_count, w_route.shape[0]),
         ],
         out_shape=[
             low(tok_count, width), low(tok_count, width), low(tok_count, width), low(HEADS, LENGTH, LENGTH),
             full(tok_count, width), low(tok_count, width), full(tok_count, width), low(slots, width),
-            full(experts, 8, 128), full(tok_count, w_route.shape[1]),
+            full(experts, 8, 128), full(tok_count, w_route.shape[0]),
         ],
-        scratch_shapes=[pltpu.VMEM((tok_count, width), LOW), pltpu.VMEM((tok_count, width), F32)],
+        scratch_shapes=[pltpu.VMEM((tok_count, width), LOW)],
         cost=pl.CostEstimate(
             flops=30 * 10**9, bytes_accessed=50 * 2**20, transcendentals=HEADS * LENGTH * LENGTH
         ),
         name="forward_stage",
-        args=(tokens, gain_one, wq, wk, wv, wo, gain_two, w_route, embed, slot_index, route_ids),
-    )
-
-
-def dispatch_kernel(slot_ref, rows_ref, *out_refs, slots):
+        args=(tokens, gain_one, wq, wk, wv, wo, gain_two, w_route, embed, *ids),
+    )
+
+
+def dispatch_kernel(ids_ref, slot_ids_ref, keep_ref, rows_ref, *out_refs, slots, slot_cap):
     for m, out_ref in enumerate(out_refs):
 
         @pl.when(pl.program_id(0) == m)
         def _():
+            slot_row = slot_line(m, ids_ref, slot_ids_ref, keep_ref, slot_cap)
             for begin in range(0, slots, 256):
-                table = slot_rows(slot_ref[...], begin, 256)
+                table = slot_rows(slot_row, begin, 256)
                 out_ref[begin : begin + 256, :] = dot(table, rows_ref[...]).astype(LOW)
 
 
-def dispatch(slot_index, rows, slots):
+def dispatch(ids, rows, slots, slot_cap):
     micro_count, tok_count, width = rows.shape
     return pl.pallas_call(
-        functools.partial(dispatch_kernel, slots=slots),
+        functools.partial(dispatch_kernel, slots=slots, slot_cap=slot_cap),
         grid=(micro_count,),
-        in_specs=[
-            pl.BlockSpec((None, 1, tok_count), lambda m: (m, 0, 0)),
-            pl.BlockSpec((None, tok_count, width), lambda m: (m, 0, 0)),
-        ],
+        in_specs=[pl.BlockSpec(ids[0].shape, lambda m: (0, 0))] * 3
+        + [pl.BlockSpec((None, tok_count, width), lambda m: (m, 0, 0))],
         out_specs=[pl.BlockSpec((slots, width), lambda m: (0, 0))] * micro_count,
         out_shape=[jax.ShapeDtypeStruct((slots, width), LOW)] * micro_count,
         compiler_params=pltpu.CompilerParams(vmem_limit_bytes=VMEM_BYTES),
         cost_estimate=pl.CostEstimate(flops=3 * 10**9, bytes_accessed=6 * 2**20, transcendentals=0),
         name="dispatch",
-    )(slot_index, rows)
+    )(*ids, rows)
 
 
 def attend_pair_back(query, keys, values, grad, mixed, soft_ref, place, inverses, rows):
@@ -607,14 +598,15 @@
 
 
 def backward_kernel(
-    tokens_ref, cot_ref, gain_one_ref, wq_ref, wk_ref, wv_ref, wo_ref, gain_two_ref, route_ref, embed_ref, slot_ref,
-    id_ref, first_ref, projected_ref, home_ref, dots_ref, q_ref, k_ref, v_ref, mixed_ref, soft_ref, inv_ref,
+    tokens_ref, cot_ref, gain_one_ref, wq_ref, wk_ref, wv_ref, wo_ref, gain_two_ref, route_ref, embed_ref,
+    ids_ref, slot_ids_ref, keep_ref, first_ref, projected_ref, home_ref, dots_ref,
+    q_ref, k_ref, v_ref, mixed_ref, soft_ref, inv_ref,
     dwq_ref, dwk_ref, dwv_ref, dwo_ref, gtok_ref, small_ref,
     grad_first, branch, normed_t, total, mixed_grad, dq_sc, dk_sc, dv_sc, soft_buf, soft_sem,
-    *, steps, slots, slot_cap,
+    *, m, steps, slots, slot_cap,
 ):
     step = pl.program_id(0)
-    width = tokens_ref.shape[1]
+    height, width = tokens_ref.shape
     experts, router_dim = embed_ref.shape
     pairs = GROUP // 2
 
@@ -625,10 +617,16 @@
     @pl.when(step == 0)
     def _():
         soft_pair(0).start()
-        normed_one = normalise(tokens_ref[...].astype(F32))[0]
-        normed_t[...] = (normed_one * gain_one_ref[...]).astype(LOW).T
-        slot_column = to_column(slot_ref[...].astype(F32)).astype(jnp.int32)
-        route_column = to_column(id_ref[...].astype(F32)).astype(jnp.int32)
+        gain_one, gain_two = gain_one_ref[...], gain_two_ref[...]
+
+        def ahead(rows, _):
+            branch[rows, :] = (normalise(tokens_ref[rows, :].astype(F32))[0] * gain_one).astype(LOW)
+
+        by_rows(height, 32, ahead)
+        normed_t[...] = branch[...].T
+        slot_row = slot_line(m, ids_ref, slot_ids_ref, keep_ref, slot_cap)
+        slot_column = to_column(slot_row.astype(F32)).astype(jnp.int32)
+        route_column = to_column(ids_ref[m : m + 1, :].astype(F32)).astype(jnp.int32)
         columns = [
             jnp.sum(jnp.where(diagonal(slot_cap), dots_ref[w, 0:1, :], 0.0), axis=1, keepdims=True)
             for w in range(experts)
@@ -636,7 +634,7 @@
         dots = spread_parts(jnp.concatenate(columns, axis=0))
         grads = []
         block = 256
-        for begin in range(0, slot_column.shape[0], block):
+        for begin in range(0, height, block):
             table = token_rows(slot_column[begin : begin + block, :], slots)
             grad_first[begin : begin + block, :] = dot(table, home_ref[...])
             grads.append(jnp.sum(dot(table, dots), axis=1, keepdims=True))
@@ -654,21 +652,30 @@
         term_embed = anchor_inverse * grad_anchor - anchor_inverse**3 * embed_rows * jnp.sum(
             embed_rows * grad_anchor, axis=-1, keepdims=True
         )
-        normed_two, inverse_two = normalise(first_ref[...])
-        second = (normed_two * gain_two_ref[...]).astype(LOW)
-        grad_second = grad_first[...]
-        term_route = None
-        for part in three_parts(grad_projected):
-            grad_second += dot(part, route_ref[...], NT)
-            term = dot(part, second, TN)
-            term_route = term if term_route is None else term_route + term
+        parts = three_parts(grad_projected)
+        for begin in range(0, height, block):
+            some = slice(begin, begin + block)
+            grad_first[some, :] += sum(dot(part[some, :], route_ref[...]) for part in parts)
+        thirds = (dq_sc, dk_sc, dv_sc)
+        third = width // 3
+
+        def middle(rows, gathered):
+            normed_two, inverse_two = normalise(first_ref[rows, :])
+            second = (normed_two * gain_two).astype(LOW)
+            for at, ref in enumerate(thirds):
+                ref[rows, :] = second[:, at * third : (at + 1) * third]
+            grad_second = grad_first[rows, :]
+            value = cot_ref[rows, :].astype(F32) + normalise_back(grad_second * gain_two, normed_two, inverse_two)
+            grad_first[rows, :] = value
+            branch[rows, :] = value.astype(LOW)
+            return gathered + fold_rows(grad_second * normed_two)
+
+        gathered = by_rows(height, 32, middle, jnp.zeros((8, width), F32))
         small_ref[...] = jnp.zeros_like(small_ref)
-        small_ref[0:router_dim, 0:width] = term_route
-        small_ref[router_dim + 1 : router_dim + 2, 0:width] = jnp.sum(grad_second * normed_two, axis=0, keepdims=True)
+        for at, ref in enumerate(thirds):
+            small_ref[0:router_dim, at * third : (at + 1) * third] = sum(dot(part, ref[...], TN) for part in parts)
+        small_ref[router_dim + 1 : router_dim + 2, 0:width] = jnp.sum(gathered, axis=0, keepdims=True)
         small_ref[0:experts, width : width + router_dim] = term_embed
-        value = cot_ref[...].astype(F32) + normalise_back(grad_second * gain_two_ref[...], normed_two, inverse_two)
-        grad_first[...] = value
-        branch[...] = value.astype(LOW)
         total[...] = jnp.zeros_like(total)
 
     rows = branch[...]
@@ -702,16 +709,21 @@
 
     @pl.when(step == steps - 1)
     def _():
-        normed_one, inverse_one = normalise(tokens_ref[...].astype(F32))
-        grad = total[...]
-        small_ref[router_dim : router_dim + 1, 0:width] = jnp.sum(grad * normed_one, axis=0, keepdims=True)
-        gtok_ref[...] = (
-            grad_first[...] + normalise_back(grad * gain_one_ref[...], normed_one, inverse_one)
-        ).astype(LOW)
+        gain_one = gain_one_ref[...]
+
+        def behind(rows, gathered):
+            normed_one, inverse_one = normalise(tokens_ref[rows, :].astype(F32))
+            grad = total[rows, :]
+            value = grad_first[rows, :] + normalise_back(grad * gain_one, normed_one, inverse_one)
+            gtok_ref[rows, :] = value.astype(LOW)
+            return gathered + fold_rows(grad * normed_one)
+
+        gathered = by_rows(height, 32, behind, jnp.zeros((8, width), F32))
+        small_ref[router_dim : router_dim + 1, 0:width] = jnp.sum(gathered, axis=0, keepdims=True)
 
 
 def backward_stage(
-    m, tokens, grad_out, gains, weights, w_route, embed, slot_index, route_ids, kept, home, slot_cap, moves, pushes, cid
+    m, tokens, grad_out, gains, weights, w_route, embed, ids, kept, home, slot_cap, moves, pushes, cid
 ):
     tok_count, width = tokens.shape[1:]
     experts, router_dim = embed.shape
@@ -729,15 +741,15 @@
     low = lambda *shape: jax.ShapeDtypeStruct(shape, LOW)
     small = (-(-max(experts, router_dim + 2) // 8) * 8, width + 128)
     return call_with_moves(
-        functools.partial(backward_kernel, steps=steps, slots=slots, slot_cap=slot_cap),
+        functools.partial(backward_kernel, m=m, steps=steps, slots=slots, slot_cap=slot_cap),
         moves,
         pushes,
         cid,
         grid=(steps,),
         in_specs=[
             of_m(tok_count, width), of_m(tok_count, width), fixed((1, width)), columns(width), columns(width),
-            columns(width), lines, fixed((1, width)), fixed(w_route.shape), fixed(embed.shape), of_m(1, tok_count),
-            of_m(1, tok_count), fixed(first.shape), fixed(projected.shape), fixed(home[0].shape), fixed(home[1].shape),
+            columns(width), lines, fixed((1, width)), fixed(w_route.shape), fixed(embed.shape),
+            *[fixed(ids[0].shape)] * 3, fixed(first.shape), fixed(projected.shape), fixed(home[0].shape), fixed(home[1].shape),
             columns(tok_count), columns(tok_count), columns(tok_count), columns(tok_count),
             pl.BlockSpec(memory_space=pl.ANY), columns(tok_count),
         ],
@@ -757,54 +769,99 @@
         cost=pl.CostEstimate(flops=40 * 10**9, bytes_accessed=50 * 2**20, transcendentals=0),
         name="backward_stage",
         args=(
-            tokens, grad_out, gain_one, wq, wk, wv, wo, gain_two, w_route, embed, slot_index, route_ids, first,
+            tokens, grad_out, gain_one, wq, wk, wv, wo, gain_two, w_route, embed, *ids, first,
             projected, *home, q, k, v, mixed, soft, inverses,
         ),
     )
 
 
-def finish_kernel(*refs, micro_count, slots):
-    slot_ref, id_ref, embed_ref = refs[:3]
-    ins, (out_ref, grad_ref) = refs[3:-2], refs[-2:]
+def finish_kernel(*refs, micro_count, blocks, slots, slot_cap, tiles, wide_steps, per_tile):
+    ids_ref, slot_ids_ref, keep_ref, embed_ref = refs[:4]
+    ins, refs = refs[4 : 4 + 4 * micro_count], refs[4 + 4 * micro_count :]
+    near_in, near_outer = refs[:2]
+    far_in, far_outer = refs[2 : 2 + tiles], refs[2 + tiles : 2 + 2 * tiles]
+    big_ref = refs[2 + 2 * tiles]
+    out_ref, grad_ref, din_ref, douter_ref, *big_outs = refs[3 + 2 * tiles :]
+    step = pl.program_id(0)
+    rows, width = out_ref.shape
     for m in range(micro_count):
         first_ref, projected_ref, home_ref, gtok_ref = ins[4 * m : 4 * m + 4]
-
-        @pl.when(pl.program_id(0) == m)
+        for block in range(blocks):
+
+            @pl.when(step == m * blocks + block)
+            def _():
+                some = slice(block * rows, (block + 1) * rows)
+                slot_row = slot_line(m, ids_ref, slot_ids_ref, keep_ref, slot_cap)
+                slot_column = to_column(slot_row[:, some].astype(F32)).astype(jnp.int32)
+                route_column = to_column(ids_ref[m : m + 1, some].astype(F32)).astype(jnp.int32)
+                gate = route_probs(projected_ref[...], embed_ref[...], route_column)[-1]
+                returned = dot(token_rows(slot_column, slots), home_ref[...])
+                out_ref[...] = (first_ref[...] + gate * returned).astype(LOW)
+                grad_ref[...] = gtok_ref[...]
+
+    for t in range(tiles):
+
+        @pl.when((step >= t * per_tile) & (step < (t + 1) * per_tile))
         def _():
-            slot_column = to_column(slot_ref[...].astype(F32)).astype(jnp.int32)
-            route_column = to_column(id_ref[...].astype(F32)).astype(jnp.int32)
-            gate = route_probs(projected_ref[...], embed_ref[...], route_column)[-1]
-            returned = dot(token_rows(slot_column, slots), home_ref[...])
-            out_ref[...] = (first_ref[...] + gate * returned).astype(LOW)
-            grad_ref[...] = gtok_ref[...]
-
-
-def finish(slot_index, route_ids, embed, parts, slots):
-    micro_count, _, tok_count = slot_index.shape
+            din_ref[0] = near_in[...] + sum(far_in[t][j].astype(F32) for j in range(far_in[t].shape[0]))
+            douter_ref[0] = near_outer[...] + sum(far_outer[t][j].astype(F32) for j in range(far_outer[t].shape[0]))
+
+    for k, big_out in enumerate(big_outs):
+        big_out[...] = big_ref[:, k * width : (k + 1) * width].astype(F32)
+
+
+def finish(ids, embed, parts, near, far, big, slots, slot_cap):
+    micro_count, tok_count = ids[0].shape
     width = parts[0][0].shape[1]
+    near_in, near_outer = near
+    tiles = len(far) // 2
+    spread, _, tile = far[0].shape
+    units = near_in.shape[1]
+    span = 256 if tile % 256 == 0 else 128
+    wide_steps, per_tile = units // span, tile // span
     rows = 256
     blocks = tok_count // rows
-    row = pl.BlockSpec((None, 1, rows), lambda m, i: (m, 0, i))
-    whole = lambda shape: pl.BlockSpec(shape, lambda m, i: (0, 0))
-    in_specs, args = [row, row, whole(embed.shape)], [slot_index, route_ids, embed]
+    steps = micro_count * blocks
+    lines = big.shape[0] // steps
+    whole = lambda shape: pl.BlockSpec(shape, lambda i: (0, 0), pipeline_mode=pl.Buffered(1))
+    in_specs, args = [whole(ids[0].shape)] * 3 + [whole(embed.shape)], [*ids, embed]
     for at, (first, projected, home, gtok) in enumerate(parts):
-        place = lambda m, i, at=at: (jnp.where(m == at, i, jnp.where(m < at, 0, blocks - 1)), 0)
+        place = lambda i, at=at: (jnp.clip(i - at * blocks, 0, blocks - 1), 0)
         in_specs += [
             pl.BlockSpec((rows, width), place), pl.BlockSpec((rows, projected.shape[1]), place), whole(home.shape),
             pl.BlockSpec((rows, width), place),
         ]
         args += [first, projected, home, gtok]
-    out = pl.BlockSpec((None, rows, width), lambda m, i: (m, i, 0))
+    near_at = lambda i: jnp.minimum(i, wide_steps - 1)
+    far_at = lambda i, t: jnp.clip(i - t * per_tile, 0, per_tile - 1)
+    in_specs += [
+        pl.BlockSpec((width, span), lambda i: (0, near_at(i))), pl.BlockSpec((span, width), lambda i: (near_at(i), 0)),
+    ]
+    in_specs += [pl.BlockSpec((spread, width, span), lambda i, t=t: (0, 0, far_at(i, t))) for t in range(tiles)]
+    in_specs += [pl.BlockSpec((spread, span, width), lambda i, t=t: (0, far_at(i, t), 0)) for t in range(tiles)]
+    in_specs += [pl.BlockSpec((lines, big.shape[1]), lambda i: (i, 0))]
+    row_out = pl.BlockSpec((None, rows, width), lambda i: (i // blocks, i % blocks, 0))
+    line_out = pl.BlockSpec((lines, width), lambda i: (i, 0))
+    kinds = big.shape[1] // width
     return pl.pallas_call(
-        functools.partial(finish_kernel, micro_count=micro_count, slots=slots),
-        grid=(micro_count, blocks),
+        functools.partial(
+            finish_kernel, micro_count=micro_count, blocks=blocks, slots=slots, slot_cap=slot_cap, tiles=tiles,
+            wide_steps=wide_steps, per_tile=per_tile,
+        ),
+        grid=(steps,),
         in_specs=in_specs,
-        out_specs=[out, out],
-        out_shape=[jax.ShapeDtypeStruct((micro_count, tok_count, width), LOW)] * 2,
+        out_specs=[
+            row_out, row_out, pl.BlockSpec((1, width, span), lambda i: (0, 0, near_at(i))),
+            pl.BlockSpec((1, span, width), lambda i: (0, near_at(i), 0)),
+        ]
+        + [line_out] * kinds,
+        out_shape=[jax.ShapeDtypeStruct((micro_count, tok_count, width), LOW)] * 2
+        + [jax.ShapeDtypeStruct((1, *near_in.shape), F32), jax.ShapeDtypeStruct((1, *near_outer.shape), F32)]
+        + [jax.ShapeDtypeStruct((big.shape[0], width), F32)] * kinds,
         compiler_params=pltpu.CompilerParams(vmem_limit_bytes=VMEM_BYTES),
-        cost_estimate=pl.CostEstimate(flops=3 * 10**9, bytes_accessed=18 * 2**20, transcendentals=0),
+        cost_estimate=pl.CostEstimate(flops=3 * 10**9, bytes_accessed=56 * 2**20, transcendentals=0),
         name="finish",
-    )(*args)
+    )(*args, near_in, near_outer, *far, big)
 
 
 def gelu_and_slope(values):
@@ -1013,11 +1070,10 @@
         (own_outer, lambda ref, j, t=t: ref.at[t * tile : (t + 1) * tile, :], (tile, feat_width)) for t in range(per)
     ]
     early = len(weight_pushes) // 3
-    slot_index = jnp.where(keep_ids > 0, route_ids * slot_cap + slot_ids, -1)[:, None, :]
-    route_rows = route_ids[:, None, :]
     gains = (gain_one[None], gain_two[None])
     mixers = (w_query, w_key, w_value, w_out)
-    router = (w_route, embed, slot_index, route_rows)
+    ids = (route_ids, slot_ids, keep_ids)
+    router = (w_route.T, embed, ids)
 
     def boxes(rows):
         return rows.reshape((expert_count, slot_cap) + rows.shape[1:])
@@ -1025,7 +1081,7 @@
     def flat(boxed):
         return boxed.reshape((expert_count * slot_cap,) + boxed.shape[2:])
 
-    cot_boxes = [boxes(rows) for rows in dispatch(slot_index, grad_out, slots)]
+    cot_boxes = [boxes(rows) for rows in dispatch(ids, grad_out, slots, slot_cap)]
     (*ahead_0, sent, gates, projected), (cot_0,), far_a = forward_stage(
         0, tokens, gains, mixers, *router, slot_cap, (cot_boxes[0],), weight_pushes[:early], 1
     )
@@ -1048,7 +1104,7 @@
     ] + [
         (far_douter, lambda ref, j, t=t: ref.at[j * per + t], (tile, feat_width)) for t in range(per)
     ]
-    later = len(grad_pushes) - early
+    later = len(grad_pushes) // 2
 
     def kept(ahead):
         q, k, v, soft, inverses, mixed, first, projected = ahead
@@ -1062,18 +1118,16 @@
         1, tokens, grad_out, gains, mixers, *router, kept(ahead_1), (flat(home_grad_1), home_dots_1), slot_cap,
         (boxes(result_0), boxes(result_1)), grad_pushes[later:], 6
     )
-    block_out, grad_tokens = finish(
-        slot_index, route_rows, embed,
+    big, small = reduce_everywhere(list(zip(big_0, big_1)), (small_0, small_1), 7)
+    block_out, grad_tokens, grad_in, grad_outer, *big = finish(
+        ids, embed,
         (
             (ahead_0[6], ahead_0[7], flat(home_result_0), gtok_0),
             (ahead_1[6], ahead_1[7], flat(home_result_1), gtok_1),
         ),
-        slots,
-    )
-    big, small = reduce_everywhere(list(zip(big_0, big_1)), (small_0, small_1), 7)
-    big = [big[:, k * feat_width : (k + 1) * feat_width].astype(F32) for k in range(4)]
+        (near_din, near_douter), [*got_a, *got_b], big, slots, slot_cap,
+    )
     router_dim = w_route.shape[1]
-    got = [*got_a, *got_b]
     return (
         block_out,
         grad_tokens,
@@ -1082,8 +1136,8 @@
         small[router_dim + 1, :feat_width],
         small[:router_dim, :feat_width].T,
         small[:expert_count, feat_width : feat_width + router_dim],
-        join(near_din, got[:per], 1),
-        join(near_douter, got[per:], 0),
+        grad_in,
+        grad_outer,
     )
 
 

time: 537 us -> 502 us (0.935)
  Pallas kernels: 515 us -> 494 us
  other arithmetic: 6.94 us -> 0 us
  local copies, waits for them, and re-layouts: 10.1 us -> 4.38 us
    pallas_call x3 -> x1, Pallas kernels: 19 us -> 6.69 us  [dispatch(): pl.pallas_call(functools.partial(dispatch_kernel, slots=slots, slot_cap=s...]
    pallas_call x6, Pallas kernels: 393 us -> 382 us  [call_with_moves(): pl.pallas_call(kernel, grid=grid, in_specs=list(in_specs) + [anywhere] *...]
    pallas_call x1, Pallas kernels: 13.1 us -> 22.3 us  [finish(): pl.pallas_call(functools.partial(finish_kernel, micro_count=micro_count,...]
    pallas_call x1, Pallas kernels: 90.7 us -> 82.3 us  [reduce_everywhere(): pl.pallas_call(functools.partial(reduce_kernel, orders=orders, width=widt...]
    convert_element_type x1 -> x0, other arithmetic: 6.2 us -> none  [local(): big[:, k * feat_width:(k + 1) * feat_width].astype(F32)]
where the time goes in v5:
time: 502 us; the launch traced here: 499 us
  Pallas kernels  494 us (98%)
    pallas_call x6, Pallas kernels, call_with_moves(): pl.pallas_call(kernel, grid=grid, in_specs=list(in_specs) + [anywhere] *...  382 us
    pallas_call x1, Pallas kernels, reduce_everywhere(): pl.pallas_call(functools.partial(reduce_kernel, orders=orders, width=widt...  82.3 us
    pallas_call x1, Pallas kernels, finish(): pl.pallas_call(functools.partial(finish_kernel, micro_count=micro_count,...  22.3 us

profile of v5, /device:TPU:0, one launch (start us, length us, event | category | flops | bytes accessed | tf_op | source)
XLA Modules:
  0.0 499.1 jit_solution(11023703019045058256)
XLA Ops:
  0.6 1.3 broadcast_in_dim.6.refs_1_.refs_2_
  1.9 1.3 broadcast_in_dim.7.refs_6_.refs_7_
  3.2 6.7 %dispatch.1 = (bf16[1024,768]{1,0:T(8,128)(2,1)}, bf16[1024,768]{1,0:T(8,128)(2,1)}) custom-call(s32[2,1024]{1,0:T(2,128)} %refs_0_.9, s32[2,1024]{1,0:T(2,128)} %refs_1_.5, s32[2,1024]{1,0:T(2,128)} %refs_2_.5, bf16[2,1024,768]{2,1,0:T(8,128)(2,1)} %refs_1_.4), custom_call_target="tpu_custom_call" | custom-call | flops 3000000000 | bytes 6291456 | tf_op jit(solution)/shard_map/dispatch/pallas_call | solution.py:553
  9.9 51.2 %forward_stage.2 = (bf16[1024,768]{1,0:T(8,128)(2,1)}, bf16[1024,768]{1,0:T(8,128)(2,1)}, bf16[1024,768]{1,0:T(8,128)(2,1)}, bf16[12,1024,1024]{2,1,0:T(8,128)(2...) custom-call(bf16[2,1024,768]{2,1,0:T(8,128)(2,1)} %refs_0_.8, ...), custom_call_target="tpu_custom_call" | custom-call | flops 30000001024 | bytes 52428800 | tf_op jit(solution)/shard_map/forward_stage/pallas_call | solution.py:200
  61.1 81.8 %forward_stage.3 = (bf16[1024,768]{1,0:T(8,128)(2,1)}, bf16[1024,768]{1,0:T(8,128)(2,1)}, bf16[1024,768]{1,0:T(8,128)(2,1)}, bf16[12,1024,1024]{2,1,0:T(8,128)(2...) custom-call(bf16[2,1024,768]{2,1,0:T(8,128)(2,1)} %refs_0_.8, ...), custom_call_target="tpu_custom_call" | custom-call | flops 30000001024 | bytes 52428800 | tf_op jit(solution)/shard_map/forward_stage/pallas_call | solution.py:200
  142.9 46.9 %expert_stage.2 = (bf16[1024,768]{1,0:T(8,128)(2,1)}, bf16[1024,768]{1,0:T(8,128)(2,1)}, f32[16,8,128]{2,1,0:T(8,128)}, f32[6,768,512]{2,1,0:T(8,128)}, f32[6,51...) custom-call(bf16[1024,768]{1,0:T(8,128)(2,1)} %bitcast.44, bf16[1024,768]{1,0:T(8,128)(2,1)} %bitcast.37, ...), custom_call_target="tpu_custom_call" | custom-call | flops 28991029248 | bytes 35651584 | tf_op jit(solution)/shard_map/expert_stage/pallas_call | solution.py:200
  189.8 48.6 %expert_stage.3 = (bf16[1024,768]{1,0:T(8,128)(2,1)}, bf16[1024,768]{1,0:T(8,128)(2,1)}, f32[16,8,128]{2,1,0:T(8,128)}, f32[768,1536]{1,0:T(8,128)}, f32[1536,76...) custom-call(bf16[1024,768]{1,0:T(8,128)(2,1)} %bitcast.46, ...), custom_call_target="tpu_custom_call" | custom-call | flops 28991029248 | bytes 35651584 | tf_op jit(solution)/shard_map/expert_stage/pallas_call | solution.py:200
  238.4 84.1 %backward_stage.2 = (bf16[768,768]{1,0:T(8,128)(2,1)}, bf16[768,768]{1,0:T(8,128)(2,1)}, bf16[768,768]{1,0:T(8,128)(2,1)}, bf16[768,768]{1,0:T(8,128)(2,1)}, bf1...) custom-call(bf16[2,1024,768]{2,1,0:T(8,128)(2,1)} %refs_0_.8, ...), custom_call_target="tpu_custom_call" | custom-call | flops 40000000000 | bytes 52428800 | tf_op jit(solution)/shard_map/backward_stage/pallas_call | solution.py:200
  322.5 69.9 %backward_stage.3 = (bf16[768,768]{1,0:T(8,128)(2,1)}, bf16[768,768]{1,0:T(8,128)(2,1)}, bf16[768,768]{1,0:T(8,128)(2,1)}, bf16[768,768]{1,0:T(8,128)(2,1)}, bf1...) custom-call(bf16[2,1024,768]{2,1,0:T(8,128)(2,1)} %refs_0_.8, ...), custom_call_target="tpu_custom_call" | custom-call | flops 40000000000 | bytes 52428800 | tf_op jit(solution)/shard_map/backward_stage/pallas_call | solution.py:200
  392.3 82.3 %reduce_everywhere.1 = (bf16[768,3072]{1,0:T(8,128)(2,1)}, f32[24,896]{1,0:T(8,128)}) custom-call(bf16[768,768]{1,0:T(8,128)(2,1)} %get-tuple-element.152.refs_0_, bf16[768,768]{1,0:T(8,128)(2,1)} %get-tuple-element.153.refs_1_, bf16[768,768]{1,0:T(8,128)(2,1)} %get-tuple-element.154.refs_2_, bf16[768,768]{1,0:T(8,128)(2,1)} %get-tuple-element.155.refs_3_, ...), custom_call_target="tpu_custom_call" | custom-call | flops 1000000000 | bytes 20971520 | tf_op jit(solution)/shard_map/reduce_everywhere/pallas_call | solution.py:389
  474.7 0.0 copy-start
  474.7 22.3 %finish.1 = (bf16[2,1024,768]{2,1,0:T(8,128)(2,1)}, bf16[2,1024,768]{2,1,0:T(8,128)(2,1)}, f32[1,768,1536]{2,1,0:T(8,128)}, f32[1,1536,768]{2,1,0:T(8,128)}, f32...) custom-call(s32[2,1024]{1,0:T(2,128)} %refs_0_.9, s32[2,1024]{1,0:T(2,128)} %refs_1_.5, ...), custom_call_target="tpu_custom_call" | custom-call | flops 3000000000 | bytes 58720256 | tf_op jit(solution)/shard_map/finish/pallas_call | solution.py:846
  497.0 0.0 copy-done
  497.0 0.6 slice.15
  497.6 0.6 slice_reduce_fusion
  498.2 0.6 slice_bitcast_fusion
Async XLA Ops:
  474.7 22.3 %copy-start = (f32[24,896]{1,0:T(8,128)S(1)}, f32[24,896]{1,0:T(8,128)}, u32[]{:S(2)}) copy-start(f32[24,896]{1,0:T(8,128)} %get-tuple-element.165) | copy-start | bytes 258052

commit v6 on v5

--- a/solution.py
+++ b/solution.py
@@ -13,6 +13,7 @@
 LENGTH = 1024
 PAIR = 2 * HEAD_DIM
 GROUP = 4
+PIECES = 4
 NN = (((1,), (0,)), ((), ()))
 NT = (((1,), (1,)), ((), ()))
 TN = (((0,), (0,)), ((), ()))
@@ -41,7 +42,7 @@
 
 def by_rows(count, size, body, carry=None):
     return lax.fori_loop(
-        0, count // size, lambda i, c: body(pl.ds(pl.multiple_of(i * size, size), size), c), carry, unroll=2
+        0, count // size, lambda i, c: body(pl.ds(pl.multiple_of(i * size, size), size), c), carry
     )
 
 
@@ -97,6 +98,13 @@
     return jnp.where(keep_ref[line, :] > 0, route_ref[line, :] * slot_cap + slot_ref[line, :], -1)
 
 
+def piece_line(m, route_ref, slot_ref, keep_ref, low, high):
+    line = slice(m, m + 1)
+    slot = slot_ref[line, :]
+    inside = (keep_ref[line, :] > 0) & (slot >= low) & (slot < high)
+    return jnp.where(inside, route_ref[line, :] * (high - low) + slot - low, -1)
+
+
 def slot_rows(slot_row, first, count):
     slot = lax.broadcasted_iota(jnp.int32, (count, slot_row.shape[1]), 0) + first
     return jnp.where(slot == slot_row, 1.0, 0.0).astype(LOW)
@@ -111,7 +119,7 @@
 
 
 def call_with_moves(
-    body, moves, pushes, cid, *, grid, in_specs, out_specs, out_shape, scratch_shapes=(), cost, name, args
+    body, moves, pushes, cid, *, grid, in_specs, out_specs, out_shape, scratch_shapes=(), cost, name, args, late=False
 ):
     members, spread = lax.axis_size("wide"), lax.axis_size("narrow")
     n_in, n_out, n_moves, n_scratch = len(in_specs), len(out_specs), len(moves), len(scratch_shapes)
@@ -135,10 +143,13 @@
         me, side = lax.axis_index("wide"), lax.axis_index("narrow")
         step = pl.program_id(0)
 
+        def piece(i, w):
+            return sources[i].at[w, moves[i][1] : moves[i][2]]
+
         def remote(i, d):
             peer = lax.rem(me + d, members)
             return pltpu.make_async_remote_copy(
-                src_ref=sources[i].at[peer],
+                src_ref=piece(i, peer),
                 dst_ref=targets[i].at[me],
                 send_sem=send_sem.at[i, d],
                 recv_sem=recv_sem.at[i, d],
@@ -146,15 +157,22 @@
                 device_id_type=MESH,
             )
 
-        def push(k, j):
+        def push(k, j, part):
+            size = pushes[k][2][0] // PIECES
+            some = slice(part * size, (part + 1) * size)
             return pltpu.make_async_remote_copy(
-                src_ref=pushes[k][1](pushed[which[k]], j),
-                dst_ref=landings[k].at[j],
-                send_sem=push_send.at[k, j],
-                recv_sem=push_recv.at[k, j],
+                src_ref=pushes[k][1](pushed[which[k]], j).at[some],
+                dst_ref=landings[k].at[j].at[some],
+                send_sem=push_send.at[k, j * PIECES + part],
+                recv_sem=push_recv.at[k, j * PIECES + part],
                 device_id={"narrow": lax.rem(side + j + 1, spread)},
                 device_id_type=MESH,
             )
+
+        def settle(k):
+            for j in range(spread - 1):
+                for part in range(PIECES):
+                    push(k, j, part).wait()
 
         @pl.when(step == 0)
         def _():
@@ -173,28 +191,32 @@
                     )
                 count += spread - 1
             pl.semaphore_wait(barrier, count)
-            for k in range(n_pushes):
-                for j in range(spread - 1):
-                    push(k, j).start()
             for i in range(n_moves):
                 for d in range(1, members):
                     remote(i, d).start()
-                pltpu.make_async_copy(sources[i].at[me], stages[i], own_sem.at[i]).start()
-
-        body(*ins, *outs, *scratch)
+                pltpu.make_async_copy(piece(i, me), stages[i], own_sem.at[i]).start()
+            for k in range(n_pushes):
+                for j in range(spread - 1):
+                    for part in range(PIECES):
+                        push(k, j, part).start()
+
+        if late:
+            body(*ins, *outs, *scratch, landings=landings, settle=settle)
+        else:
+            body(*ins, *outs, *scratch)
 
         @pl.when(step == grid[0] - 1)
         def _():
             for i in range(n_moves):
-                pltpu.make_async_copy(sources[i].at[me], stages[i], own_sem.at[i]).wait()
+                pltpu.make_async_copy(piece(i, me), stages[i], own_sem.at[i]).wait()
                 pltpu.make_async_copy(stages[i], targets[i].at[me], own_sem.at[i]).start()
             for i in range(n_moves):
                 pltpu.make_async_copy(stages[i], targets[i].at[me], own_sem.at[i]).wait()
                 for d in range(1, members):
                     remote(i, d).wait()
-            for k in range(n_pushes):
-                for j in range(spread - 1):
-                    push(k, j).wait()
+            if not late:
+                for k in range(n_pushes):
+                    settle(k)
 
     anywhere = pl.BlockSpec(memory_space=pl.ANY)
     results = pl.pallas_call(
@@ -203,23 +225,23 @@
         in_specs=list(in_specs) + [anywhere] * (n_moves + n_arrays),
         out_specs=list(out_specs) + [anywhere] * (n_moves + n_pushes),
         out_shape=list(out_shape)
-        + [jax.ShapeDtypeStruct(a.shape, a.dtype) for a in moves]
+        + [jax.ShapeDtypeStruct((a.shape[0], high - low, *a.shape[2:]), a.dtype) for a, low, high in moves]
         + [jax.ShapeDtypeStruct((spread - 1, *shape), a.dtype) for a, _, shape in pushes],
         scratch_shapes=list(scratch_shapes)
-        + [pltpu.VMEM(a.shape[1:], a.dtype) for a in moves]
+        + [pltpu.VMEM((high - low, *a.shape[2:]), a.dtype) for a, low, high in moves]
         + [
             pltpu.SemaphoreType.DMA((max(1, n_moves), members)),
             pltpu.SemaphoreType.DMA((max(1, n_moves), members)),
             pltpu.SemaphoreType.DMA((max(1, n_moves),)),
-            pltpu.SemaphoreType.DMA((max(1, n_pushes), spread)),
-            pltpu.SemaphoreType.DMA((max(1, n_pushes), spread)),
+            pltpu.SemaphoreType.DMA((max(1, n_pushes), spread * PIECES)),
+            pltpu.SemaphoreType.DMA((max(1, n_pushes), spread * PIECES)),
         ],
         compiler_params=pltpu.CompilerParams(
             vmem_limit_bytes=VMEM_BYTES, collective_id=cid, has_side_effects=True
         ),
         cost_estimate=cost,
         name=name,
-    )(*args, *moves, *arrays)
+    )(*args, *(move[0] for move in moves), *arrays)
     return results[:n_out], results[n_out : n_out + n_moves], results[n_out + n_moves :]
 
 
@@ -451,7 +473,7 @@
             normed[rows, :] = (normalise(values)[0] * gain).astype(LOW)
             first_ref[rows, :] = values
 
-        by_rows(height, 32, body)
+        by_rows(height, 256, body)
 
     rows = normed[...]
     q_ref[...] = dot(rows, wq_ref[...]).astype(LOW)
@@ -471,7 +493,7 @@
         def body(rows, _):
             normed[rows, :] = (normalise(first_ref[rows, :])[0] * gain).astype(LOW)
 
-        by_rows(height, 32, body)
+        by_rows(height, 256, body)
         second = normed[...]
         projected = dot(second, route_ref[...], NT)
         projected_ref[...] = projected
@@ -622,7 +644,7 @@
         def ahead(rows, _):
             branch[rows, :] = (normalise(tokens_ref[rows, :].astype(F32))[0] * gain_one).astype(LOW)
 
-        by_rows(height, 32, ahead)
+        by_rows(height, 256, ahead)
         normed_t[...] = branch[...].T
         slot_row = slot_line(m, ids_ref, slot_ids_ref, keep_ref, slot_cap)
         slot_column = to_column(slot_row.astype(F32)).astype(jnp.int32)
@@ -670,7 +692,7 @@
             branch[rows, :] = value.astype(LOW)
             return gathered + fold_rows(grad_second * normed_two)
 
-        gathered = by_rows(height, 32, middle, jnp.zeros((8, width), F32))
+        gathered = by_rows(height, 256, middle, jnp.zeros((8, width), F32))
         small_ref[...] = jnp.zeros_like(small_ref)
         for at, ref in enumerate(thirds):
             small_ref[0:router_dim, at * third : (at + 1) * third] = sum(dot(part, ref[...], TN) for part in parts)
@@ -718,7 +740,7 @@
             gtok_ref[rows, :] = value.astype(LOW)
             return gathered + fold_rows(grad * normed_one)
 
-        gathered = by_rows(height, 32, behind, jnp.zeros((8, width), F32))
+        gathered = by_rows(height, 256, behind, jnp.zeros((8, width), F32))
         small_ref[router_dim : router_dim + 1, 0:width] = jnp.sum(gathered, axis=0, keepdims=True)
 
 
@@ -775,27 +797,33 @@
     )
 
 
-def finish_kernel(*refs, micro_count, blocks, slots, slot_cap, tiles, wide_steps, per_tile):
+def finish_kernel(*refs, cuts, blocks, tiles, per_tile):
     ids_ref, slot_ids_ref, keep_ref, embed_ref = refs[:4]
-    ins, refs = refs[4 : 4 + 4 * micro_count], refs[4 + 4 * micro_count :]
+    ins, refs = [], refs[4:]
+    for pieces in cuts:
+        ins.append(refs[: 3 + len(pieces)])
+        refs = refs[3 + len(pieces) :]
     near_in, near_outer = refs[:2]
     far_in, far_outer = refs[2 : 2 + tiles], refs[2 + tiles : 2 + 2 * tiles]
     big_ref = refs[2 + 2 * tiles]
     out_ref, grad_ref, din_ref, douter_ref, *big_outs = refs[3 + 2 * tiles :]
     step = pl.program_id(0)
     rows, width = out_ref.shape
-    for m in range(micro_count):
-        first_ref, projected_ref, home_ref, gtok_ref = ins[4 * m : 4 * m + 4]
+    for m, pieces in enumerate(cuts):
+        first_ref, projected_ref, gtok_ref, *home_refs = ins[m]
         for block in range(blocks):
 
             @pl.when(step == m * blocks + block)
             def _():
                 some = slice(block * rows, (block + 1) * rows)
-                slot_row = slot_line(m, ids_ref, slot_ids_ref, keep_ref, slot_cap)
-                slot_column = to_column(slot_row[:, some].astype(F32)).astype(jnp.int32)
+                returned = None
+                for (low, high), home_ref in zip(pieces, home_refs):
+                    line = piece_line(m, ids_ref, slot_ids_ref, keep_ref, low, high)[:, some]
+                    column = to_column(line.astype(F32)).astype(jnp.int32)
+                    term = dot(token_rows(column, home_ref.shape[0]), home_ref[...])
+                    returned = term if returned is None else returned + term
                 route_column = to_column(ids_ref[m : m + 1, some].astype(F32)).astype(jnp.int32)
                 gate = route_probs(projected_ref[...], embed_ref[...], route_column)[-1]
-                returned = dot(token_rows(slot_column, slots), home_ref[...])
                 out_ref[...] = (first_ref[...] + gate * returned).astype(LOW)
                 grad_ref[...] = gtok_ref[...]
 
@@ -810,7 +838,7 @@
         big_out[...] = big_ref[:, k * width : (k + 1) * width].astype(F32)
 
 
-def finish(ids, embed, parts, near, far, big, slots, slot_cap):
+def finish(ids, embed, parts, near, far, big):
     micro_count, tok_count = ids[0].shape
     width = parts[0][0].shape[1]
     near_in, near_outer = near
@@ -825,13 +853,13 @@
     lines = big.shape[0] // steps
     whole = lambda shape: pl.BlockSpec(shape, lambda i: (0, 0), pipeline_mode=pl.Buffered(1))
     in_specs, args = [whole(ids[0].shape)] * 3 + [whole(embed.shape)], [*ids, embed]
-    for at, (first, projected, home, gtok) in enumerate(parts):
+    for at, (first, projected, gtok, homes) in enumerate(parts):
         place = lambda i, at=at: (jnp.clip(i - at * blocks, 0, blocks - 1), 0)
         in_specs += [
-            pl.BlockSpec((rows, width), place), pl.BlockSpec((rows, projected.shape[1]), place), whole(home.shape),
-            pl.BlockSpec((rows, width), place),
+            pl.BlockSpec((rows, width), place), pl.BlockSpec((rows, projected.shape[1]), place),
+            pl.BlockSpec((rows, width), place), *(whole(home.shape) for _, home in homes),
         ]
-        args += [first, projected, home, gtok]
+        args += [first, projected, gtok, *(home for _, home in homes)]
     near_at = lambda i: jnp.minimum(i, wide_steps - 1)
     far_at = lambda i, t: jnp.clip(i - t * per_tile, 0, per_tile - 1)
     in_specs += [
@@ -845,8 +873,8 @@
     kinds = big.shape[1] // width
     return pl.pallas_call(
         functools.partial(
-            finish_kernel, micro_count=micro_count, blocks=blocks, slots=slots, slot_cap=slot_cap, tiles=tiles,
-            wide_steps=wide_steps, per_tile=per_tile,
+            finish_kernel, cuts=[[cut for cut, _ in part[3]] for part in parts], blocks=blocks, tiles=tiles,
+            per_tile=per_tile,
         ),
         grid=(steps,),
         in_specs=in_specs,
@@ -875,10 +903,12 @@
     return values * below, below + values * bell * 0.3989422804014327
 
 
-def expert_kernel(*refs, more, last, per, steps, slot_cap):
-    rows_ref, cot_ref, gate_ref, own_in, own_outer = refs[:5]
-    far_in, far_outer = refs[5 : 5 + per], refs[5 + per : 5 + 2 * per]
-    refs = refs[5 + 2 * per :]
+def expert_kernel(*refs, cuts, more, last, per, steps, slot_cap, landings=(), settle=None):
+    rows_ref, gate_ref, own_in, own_outer = refs[:4]
+    cot_refs, refs = refs[4 : 4 + len(cuts)], refs[4 + len(cuts) :]
+    far_in, refs = refs[:per], refs[per:]
+    given = per - len(landings)
+    far_outer, refs = [*refs[:given], *landings], refs[given:]
     if more:
         old_in, old_outer = refs[:2]
         refs = refs[2:]
@@ -911,7 +941,8 @@
         for w in range(sources):
             part = slice(w * slot_cap, (w + 1) * slot_cap)
             gate = jnp.sum(jnp.where(diagonal(slot_cap), gate_ref[w, 0:1, :], 0.0), axis=1, keepdims=True)
-            grad_sc[part, :] = (cot_ref[part, :].astype(F32) * gate).astype(LOW)
+            cot = jnp.concatenate([ref[w] for ref in cot_refs], axis=0)
+            grad_sc[part, :] = (cot.astype(F32) * gate).astype(LOW)
         rows_t[...] = rows_ref[...].T
         acc_result[...] = jnp.zeros_like(acc_result)
         acc_sent[...] = jnp.zeros_like(acc_sent)
@@ -922,6 +953,8 @@
         def _():
             for copy in fetch(i):
                 copy.wait()
+            if landings and i + 1 == 2 * per - 1:
+                settle(0)
             if i + 1 < steps:
                 for copy in fetch(i + 1):
                     copy.start()
@@ -960,7 +993,8 @@
         sent_ref[...] = acc_sent[...].astype(LOW)
         for w in range(sources):
             part = slice(w * slot_cap, (w + 1) * slot_cap)
-            products = cot_ref[part, :].astype(F32) * result[part, :].astype(F32)
+            cot = jnp.concatenate([ref[w] for ref in cot_refs], axis=0)
+            products = cot.astype(F32) * result[part, :].astype(F32)
             column = jnp.sum(products, axis=1, keepdims=True)
             row = jnp.sum(jnp.where(diagonal(slot_cap), column, 0.0), axis=0, keepdims=True)
             dots_ref[w] = jnp.broadcast_to(row, (8, 128))
@@ -970,7 +1004,7 @@
     return min(512, units)
 
 
-def expert_stage(rows, cot, gates, weights, old, last, slot_cap, moves, pushes, cid):
+def expert_stage(rows, cots, gates, weights, old, last, slot_cap, moves, pushes, cid):
     own_in, own_outer, far_in, far_outer = weights
     width, units = own_in.shape
     count = lax.axis_size("narrow")
@@ -1011,14 +1045,16 @@
         ]
     return call_with_moves(
         functools.partial(
-            expert_kernel, more=bool(old), last=last, per=per, steps=steps, slot_cap=slot_cap
+            expert_kernel, cuts=[cot.shape[1] for cot in cots], more=bool(old), last=last, per=per, steps=steps,
+            slot_cap=slot_cap,
         ),
         moves,
         pushes,
         cid,
         grid=(steps,),
-        in_specs=[whole((height, width)), whole((height, width)), whole(gates.shape)]
-        + [anywhere] * (2 + 2 * per)
+        in_specs=[whole((height, width)), whole(gates.shape), anywhere, anywhere]
+        + [whole(cot.shape) for cot in cots]
+        + [anywhere] * (len(far_in) + len(far_outer))
         + ([din_spec, douter_spec] if old else []),
         out_specs=out_specs,
         out_shape=out_shape,
@@ -1035,7 +1071,8 @@
             flops=12 * height * width * units * count, bytes_accessed=34 * 2**20, transcendentals=0
         ),
         name="expert_stage",
-        args=(rows, cot, gates, own_in, own_outer, *far_in, *far_outer, *old),
+        args=(rows, gates, own_in, own_outer, *cots, *far_in, *far_outer, *old),
+        late=len(far_outer) < per,
     )
 
 
@@ -1064,12 +1101,13 @@
     units = own_in.shape[1]
     tile = tile_of(units)
     per = units // tile
-    weight_pushes = [
-        (own_in, lambda ref, j, t=t: ref.at[:, t * tile : (t + 1) * tile], (feat_width, tile)) for t in range(per)
-    ] + [
-        (own_outer, lambda ref, j, t=t: ref.at[t * tile : (t + 1) * tile, :], (tile, feat_width)) for t in range(per)
-    ]
-    early = len(weight_pushes) // 3
+    weight_pushes = []
+    for t in range(per):
+        some = slice(t * tile, (t + 1) * tile)
+        weight_pushes.append((own_in, lambda ref, j, some=some: ref.at[:, some], (feat_width, tile)))
+        weight_pushes.append((own_outer, lambda ref, j, some=some: ref.at[some, :], (tile, feat_width)))
+    early = 2 if per > 1 else 1
+    half = slot_cap // 2
     gains = (gain_one[None], gain_two[None])
     mixers = (w_query, w_key, w_value, w_out)
     ids = (route_ids, slot_ids, keep_ids)
@@ -1079,25 +1117,34 @@
         return rows.reshape((expert_count, slot_cap) + rows.shape[1:])
 
     def flat(boxed):
-        return boxed.reshape((expert_count * slot_cap,) + boxed.shape[2:])
+        return boxed.reshape((boxed.shape[0] * boxed.shape[1],) + boxed.shape[2:])
+
+    def entire(array):
+        return array, 0, array.shape[1]
 
     cot_boxes = [boxes(rows) for rows in dispatch(ids, grad_out, slots, slot_cap)]
     (*ahead_0, sent, gates, projected), (cot_0,), far_a = forward_stage(
-        0, tokens, gains, mixers, *router, slot_cap, (cot_boxes[0],), weight_pushes[:early], 1
+        0, tokens, gains, mixers, *router, slot_cap, (entire(cot_boxes[0]),), weight_pushes[:early], 1
     )
     ahead_0.append(projected)
     (*ahead_1, next_sent, next_gates, projected), (sent_0, gates_0, cot_1), far_b = forward_stage(
-        1, tokens, gains, mixers, *router, slot_cap, (boxes(sent), gates, cot_boxes[1]), weight_pushes[early:], 2
+        1, tokens, gains, mixers, *router, slot_cap,
+        (entire(boxes(sent)), entire(gates), entire(cot_boxes[1])), weight_pushes[early:-1], 2
     )
     ahead_1.append(projected)
 
     far = [*far_a, *far_b]
-    weights = (own_in, own_outer, far[:per], far[per:])
-    (result_0, grad_0, dots_0, *old), (sent_1, gates_1), _ = expert_stage(
-        flat(sent_0), flat(cot_0), gates_0, weights, (), False, slot_cap, (boxes(next_sent), next_gates), (), 3
-    )
-    (result_1, grad_1, dots_1, near_din, near_douter, far_din, far_douter), (home_grad_0, home_dots_0), _ = expert_stage(
-        flat(sent_1), flat(cot_1), gates_1, weights, tuple(old), True, slot_cap, (boxes(grad_0), dots_0), (), 4
+    (result_0, grad_0, dots_0, *old), (sent_1, gates_1), far_c = expert_stage(
+        flat(sent_0), (cot_0,), gates_0, (own_in, own_outer, far[0::2], far[1::2]), (), False, slot_cap,
+        (entire(boxes(next_sent)), entire(next_gates)), weight_pushes[-1:], 3
+    )
+    far = [*far, *far_c]
+    result_0 = boxes(result_0)
+    (result_1, grad_1, dots_1, near_din, near_douter, far_din, far_douter), (home_grad_0, home_dots_0), _ = (
+        expert_stage(
+            flat(sent_1), (cot_1,), gates_1, (own_in, own_outer, far[0::2], far[1::2]), tuple(old), True,
+            slot_cap, (entire(boxes(grad_0)), entire(dots_0)), (), 4
+        )
     )
     grad_pushes = [
         (far_din, lambda ref, j, t=t: ref.at[j * per + t], (feat_width, tile)) for t in range(per)
@@ -1110,22 +1157,23 @@
         q, k, v, soft, inverses, mixed, first, projected = ahead
         return first, projected, q, k, v, mixed, soft, inverses
 
-    (*big_0, gtok_0, small_0), (home_grad_1, home_dots_1), got_a = backward_stage(
+    (*big_0, gtok_0, small_0), (home_grad_1, home_dots_1, home_b), got_a = backward_stage(
         0, tokens, grad_out, gains, mixers, *router, kept(ahead_0), (flat(home_grad_0), home_dots_0), slot_cap,
-        (boxes(grad_1), dots_1), grad_pushes[:later], 5
-    )
-    (*big_1, gtok_1, small_1), (home_result_0, home_result_1), got_b = backward_stage(
+        (entire(boxes(grad_1)), entire(dots_1), (result_0, half, slot_cap)), grad_pushes[:later], 5
+    )
+    (*big_1, gtok_1, small_1), (home_1, home_c), got_b = backward_stage(
         1, tokens, grad_out, gains, mixers, *router, kept(ahead_1), (flat(home_grad_1), home_dots_1), slot_cap,
-        (boxes(result_0), boxes(result_1)), grad_pushes[later:], 6
-    )
+        (entire(boxes(result_1)), (result_0, 0, half)), grad_pushes[later:], 6
+    )
+    homes_0 = [((half, slot_cap), flat(home_b)), ((0, half), flat(home_c))]
     big, small = reduce_everywhere(list(zip(big_0, big_1)), (small_0, small_1), 7)
     block_out, grad_tokens, grad_in, grad_outer, *big = finish(
         ids, embed,
         (
-            (ahead_0[6], ahead_0[7], flat(home_result_0), gtok_0),
-            (ahead_1[6], ahead_1[7], flat(home_result_1), gtok_1),
+            (ahead_0[6], ahead_0[7], gtok_0, homes_0),
+            (ahead_1[6], ahead_1[7], gtok_1, [((0, slot_cap), flat(home_1))]),
         ),
-        (near_din, near_douter), [*got_a, *got_b], big, slots, slot_cap,
+        (near_din, near_douter), [*got_a, *got_b], big,
     )
     router_dim = w_route.shape[1]
     return (

time: 502 us -> 485 us (0.966)
  Pallas kernels: 494 us -> 477 us
    pallas_call x1, Pallas kernels: 82.3 us -> 72.5 us  [reduce_everywhere(): pl.pallas_call(functools.partial(reduce_kernel, orders=orders, width=widt...]
    pallas_call x6, Pallas kernels: 382 us -> 374 us  [call_with_moves(): pl.pallas_call(kernel, grid=grid, in_specs=list(in_specs) + [anywhere] *...]
where the time goes in v6:
time: 485 us; the launch traced here: 482 us
  Pallas kernels  477 us (98%)
    pallas_call x6, Pallas kernels, call_with_moves(): pl.pallas_call(kernel, grid=grid, in_specs=list(in_specs) + [anywhere] *...  374 us
    pallas_call x1, Pallas kernels, reduce_everywhere(): pl.pallas_call(functools.partial(reduce_kernel, orders=orders, width=widt...  72.5 us
    pallas_call x1, Pallas kernels, finish(): pl.pallas_call(functools.partial(finish_kernel, cuts=[[cut for cut, _ in...  23.7 us

profile of v6, /device:TPU:0, one launch (start us, length us, event | category | flops | bytes accessed | tf_op | source)
XLA Modules:
  0.0 482.0 jit_solution(12164770759997538101)
XLA Ops:
  0.6 1.3 broadcast_in_dim.6.refs_1_.refs_2_
  1.9 1.3 broadcast_in_dim.7.refs_6_.refs_7_
  3.2 6.7 %dispatch.1 = (bf16[1024,768]{1,0:T(8,128)(2,1)}, bf16[1024,768]{1,0:T(8,128)(2,1)}) custom-call(s32[2,1024]{1,0:T(2,128)} %refs_0_.9, s32[2,1024]{1,0:T(2,128)} %refs_1_.5, s32[2,1024]{1,0:T(2,128)} %refs_2_.5, bf16[2,1024,768]{2,1,0:T(8,128)(2,1)} %refs_1_.4), custom_call_target="tpu_custom_call" | custom-call | flops 3000000000 | bytes 6291456 | tf_op jit(solution)/shard_map/dispatch/pallas_call | solution.py:575
  9.9 51.5 %forward_stage.2 = (bf16[1024,768]{1,0:T(8,128)(2,1)}, bf16[1024,768]{1,0:T(8,128)(2,1)}, bf16[1024,768]{1,0:T(8,128)(2,1)}, bf16[12,1024,1024]{2,1,0:T(8,128)(2...) custom-call(bf16[2,1024,768]{2,1,0:T(8,128)(2,1)} %refs_0_.8, ...), custom_call_target="tpu_custom_call" | custom-call | flops 30000001024 | bytes 52428800 | tf_op jit(solution)/shard_map/forward_stage/pallas_call | solution.py:222
  61.4 70.1 %forward_stage.3 = (bf16[1024,768]{1,0:T(8,128)(2,1)}, bf16[1024,768]{1,0:T(8,128)(2,1)}, bf16[1024,768]{1,0:T(8,128)(2,1)}, bf16[12,1024,1024]{2,1,0:T(8,128)(2...) custom-call(bf16[2,1024,768]{2,1,0:T(8,128)(2,1)} %refs_0_.8, ...), custom_call_target="tpu_custom_call" | custom-call | flops 30000001024 | bytes 52428800 | tf_op jit(solution)/shard_map/forward_stage/pallas_call | solution.py:222
  131.4 59.2 %expert_stage.2 = (bf16[1024,768]{1,0:T(8,128)(2,1)}, bf16[1024,768]{1,0:T(8,128)(2,1)}, f32[16,8,128]{2,1,0:T(8,128)}, f32[6,768,512]{2,1,0:T(8,128)}, f32[6,51...) custom-call(bf16[1024,768]{1,0:T(8,128)(2,1)} %bitcast.45, ...), custom_call_target="tpu_custom_call" | custom-call | flops 28991029248 | bytes 35651584 | tf_op jit(solution)/shard_map/expert_stage/pallas_call | solution.py:222
  190.7 48.6 %expert_stage.3 = (bf16[1024,768]{1,0:T(8,128)(2,1)}, bf16[1024,768]{1,0:T(8,128)(2,1)}, f32[16,8,128]{2,1,0:T(8,128)}, f32[768,1536]{1,0:T(8,128)}, f32[1536,76...) custom-call(bf16[1024,768]{1,0:T(8,128)(2,1)} %bitcast.47, ...), custom_call_target="tpu_custom_call" | custom-call | flops 28991029248 | bytes 35651584 | tf_op jit(solution)/shard_map/expert_stage/pallas_call | solution.py:222
  239.3 79.2 %backward_stage.2 = (bf16[768,768]{1,0:T(8,128)(2,1)}, bf16[768,768]{1,0:T(8,128)(2,1)}, bf16[768,768]{1,0:T(8,128)(2,1)}, bf16[768,768]{1,0:T(8,128)(2,1)}, bf1...) custom-call(bf16[2,1024,768]{2,1,0:T(8,128)(2,1)} %refs_0_.8, ...), custom_call_target="tpu_custom_call" | custom-call | flops 40000000000 | bytes 52428800 | tf_op jit(solution)/shard_map/backward_stage/pallas_call | solution.py:222
  318.6 65.0 %backward_stage.3 = (bf16[768,768]{1,0:T(8,128)(2,1)}, bf16[768,768]{1,0:T(8,128)(2,1)}, bf16[768,768]{1,0:T(8,128)(2,1)}, bf16[768,768]{1,0:T(8,128)(2,1)}, bf1...) custom-call(bf16[2,1024,768]{2,1,0:T(8,128)(2,1)} %refs_0_.8, ...), custom_call_target="tpu_custom_call" | custom-call | flops 40000000000 | bytes 52428800 | tf_op jit(solution)/shard_map/backward_stage/pallas_call | solution.py:222
  383.6 72.5 %reduce_everywhere.1 = (bf16[768,3072]{1,0:T(8,128)(2,1)}, f32[24,896]{1,0:T(8,128)}) custom-call(bf16[768,768]{1,0:T(8,128)(2,1)} %get-tuple-element.154.refs_0_, bf16[768,768]{1,0:T(8,128)(2,1)} %get-tuple-element.155.refs_1_, bf16[768,768]{1,0:T(8,128)(2,1)} %get-tuple-element.156.refs_2_, bf16[768,768]{1,0:T(8,128)(2,1)} %get-tuple-element.157.refs_3_, ...), custom_call_target="tpu_custom_call" | custom-call | flops 1000000000 | bytes 20971520 | tf_op jit(solution)/shard_map/reduce_everywhere/pallas_call | solution.py:411
  456.1 0.0 copy-start
  456.1 23.7 %finish.1 = (bf16[2,1024,768]{2,1,0:T(8,128)(2,1)}, bf16[2,1024,768]{2,1,0:T(8,128)(2,1)}, f32[1,768,1536]{2,1,0:T(8,128)}, f32[1,1536,768]{2,1,0:T(8,128)}, f32...) custom-call(s32[2,1024]{1,0:T(2,128)} %refs_0_.9, s32[2,1024]{1,0:T(2,128)} %refs_1_.5, ...), custom_call_target="tpu_custom_call" | custom-call | flops 3000000000 | bytes 58720256 | tf_op jit(solution)/shard_map/finish/pallas_call | solution.py:874
  479.8 0.0 copy-done
  479.8 0.6 slice.15
  480.4 0.6 slice_reduce_fusion
  481.0 0.6 slice_bitcast_fusion
Async XLA Ops:
  456.1 23.7 %copy-start = (f32[24,896]{1,0:T(8,128)S(1)}, f32[24,896]{1,0:T(8,128)}, u32[]{:S(2)}) copy-start(f32[24,896]{1,0:T(8,128)} %get-tuple-element.167) | copy-start | bytes 258052

commit v7 on v6

--- a/solution.py
+++ b/solution.py
@@ -466,7 +466,7 @@
 
     @pl.when(step == 0)
     def _():
-        gain = gain_one_ref[...]
+        gain = gain_one_ref[...][None, :]
 
         def body(rows, _):
             values = tokens_ref[rows, :].astype(F32)
@@ -488,7 +488,7 @@
 
     @pl.when(step == steps - 1)
     def _():
-        gain = gain_two_ref[...]
+        gain = gain_two_ref[...][None, :]
 
         def body(rows, _):
             normed[rows, :] = (normalise(first_ref[rows, :])[0] * gain).astype(LOW)
@@ -534,8 +534,8 @@
         cid,
         grid=(steps,),
         in_specs=[
-            of_m(tok_count, width), fixed((1, width)), columns(width), columns(width), columns(width),
-            pl.BlockSpec((span, width), lambda i: (i, 0)), fixed((1, width)), fixed(w_route.shape),
+            of_m(tok_count, width), fixed((width,)), columns(width), columns(width), columns(width),
+            pl.BlockSpec((span, width), lambda i: (i, 0)), fixed((width,)), fixed(w_route.shape),
             fixed(embed.shape),
         ]
         + [fixed(ids[0].shape)] * 3,
@@ -639,7 +639,7 @@
     @pl.when(step == 0)
     def _():
         soft_pair(0).start()
-        gain_one, gain_two = gain_one_ref[...], gain_two_ref[...]
+        gain_one, gain_two = gain_one_ref[...][None, :], gain_two_ref[...][None, :]
 
         def ahead(rows, _):
             branch[rows, :] = (normalise(tokens_ref[rows, :].astype(F32))[0] * gain_one).astype(LOW)
@@ -731,7 +731,7 @@
 
     @pl.when(step == steps - 1)
     def _():
-        gain_one = gain_one_ref[...]
+        gain_one = gain_one_ref[...][None, :]
 
         def behind(rows, gathered):
             normed_one, inverse_one = normalise(tokens_ref[rows, :].astype(F32))
@@ -769,8 +769,8 @@
         cid,
         grid=(steps,),
         in_specs=[
-            of_m(tok_count, width), of_m(tok_count, width), fixed((1, width)), columns(width), columns(width),
-            columns(width), lines, fixed((1, width)), fixed(w_route.shape), fixed(embed.shape),
+            of_m(tok_count, width), of_m(tok_count, width), fixed((width,)), columns(width), columns(width),
+            columns(width), lines, fixed((width,)), fixed(w_route.shape), fixed(embed.shape),
             *[fixed(ids[0].shape)] * 3, fixed(first.shape), fixed(projected.shape), fixed(home[0].shape), fixed(home[1].shape),
             columns(tok_count), columns(tok_count), columns(tok_count), columns(tok_count),
             pl.BlockSpec(memory_space=pl.ANY), columns(tok_count),
@@ -1108,7 +1108,7 @@
         weight_pushes.append((own_outer, lambda ref, j, some=some: ref.at[some, :], (tile, feat_width)))
     early = 2 if per > 1 else 1
     half = slot_cap // 2
-    gains = (gain_one[None], gain_two[None])
+    gains = (gain_one, gain_two)
     mixers = (w_query, w_key, w_value, w_out)
     ids = (route_ids, slot_ids, keep_ids)
     router = (w_route.T, embed, ids)

time: 485 us -> 483 us (level)
  no operation moved by 1% of the time
where the time goes in v7:
time: 483 us; the launch traced here: 480 us
  Pallas kernels  477 us (99%)
    pallas_call x6, Pallas kernels, call_with_moves(): pl.pallas_call(kernel, grid=grid, in_specs=list(in_specs) + [anywhere] *...  374 us
    pallas_call x1, Pallas kernels, reduce_everywhere(): pl.pallas_call(functools.partial(reduce_kernel, orders=orders, width=widt...  72.5 us
    pallas_call x1, Pallas kernels, finish(): pl.pallas_call(functools.partial(finish_kernel, cuts=[[cut for cut, _ in...  23.7 us

profile of v7, /device:TPU:0, one launch (start us, length us, event | category | flops | bytes accessed | tf_op | source)
XLA Modules:
  0.0 479.5 jit_solution(11739170748133440004)
XLA Ops:
  0.6 6.7 %dispatch.1 = (bf16[1024,768]{1,0:T(8,128)(2,1)}, bf16[1024,768]{1,0:T(8,128)(2,1)}) custom-call(s32[2,1024]{1,0:T(2,128)} %refs_0_.9, s32[2,1024]{1,0:T(2,128)} %refs_1_.9, s32[2,1024]{1,0:T(2,128)} %refs_2_.9, bf16[2,1024,768]{2,1,0:T(8,128)(2,1)} %refs_1_.8), custom_call_target="tpu_custom_call" | custom-call | flops 3000000000 | bytes 6291456 | tf_op jit(solution)/shard_map/dispatch/pallas_call | solution.py:575
  7.3 51.5 %forward_stage.2 = (bf16[1024,768]{1,0:T(8,128)(2,1)}, bf16[1024,768]{1,0:T(8,128)(2,1)}, bf16[1024,768]{1,0:T(8,128)(2,1)}, bf16[12,1024,1024]{2,1,0:T(8,128)(2...) custom-call(bf16[2,1024,768]{2,1,0:T(8,128)(2,1)} %refs_0_.8, ...), custom_call_target="tpu_custom_call" | custom-call | flops 30000001024 | bytes 52428800 | tf_op jit(solution)/shard_map/forward_stage/pallas_call | solution.py:222
  58.9 70.1 %forward_stage.3 = (bf16[1024,768]{1,0:T(8,128)(2,1)}, bf16[1024,768]{1,0:T(8,128)(2,1)}, bf16[1024,768]{1,0:T(8,128)(2,1)}, bf16[12,1024,1024]{2,1,0:T(8,128)(2...) custom-call(bf16[2,1024,768]{2,1,0:T(8,128)(2,1)} %refs_0_.8, ...), custom_call_target="tpu_custom_call" | custom-call | flops 30000001024 | bytes 52428800 | tf_op jit(solution)/shard_map/forward_stage/pallas_call | solution.py:222
  128.9 59.2 %expert_stage.2 = (bf16[1024,768]{1,0:T(8,128)(2,1)}, bf16[1024,768]{1,0:T(8,128)(2,1)}, f32[16,8,128]{2,1,0:T(8,128)}, f32[6,768,512]{2,1,0:T(8,128)}, f32[6,51...) custom-call(bf16[1024,768]{1,0:T(8,128)(2,1)} %bitcast.45, ...), custom_call_target="tpu_custom_call" | custom-call | flops 28991029248 | bytes 35651584 | tf_op jit(solution)/shard_map/expert_stage/pallas_call | solution.py:222
  188.2 48.6 %expert_stage.3 = (bf16[1024,768]{1,0:T(8,128)(2,1)}, bf16[1024,768]{1,0:T(8,128)(2,1)}, f32[16,8,128]{2,1,0:T(8,128)}, f32[768,1536]{1,0:T(8,128)}, f32[1536,76...) custom-call(bf16[1024,768]{1,0:T(8,128)(2,1)} %bitcast.47, ...), custom_call_target="tpu_custom_call" | custom-call | flops 28991029248 | bytes 35651584 | tf_op jit(solution)/shard_map/expert_stage/pallas_call | solution.py:222
  236.8 79.3 %backward_stage.2 = (bf16[768,768]{1,0:T(8,128)(2,1)}, bf16[768,768]{1,0:T(8,128)(2,1)}, bf16[768,768]{1,0:T(8,128)(2,1)}, bf16[768,768]{1,0:T(8,128)(2,1)}, bf1...) custom-call(bf16[2,1024,768]{2,1,0:T(8,128)(2,1)} %refs_0_.8, ...), custom_call_target="tpu_custom_call" | custom-call | flops 40000000000 | bytes 52428800 | tf_op jit(solution)/shard_map/backward_stage/pallas_call | solution.py:222
  316.1 65.0 %backward_stage.3 = (bf16[768,768]{1,0:T(8,128)(2,1)}, bf16[768,768]{1,0:T(8,128)(2,1)}, bf16[768,768]{1,0:T(8,128)(2,1)}, bf16[768,768]{1,0:T(8,128)(2,1)}, bf1...) custom-call(bf16[2,1024,768]{2,1,0:T(8,128)(2,1)} %refs_0_.8, ...), custom_call_target="tpu_custom_call" | custom-call | flops 40000000000 | bytes 52428800 | tf_op jit(solution)/shard_map/backward_stage/pallas_call | solution.py:222
  381.1 72.5 %reduce_everywhere.1 = (bf16[768,3072]{1,0:T(8,128)(2,1)}, f32[24,896]{1,0:T(8,128)}) custom-call(bf16[768,768]{1,0:T(8,128)(2,1)} %get-tuple-element.154.refs_0_, bf16[768,768]{1,0:T(8,128)(2,1)} %get-tuple-element.155.refs_1_, bf16[768,768]{1,0:T(8,128)(2,1)} %get-tuple-element.156.refs_2_, bf16[768,768]{1,0:T(8,128)(2,1)} %get-tuple-element.157.refs_3_, ...), custom_call_target="tpu_custom_call" | custom-call | flops 1000000000 | bytes 20971520 | tf_op jit(solution)/shard_map/reduce_everywhere/pallas_call | solution.py:411
  453.6 0.0 copy-start
  453.6 23.7 %finish.1 = (bf16[2,1024,768]{2,1,0:T(8,128)(2,1)}, bf16[2,1024,768]{2,1,0:T(8,128)(2,1)}, f32[1,768,1536]{2,1,0:T(8,128)}, f32[1,1536,768]{2,1,0:T(8,128)}, f32...) custom-call(s32[2,1024]{1,0:T(2,128)} %refs_0_.9, s32[2,1024]{1,0:T(2,128)} %refs_1_.9, ...), custom_call_target="tpu_custom_call" | custom-call | flops 3000000000 | bytes 58720256 | tf_op jit(solution)/shard_map/finish/pallas_call | solution.py:874
  477.3 0.0 copy-done
  477.3 0.6 slice.15
  477.9 0.6 slice_reduce_fusion
  478.5 0.6 slice_bitcast_fusion
Async XLA Ops:
  453.6 23.7 %copy-start = (f32[24,896]{1,0:T(8,128)S(1)}, f32[24,896]{1,0:T(8,128)}, u32[]{:S(2)}) copy-start(f32[24,896]{1,0:T(8,128)} %get-tuple-element.167) | copy-start | bytes 258052
